TPU v7x, 32 devices: a whole 2x2x4 slice. The times are simulated.
32 devices in a mesh: dp: 16 (over z, x, core), seq: 2 (over y).
Axes of the slice: x: 2, y: 2, z: 4, core: 2. Of those that a mesh axis runs over, the one named last changes fastest.
Arguments:
- tokens: bfloat16 [64, 1024, 768], P(('dp', 'seq')), may hold values from -6 to 6
- segments: int32 [64, 1024], P(('dp', 'seq')), may hold values from 0 to 3, never falling along the last dimension, each value on 1 to 512 neighbouring positions
- cotangent: bfloat16 [64, 1024, 768], P(('dp', 'seq')), may hold values from -6 to 6
- norm_gain: float32 [768], replicated, may hold values from 0.5 to 1.5
- weight_in: bfloat16 [768, 3352], P('dp'), may hold values from -0.21875 to 0.21875
- conv_weight: float32 [4, 1792], replicated, may hold values from -3 to 3
- conv_bias: float32 [1792], replicated, may hold values from -3 to 3
- dt_bias: float32 [24], replicated, may hold values from -6 to -2
- a_log: float32 [24], replicated, may hold values from -1 to 2.5
- skip_d: float32 [24], replicated, may hold values from 0.5 to 1.5
- gate_gain: float32 [1536], replicated, may hold values from 0.5 to 1.5
- weight_out: bfloat16 [1536, 768], P('dp'), may hold values from -0.15625 to 0.15625
Outputs:
- mixed_out: bfloat16 [64, 1024, 768], P(('dp', 'seq'))
- grad_tokens: bfloat16 [64, 1024, 768], P(('dp', 'seq'))
- grad_norm_gain: float32 [768], replicated
- grad_weight_in: float32 [768, 3352], P('dp')
- grad_conv_weight: float32 [4, 1792], replicated
- grad_conv_bias: float32 [1792], replicated
- grad_dt_bias: float32 [24], replicated
- grad_a_log: float32 [24], replicated
- grad_skip_d: float32 [24], replicated
- grad_gate_gain: float32 [1536], replicated
- grad_weight_out: float32 [1536, 768], P('dp')
Inputs may be any that keep to these rules, and one draw needn't show every extreme that they name: `segments`: in each sequence the numbers never fall, all of 0 to 3 occur, each document holds 1 to 512 tokens and one holds exactly 512.
All inputs are finite; a program needn't handle non-finite values.
Results may differ from a plain program's by a relative error of at most 0.0082.
Values may be sent and summed in bfloat16 or wider, within the bound.
A program may use at most 448 MiB of HBM per device.

v0:
```python
import jax
import jax.numpy as jnp
from jax import lax
from jax.sharding import PartitionSpec as P

BLOCK = 256
MICRO = 2


eps_norm = 1e-05
highest = lax.Precision.HIGHEST


def rms_scale(values, scale_gain):
    return (
        values
        * lax.rsqrt(jnp.mean(values * values, axis=-1, keepdims=True) + eps_norm)
        * scale_gain
    )


def causal_conv(padded, seg_pad, conv_weight, conv_bias):
    tap_count = conv_weight.shape[0]
    row_count = padded.shape[1] - tap_count + 1
    summed = jnp.zeros_like(padded[:, tap_count - 1 :, :]) + conv_bias
    for offset in range(tap_count):
        window = padded[:, offset : offset + row_count, :]
        same_seg = (seg_pad[:, offset : offset + row_count] == seg_pad[:, tap_count - 1 :]).astype(
            jnp.float32
        )
        summed = summed + conv_weight[offset] * window * same_seg[..., None]
    return jax.nn.silu(summed)


def state_space(values_x, b_proj, c_proj, time_step, log_decay, seg_float, skip_d, block_len):
    seq_count, row_count, head_count, head_dim = values_x.shape
    block_count = row_count // block_len
    state_dim = b_proj.shape[-1]
    x_blocks = values_x.reshape(seq_count, block_count, block_len, head_count, head_dim)
    b_blocks = b_proj.reshape(seq_count, block_count, block_len, state_dim)
    c_blocks = c_proj.reshape(seq_count, block_count, block_len, state_dim)
    step_blocks = time_step.reshape(seq_count, block_count, block_len, head_count)
    cumulative = jnp.cumsum(
        log_decay.reshape(seq_count, block_count, block_len, head_count), axis=2
    )
    seg_blocks = seg_float.reshape(seq_count, block_count, block_len)
    positions = jnp.arange(block_len)
    causal = positions[:, None] >= positions[None, :]
    same_seg = (seg_blocks[:, :, :, None] == seg_blocks[:, :, None, :]) & causal
    in_segment = same_seg[:, :, None, :, :]
    cum_heads = jnp.moveaxis(cumulative, 3, 2)
    log_gap = cum_heads[..., :, None] - cum_heads[..., None, :]
    decay_mat = jnp.exp(jnp.where(in_segment, log_gap, 0.0)) * in_segment.astype(jnp.float32)
    scores = jnp.einsum("skin,skjn->skij", c_blocks, b_blocks, precision=highest)
    x_scaled = x_blocks * step_blocks[..., None]
    within = jnp.einsum(
        "skhij,skjhp->skihp", decay_mat * scores[:, :, None], x_scaled, precision=highest
    )
    last_seg = seg_blocks[:, :, -1]
    to_end = (seg_blocks == last_seg[..., None]).astype(jnp.float32)[..., None] * jnp.exp(
        cumulative[:, :, -1:, :] - cumulative
    )
    own_state = jnp.einsum(
        "skjhp,skjn->skhpn", x_scaled * to_end[..., None], b_blocks, precision=highest
    )
    block_decay = jnp.exp(cumulative[:, :, -1, :])
    prev_seg = jnp.concatenate(
        [jnp.full((seq_count, 1), -1.0, jnp.float32), last_seg[:, :-1]], axis=1
    )
    keep_flag = (last_seg == prev_seg).astype(jnp.float32)
    carried = jnp.zeros((seq_count, head_count, head_dim, state_dim), jnp.float32)
    entering = []
    for block_idx in range(block_count):
        entering.append(carried)
        carried = (
            own_state[:, block_idx]
            + (keep_flag[:, block_idx, None] * block_decay[:, block_idx])[..., None, None] * carried
        )
    entering = jnp.stack(entering, axis=1)
    from_prev = (seg_blocks == prev_seg[..., None]).astype(jnp.float32)[..., None] * jnp.exp(
        cumulative
    )
    state_part = (
        jnp.einsum("skin,skhpn->skihp", c_blocks, entering, precision=highest)
        * from_prev[..., None]
    )
    result = within + state_part + skip_d[:, None] * x_blocks
    return result.reshape(seq_count, row_count, head_count, head_dim)


def mixer_core(
    conv_in, dt_raw, conv_weight, conv_bias, dt_bias, a_log, skip_d, seg_float, inner, block_len
):
    seq_count, row_count, channels = conv_in.shape
    head_count = dt_bias.shape[0]
    rim_width = conv_weight.shape[0] - 1
    padded = jnp.concatenate(
        [jnp.zeros((seq_count, rim_width, channels), jnp.float32), conv_in], axis=1
    )
    seg_pad = jnp.concatenate(
        [jnp.full((seq_count, rim_width), -1.0, jnp.float32), seg_float], axis=1
    )
    conv_out = causal_conv(padded, seg_pad, conv_weight, conv_bias)
    state_dim = (channels - inner) // 2
    values_x = conv_out[..., :inner].reshape(seq_count, row_count, head_count, inner // head_count)
    b_proj = conv_out[..., inner : inner + state_dim]
    c_proj = conv_out[..., inner + state_dim :]
    time_step = jax.nn.softplus(dt_raw + dt_bias)
    log_decay = -jnp.exp(a_log) * time_step
    return state_space(values_x, b_proj, c_proj, time_step, log_decay, seg_float, skip_d, block_len)


def gate_norm(mixed, gate_z, gate_gain):
    gated = mixed.reshape(gate_z.shape[0], gate_z.shape[1], -1) * jax.nn.silu(gate_z)
    return rms_scale(gated, gate_gain)


def per_device(
    tokens,
    segments,
    cotangent,
    norm_gain,
    weight_in,
    conv_weight,
    conv_bias,
    dt_bias,
    a_log,
    skip_d,
    gate_gain,
    weight_out,
):
    seq_count, row_count, width = tokens.shape
    per_micro = seq_count // MICRO
    inner = gate_gain.shape[0]
    channels = conv_bias.shape[0]
    acc_in = jnp.zeros((width, weight_in.shape[1]), jnp.float32)
    acc_out = jnp.zeros((inner, width), jnp.float32)
    acc_ngain = jnp.zeros_like(norm_gain)
    acc_cw = jnp.zeros_like(conv_weight)
    acc_cb = jnp.zeros_like(conv_bias)
    acc_dtb = jnp.zeros_like(dt_bias)
    acc_alog = jnp.zeros_like(a_log)
    acc_skip = jnp.zeros_like(skip_d)
    acc_ggain = jnp.zeros_like(gate_gain)
    results = []
    input_grads = []
    for micro_idx in range(MICRO):
        first_row = micro_idx * per_micro
        part_tok = tokens[first_row : first_row + per_micro].astype(jnp.float32)
        part_cot = cotangent[first_row : first_row + per_micro]
        seg_float = segments[first_row : first_row + per_micro].astype(jnp.float32)
        full_in, full_out = (
            lax.all_gather(weight_in, "dp", axis=0, tiled=True),
            lax.all_gather(weight_out, "dp", axis=0, tiled=True),
        )
        normed, pull_norm = jax.vjp(rms_scale, part_tok, norm_gain)
        normed_low = normed.astype(jnp.bfloat16)
        projected = jnp.einsum(
            "srd,de->sre", normed_low, full_in, preferred_element_type=jnp.float32
        )
        gate_z = projected[..., :inner]
        conv_in = projected[..., inner : inner + channels]
        dt_raw = projected[..., inner + channels :]

        def mixer_part(conv_part, dt_part, conv_taps, bias_conv, bias_dt, log_rates, skip_part):
            return mixer_core(
                conv_part,
                dt_part,
                conv_taps,
                bias_conv,
                bias_dt,
                log_rates,
                skip_part,
                seg_float,
                inner,
                BLOCK,
            )

        mixed, pull_mixer = jax.vjp(
            mixer_part, conv_in, dt_raw, conv_weight, conv_bias, dt_bias, a_log, skip_d
        )
        gnormed, pull_gate = jax.vjp(gate_norm, mixed, gate_z, gate_gain)
        gnormed_low = gnormed.astype(jnp.bfloat16)
        branch = jnp.einsum(
            "sri,id->srd", gnormed_low, full_out, preferred_element_type=jnp.float32
        )
        results.append((part_tok + branch).astype(jnp.bfloat16))
        full_in, full_out = (
            lax.all_gather(weight_in, "dp", axis=0, tiled=True),
            lax.all_gather(weight_out, "dp", axis=0, tiled=True),
        )
        acc_out = acc_out + jnp.einsum(
            "sri,srd->id", gnormed_low, part_cot, preferred_element_type=jnp.float32
        )
        grad_gnormed = jnp.einsum(
            "srd,id->sri", part_cot, full_out, preferred_element_type=jnp.float32
        )
        grad_mixed, grad_z, grad_ggain = pull_gate(grad_gnormed)
        grad_conv_in, grad_dt_raw, grad_cw, grad_cb, grad_dtb, grad_alog, grad_skip = pull_mixer(
            grad_mixed
        )
        grad_proj = jnp.concatenate([grad_z, grad_conv_in, grad_dt_raw], axis=-1).astype(
            jnp.bfloat16
        )
        acc_in = acc_in + jnp.einsum(
            "srd,sre->de", normed_low, grad_proj, preferred_element_type=jnp.float32
        )
        grad_normed = jnp.einsum(
            "sre,de->srd", grad_proj, full_in, preferred_element_type=jnp.float32
        )
        grad_tok, grad_ngain = pull_norm(grad_normed)
        input_grads.append((grad_tok + part_cot.astype(jnp.float32)).astype(jnp.bfloat16))
        acc_ngain = acc_ngain + grad_ngain
        acc_cw = acc_cw + grad_cw
        acc_cb = acc_cb + grad_cb
        acc_dtb = acc_dtb + grad_dtb
        acc_alog = acc_alog + grad_alog
        acc_skip = acc_skip + grad_skip
        acc_ggain = acc_ggain + grad_ggain
    shard_in, shard_out = (
        lax.psum_scatter(acc_in, "dp", scatter_dimension=0, tiled=True),
        lax.psum_scatter(acc_out, "dp", scatter_dimension=0, tiled=True),
    )
    shard_in, shard_out = (
        lax.psum(shard_in.astype(jnp.bfloat16), "seq").astype(jnp.float32),
        lax.psum(shard_out.astype(jnp.bfloat16), "seq").astype(jnp.float32),
    )
    sum_ngain, sum_cw, sum_cb, sum_dtb, sum_alog, sum_skip, sum_ggain = lax.psum(
        (acc_ngain, acc_cw, acc_cb, acc_dtb, acc_alog, acc_skip, acc_ggain), ("dp", "seq")
    )
    return (
        jnp.concatenate(results, axis=0),
        jnp.concatenate(input_grads, axis=0),
        sum_ngain,
        shard_in,
        sum_cw,
        sum_cb,
        sum_dtb,
        sum_alog,
        sum_skip,
        sum_ggain,
        shard_out,
    )


def solution(mesh):
    placed = (
        P(("dp", "seq"), None, None),
        P(("dp", "seq"), None),
        P(("dp", "seq"), None, None),
        P(),
        P("dp", None),
        P(),
        P(),
        P(),
        P(),
        P(),
        P(),
        P("dp", None),
    )
    return jax.shard_map(
        per_device,
        mesh=mesh,
        in_specs=placed,
        out_specs=(
            P(("dp", "seq"), None, None),
            P(("dp", "seq"), None, None),
            P(),
            P("dp", None),
            P(),
            P(),
            P(),
            P(),
            P(),
            P(),
            P("dp", None),
        ),
        check_vma=False,
    )
```

profile of v0, /device:TPU:0, one launch (start us, length us, event | category | flops | bytes accessed | tf_op | source)
XLA Modules:
  0.0 1085.5 jit_solution(14046305234826929759)
XLA Ops:
  19.9 35.4 %all-gather.5.cloned.1.call-done = bf16[1536,768]{1,0:T(8,128)(2,1)} async-done(((bf16[96,768]{1,0:T(8,128)(2,1)}), bf16[1536,768]{1,0:T(8,128)(2,1)}) %all-gather.5.cloned.1.call-update) | async-done | bytes 2359312 | tf_op jit(solution)/shard_map/all_gather | solution.py:154
  62.6 49.8 %all-gather.3.cloned.1.call-done = bf16[768,3352]{1,0:T(8,128)(2,1)} async-done(((bf16[48,3352]{1,0:T(8,128)(2,1)}), bf16[768,3352]{1,0:T(8,128)(2,1)}) %all-gather.3.cloned.1.call-update) | async-done | bytes 5148688 | tf_op jit(solution)/shard_map/all_gather | solution.py:153
  112.5 8.7 convolution_bitcast_fusion
  121.2 9.7 convolution_bitcast_fusion.1
  135.3 8.4 slice.270
  145.8 28.0 %fusion.47 = (f32[1,1024,1792]{1,2,0:T(8,128)}, f32[1,1024,1792]{1,2,0:T(8,128)}, f32[1,1024,1792]{1,2,0:T(8,128)}, f32[1,1024,1792]{1,2,0:T(8,128)}) fusion(f32[1024]{0:T(1024)S(1)} %bitcast.611, f32[1,1024,1792]{1,2,0:T(8,128)} %slice.270, f32[1792]{0:T(1024)S(1)} %get-tuple-element.69, f32[1024]{0:T(1024)S(1)} %bitcast.596, ...), kind=kLoop, calls=%fused_computation.80 | loop fusion | flops 58720256 | bytes 44108800 | tf_op jit(solution)/shard_map/jvp(jit(silu))/mul | solution.py:32
  181.6 8.1 reshape.1899
  189.7 8.1 reshape.1912
  211.1 8.2 reshape.1916
  219.3 8.1 reshape.1929
  236.4 10.0 fusion.151
  254.3 30.9 %fusion.55 = f32[1,4,256,24,64]{2,4,3,1,0:T(8,128)} fusion(f32[4,256,24,64]{1,3,2,0:T(8,128)S(1)} %fusion.146, f32[1,4,256,24,64]{2,1,4,3,0:T(4,128)S(1)} %bitcast.556, f32[24]{0:T(128)S(1)} %copy-done.167, f32[4,256,24]{1,2,0:T(8,128)S(1)} %bitcast.577, f32[4,256,256]{2,1,0:T(8,128)S(1)} %fusion.284, f32[4,256,256]{2,1,0:T(8,128)S(1)} %copy-done.62, ...), kind=kOutput, calls=%fused_computation.104 | convolution fusion | flops 4864868352 | bytes 27820128 | tf_op jit(solution)/shard_map/jvp(skhij,skjhp->skihp)/dot_general | solution.py:56
  285.3 10.3 copy.351
  295.6 8.2 reshape.1913
  319.6 9.9 fusion.154
  337.6 30.8 %fusion.54 = f32[1,4,256,24,64]{2,4,3,1,0:T(8,128)} fusion(f32[4,256,24,64]{1,3,2,0:T(8,128)S(1)} %fusion.145, f32[1,4,256,24,64]{2,1,4,3,0:T(4,128)S(1)} %bitcast.552, f32[4,256,24]{1,2,0:T(8,128)S(1)} %bitcast.580, f32[24]{0:T(128)S(1)} %copy-done.167, f32[4,256,256]{2,1,0:T(8,128)S(1)} %fusion.285, f32[4,256,256]{2,1,0:T(8,128)S(1)} %copy-done.60, ...), kind=kOutput, calls=%fused_computation.102 | convolution fusion | flops 4864868352 | bytes 27820128 | tf_op jit(solution)/shard_map/jvp(skhij,skjhp->skihp)/dot_general | solution.py:56
  368.4 10.4 copy.366
  378.7 8.4 reshape.1930
  398.9 8.0 fusion.57
  407.0 24.2 %multiply_reduce_fusion.11 = (f32[1536]{0:T(1024)}, f32[1,1024,1536]{1,2,0:T(8,128)}, bf16[1024,1536]{0,1:T(8,128)(2,1)}, bf16[1024,1536]{0,1:T(8,128)(2,1)}, f32[1536]{0:T(1024)}, /*index=5*/f32[1,1024,1536]{1,2,0:T(8,128)}) fusion(f32[1,1024,1792]{1,2,0:T(8,128)} %get-tuple-element.109, f32[1,1024,3352]{1,2,0:T(8,128)} %convolution_bitcast_fusion.1, ...), kind=kLoop, calls=%fused_computation.128 | loop fusion | flops 62911488 | bytes 81823744 | tf_op jit(solution)/shard_map/transpose(jvp())/reduce_sum | solution.py:87
  431.1 8.1 reshape.1933
  439.2 8.2 reshape.1934
  447.4 13.8 %fusion.173 = f32[4,256,128]{2,1,0:T(8,128)} fusion(f32[1,1,24,64,128]{4,3,2,1,0:T(8,128)S(1)} %copy-done.37, f32[1,1,24,64,128]{4,3,2,1,0:T(8,128)S(1)} %copy-done.39, f32[1,1,24,64,128]{4,3,2,1,0:T(8,128)} %copy-done.40, f32[4]{0:T(128)S(1)} %pad.172.clone, f32[4,256,24,64]{1,0,3,2:T(4,128)} %reshape.1933, f32[4,256,24]{1,2,0:T(8,128)S(1)} %bitcast.578), kind=kOutput, calls=%fused_computation.253 | convolution fusion | flops 2419851264 | bytes 9273360 | tf_op jit(solution)/shard_map/transpose(jvp(skin,skhpn->skihp))/dot_general | solution.py:84
  461.3 7.7 fusion.150
  469.0 8.4 reshape.1948
  477.5 8.2 reshape.1949
  485.7 14.2 %fusion.172 = f32[4,256,128]{2,1,0:T(8,128)} fusion(f32[1,1,24,64,128]{4,3,2,1,0:T(8,128)} %copy-done.41, f32[1,1,24,64,128]{4,3,2,1,0:T(8,128)} %copy-done.42, f32[1,1,24,64,128]{4,3,2,1,0:T(8,128)} %copy-done.43, f32[4]{0:T(128)S(1)} %pad.172.clone, f32[4,256,24,64]{1,0,3,2:T(4,128)} %reshape.1948, f32[4,256,24]{1,2,0:T(8,128)S(1)} %bitcast.581), kind=kOutput, calls=%fused_computation.252 | convolution fusion | flops 2419851264 | bytes 9273360 | tf_op jit(solution)/shard_map/transpose(jvp(skin,skhpn->skihp))/dot_general | solution.py:84
  531.6 42.5 %fusion.13 = (f32[4,24,256]{2,1,0:T(8,128)}, f32[4,24,256]{2,1,0:T(8,128)}, f32[4,256,256]{2,1,0:T(8,128)S(1)}) fusion(f32[4,256,256]{2,1,0:T(8,128)S(1)} %copy-done.57, f32[4,256,256]{2,1,0:T(8,128)} %get-tuple-element.145, f32[4,24,256]{2,1,0:T(8,128)S(1)} %copy-done.100, pred[4,256,256]{2,1,0:T(8,128)(4,1)S(1)} %copy-done.91, ...), kind=kOutput, calls=%fused_computation.15 | convolution fusion | flops 4902305792 | bytes 16384000 | tf_op jit(solution)/shard_map/transpose(jvp(skhij,skjhp->skihp))/dot_general | solution.py:56
  593.9 27.8 %fusion.63 = (f32[4,256,24]{1,2,0:T(8,128)}, f32[4,256,24]{1,2,0:T(8,128)}, f32[1,4,256,24,64]{2,4,3,1,0:T(8,128)S(1)}) fusion(f32[4,24,64,256]{3,2,1,0:T(8,128)S(1)} %fusion.111, f32[1,4,256,24,64]{2,1,4,3,0:T(4,128)S(1)} %bitcast.558, f32[4,256,24]{1,2,0:T(8,128)S(1)} %copy-done.67, f32[1,4,256,24,64]{2,1,4,3,0:T(4,128)} %reshape.1934, ...), kind=kOutput, calls=%fused_computation.119 | convolution fusion | flops 4872683520 | bytes 28016736 | tf_op jit(solution)/shard_map/transpose(jvp(skhij,skjhp->skihp))/dot_general | solution.py:56
  621.7 7.6 copy.380
  629.3 8.4 reshape.1939
  637.8 42.5 %fusion.15 = (f32[4,24,256]{2,1,0:T(8,128)}, f32[4,24,256]{2,1,0:T(8,128)}, f32[4,256,256]{2,1,0:T(8,128)S(1)}) fusion(f32[4,256,256]{2,1,0:T(8,128)S(1)} %copy-done.59, f32[4,256,256]{2,1,0:T(8,128)S(1)} %copy-done.61, f32[4,24,256]{2,1,0:T(8,128)} %copy-done.102, pred[4,256,256]{2,1,0:T(8,128)(4,1)} %get-tuple-element.149, ...), kind=kOutput, calls=%fused_computation.17 | convolution fusion | flops 4902305792 | bytes 16384000 | tf_op jit(solution)/shard_map/transpose(jvp(skhij,skjhp->skihp))/dot_general | solution.py:56
  699.8 28.2 %fusion.58 = (f32[4,256,24]{1,2,0:T(8,128)}, f32[4,256,24]{1,2,0:T(8,128)}, f32[1,4,256,24,64]{2,4,3,1,0:T(8,128)S(1)}) fusion(f32[4,24,64,256]{3,2,1,0:T(8,128)S(1)} %fusion.108, f32[1,4,256,24,64]{2,1,4,3,0:T(4,128)S(1)} %bitcast.554, f32[4,256,24]{1,2,0:T(8,128)S(1)} %copy-done.73, f32[1,4,256,24,64]{2,1,4,3,0:T(4,128)} %reshape.1949, ...), kind=kOutput, calls=%fused_computation.111 | convolution fusion | flops 4872683520 | bytes 28016736 | tf_op jit(solution)/shard_map/transpose(jvp(skhij,skjhp->skihp))/dot_general | solution.py:56
  728.0 7.7 copy.405
  735.8 8.4 reshape.1954
  752.6 10.0 reduce-window.34
  774.1 22.6 %fusion.267 = (f32[1792]{0:T(1024)}, f32[1792]{0:T(1024)}, f32[1792]{0:T(1024)}, f32[1792]{0:T(1024)}, f32[1792]{0:T(1024)}, /*index=5*/f32[1,1024,1792]{1,2,0:T(8,128)}) fusion(f32[1,1024,3352]{1,2,0:T(8,128)} %convolution_bitcast_fusion.1, f32[1024]{0:T(1024)S(1)} %bitcast.613, f32[1,1024,1792]{1,2,0:T(8,128)} %slice.270, f32[1024]{0:T(1024)S(1)} %bitcast.595, ...), kind=kLoop, calls=%fused_computation.431 | loop fusion | flops 44031232 | bytes 36752384 | tf_op jit(solution)/shard_map/transpose(jvp())/reduce_sum | solution.py:25
  796.8 15.8 %fusion.266 = (f32[1792]{0:T(1024)}, f32[1792]{0:T(1024)}, f32[1792]{0:T(1024)}, f32[1792]{0:T(1024)}, f32[1792]{0:T(1024)}, /*index=5*/f32[1,1024,1792]{1,2,0:T(8,128)}) fusion(f32[1,1024,3352]{1,2,0:T(8,128)} %copy-done.4, f32[1024]{0:T(1024)S(1)} %bitcast.616, f32[1,1024,1792]{1,2,0:T(8,128)S(1)} %bitcast.538, f32[1024]{0:T(1024)S(1)} %bitcast.604, ...), kind=kLoop, calls=%fused_computation.430 | loop fusion | flops 44031232 | bytes 36752384 | tf_op jit(solution)/shard_map/transpose(jvp())/reduce_sum | solution.py:25
  812.9 10.0 reduce-window.36
  826.0 24.1 %multiply_multiply_fusion.3 = (f32[1,1024,1792]{1,2,0:T(8,128)}, f32[1,1024,1792]{1,2,0:T(8,128)}, f32[1,1024,1792]{1,2,0:T(8,128)}, f32[1,1024,1792]{1,2,0:T(8,...) fusion(f32[1,1024,1792]{1,2,0:T(8,128)} %get-tuple-element.91, ...), kind=kLoop, calls=%fused_computation.86 | loop fusion | flops 29360128 | bytes 73461760 | tf_op jit(solution)/shard_map/transpose(jvp())/mul | solution.py:31
  850.1 14.3 %fusion.90 = bf16[1024,1792]{0,1:T(8,128)(2,1)} fusion(f32[1,1024,1792]{1,2,0:T(8,128)} %get-tuple-element.154, f32[1,1024,1792]{1,2,0:T(8,128)} %get-tuple-element.153, f32[1,1024,1792]{1,2,0:T(8,128)} %get-tuple-element.152, f32[1,1024,1792]{1,2,0:T(8,128)} %get-tuple-element.155), kind=kLoop, calls=%fused_computation.178 | loop fusion | flops 7340032 | bytes 33030144 | tf_op jit(solution)/shard_map/concatenate | solution.py:202
  864.8 10.9 %fusion.91 = bf16[1024,1792]{0,1:T(8,128)(2,1)} fusion(f32[1,1024,1792]{1,2,0:T(8,128)S(1)} %copy-done.7, f32[1,1024,1792]{1,2,0:T(8,128)} %get-tuple-element.130, f32[1,1024,1792]{1,2,0:T(8,128)} %get-tuple-element.131, f32[1,1024,1792]{1,2,0:T(8,128)S(1)} %copy-done.6), kind=kLoop, calls=%fused_computation.179 | loop fusion | flops 7340032 | bytes 33030144 | tf_op jit(solution)/shard_map/concatenate | solution.py:202
  875.8 13.3 %fusion.135 = f32[768,3352]{1,0:T(8,128)} fusion(bf16[1024,24]{0,1:T(8,128)(2,1)S(1)} %bitcast.617, bf16[1024,1792]{0,1:T(8,128)(2,1)} %fusion.90, bf16[1024,1536]{0,1:T(8,128)(2,1)} %get-tuple-element.122, f32[768]{0:T(1024)S(1)} %copy-done.162, f32[1024]{0:T(1024)S(1)} %copy-done.156, bf16[2,1024,768]{2,1,0:T(8,128)(2,1)S(1)} %copy-done.16), kind=kOutput, calls=%fused_computation.229 | convolution fusion | flops 5295980544 | bytes 18743296 | tf_op jit(solution)/shard_map/srd,sre->de/dot_general | solution.py:205
  889.1 16.3 %convolution_add_fusion = f32[768,3352]{1,0:T(8,128)} fusion(f32[768,3352]{1,0:T(8,128)} %fusion.135, bf16[1024,24]{0,1:T(8,128)(2,1)S(1)} %bitcast.619, bf16[1024,1792]{0,1:T(8,128)(2,1)} %fusion.91, bf16[1024,1536]{0,1:T(8,128)(2,1)} %get-tuple-element.156, f32[1024]{0:T(1024)S(1)} %copy-done.154, f32[768]{0:T(1024)S(1)} %copy-done.162, ...), kind=kOutput, calls=%fused_computation.82 | convolution fusion | flops 5298554880 | bytes 29040640 | tf_op jit(solution)/shard_map/srd,sre->de/dot_general | solution.py:205
  906.3 11.1 %fusion.134 = f32[1024,768]{1,0:T(8,128)} fusion(bf16[768,3352]{1,0:T(8,128)(2,1)} %all-gather.3.cloned.1.call-done, bf16[1024,24]{0,1:T(8,128)(2,1)S(1)} %bitcast.620, bf16[1024,1792]{0,1:T(8,128)(2,1)} %fusion.91, bf16[1024,1536]{0,1:T(8,128)(2,1)} %get-tuple-element.156), kind=kOutput, calls=%fused_computation.228 | convolution fusion | flops 5292834816 | bytes 15159296 | tf_op jit(solution)/shard_map/sre,de->srd/dot_general | solution.py:208
  917.5 13.9 %fusion.95 = (f32[768]{0:T(1024)S(1)}, f32[1024]{0:T(1024)S(1)}, f32[1024]{0:T(1024)S(1)}, f32[768]{0:T(1024)S(1)}, f32[1024,768]{1,0:T(8,128)}) fusion(f32[1024]{0:T(1024)S(1)} %copy-done.156, bf16[2,1024,768]{2,1,0:T(8,128)(2,1)S(1)} %copy-done.16, f32[768]{0:T(1024)S(1)} %copy-done.162, f32[1024,768]{1,0:T(8,128)} %fusion.134, ...), kind=kOutput, calls=%fused_computation.183 | convolution fusion | flops 5303840768 | bytes 21476352 | tf_op jit(solution)/shard_map/sre,de->srd/dot_general | solution.py:208
  948.1 77.1 %reduce-scatter.3.cloned.1.call-done = f32[48,3352]{1,0:T(8,128)} async-done(((f32[768,3352]{1,0:T(8,128)}), f32[48,3352]{1,0:T(8,128)}) %reduce-scatter.3.cloned.1.call-update) | async-done | bytes 643600 | tf_op jit(solution)/shard_map/reduce_scatter | solution.py:221
  1027.6 41.9 %all-reduce.42 = (f32[768]{0:T(1024)}, f32[4,1792]{1,0:T(4,128)}, f32[1792]{0:T(1024)}, f32[24]{0:T(128)}, f32[24]{0:T(128)}, /*index=5*/f32[24]{0:T(128)}, f32[1536]{0:T(1024)}) all-reduce(f32[768]{0:T(1024)S(1)} %add.394, f32[4,1792]{1,0:T(4,128)S(1)} %add_add_fusion.4, ...), channel_id=1, replica_groups=mesh['dp'=16,'seq'=2] {'dp','seq'}, use_global_device_ids=true, to_apply=%region_38.40 | all-reduce | flops 11336 | bytes 90688 | tf_op jit(solution)/shard_map/psum | solution.py:228
  (622 shorter events, 221.7 us)
Async XLA Ops:
  7.2 48.1 %all-gather.5.cloned.1.call-start = ((), (), s32[]{:S(2)}) async-start(), calls=%async_computation.3 | async-start | bytes 2506752 | tf_op jit(solution)/shard_map/all_gather | solution.py:154
  7.9 104.6 %all-gather.3.cloned.1.call-start = ((), (), s32[]{:S(2)}) async-start(), calls=%async_computation.2 | async-start | bytes 5640192 | tf_op jit(solution)/shard_map/all_gather | solution.py:153
  8.7 937.7 %reduce-scatter.5.cloned.1.call-start = ((), (), s32[]{:S(2)}) async-start(), calls=%async_computation.5 | async-start | bytes 5013504 | tf_op jit(solution)/shard_map/reduce_scatter | solution.py:222
  13.2 132.4 %copy-start.106 = (f32[1792]{0:T(1024)}, f32[1792]{0:T(1024)S(1)}, u32[]{:S(2)}) copy-start(f32[1792]{0:T(1024)S(1)} %get-tuple-element.67) | copy-start | bytes 21508
  13.3 132.4 %copy-start.108 = (f32[1792]{0:T(1024)}, f32[1792]{0:T(1024)S(1)}, u32[]{:S(2)}) copy-start(f32[1792]{0:T(1024)S(1)} %get-tuple-element.68) | copy-start | bytes 21508
  13.3 132.4 %copy-start.110 = (f32[1792]{0:T(1024)}, f32[1792]{0:T(1024)S(1)}, u32[]{:S(2)}) copy-start(f32[1792]{0:T(1024)S(1)} %get-tuple-element.69) | copy-start | bytes 21508
  13.3 132.4 %copy-start.111 = (f32[1792]{0:T(1024)}, f32[1792]{0:T(1024)S(1)}, u32[]{:S(2)}) copy-start(f32[1792]{0:T(1024)S(1)} %get-tuple-element.70) | copy-start | bytes 21508
  14.0 117.0 %copy-start.164 = (f32[24]{0:T(128)}, f32[24]{0:T(128)S(1)}, u32[]{:S(2)}) copy-start(f32[24]{0:T(128)S(1)} %exponential_negate_fusion) | copy-start | bytes 292
  16.6 95.9 %copy-start.153 = (f32[1024]{0:T(1024)}, f32[1024]{0:T(1024)S(1)}, u32[]{:S(2)}) copy-start(f32[1024]{0:T(1024)S(1)} %fusion.238) | copy-start | bytes 12292
  16.6 104.6 %copy-start.155 = (f32[1024]{0:T(1024)}, f32[1024]{0:T(1024)S(1)}, u32[]{:S(2)}) copy-start(f32[1024]{0:T(1024)S(1)} %fusion.236) | copy-start | bytes 12292
  16.7 212.6 %copy-start.130 = (f32[4,256]{1,0:T(4,128)}, f32[4,256]{1,0:T(4,128)S(1)}, u32[]{:S(2)}) copy-start(f32[4,256]{1,0:T(4,128)S(1)} %get-tuple-element.165) | copy-start | bytes 12292
  16.7 213.9 %copy-start.132 = (f32[4,256]{1,0:T(4,128)}, f32[4,256]{1,0:T(4,128)S(1)}, u32[]{:S(2)}) copy-start(f32[4,256]{1,0:T(4,128)S(1)} %get-tuple-element.166) | copy-start | bytes 12292
  16.7 295.7 %copy-start.128 = (f32[4,256]{1,0:T(4,128)}, f32[4,256]{1,0:T(4,128)S(1)}, u32[]{:S(2)}) copy-start(f32[4,256]{1,0:T(4,128)S(1)} %get-tuple-element.170) | copy-start | bytes 12292
  16.7 297.0 %copy-start.131 = (f32[4,256]{1,0:T(4,128)}, f32[4,256]{1,0:T(4,128)S(1)}, u32[]{:S(2)}) copy-start(f32[4,256]{1,0:T(4,128)S(1)} %get-tuple-element.171) | copy-start | bytes 12292
  16.8 128.8 %copy-start.112 = (f32[1,1024]{1,0:T(1,128)}, f32[1,1024]{1,0:T(1,128)S(1)}, u32[]{:S(2)}) copy-start(f32[1,1024]{1,0:T(1,128)S(1)} %get-tuple-element.167) | copy-start | bytes 12292
  16.9 128.8 %copy-start.114 = (f32[1,1024]{1,0:T(1,128)}, f32[1,1024]{1,0:T(1,128)S(1)}, u32[]{:S(2)}) copy-start(f32[1,1024]{1,0:T(1,128)S(1)} %get-tuple-element.168) | copy-start | bytes 12292
  16.9 128.8 %copy-start.116 = (f32[1,1024]{1,0:T(1,128)}, f32[1,1024]{1,0:T(1,128)S(1)}, u32[]{:S(2)}) copy-start(f32[1,1024]{1,0:T(1,128)S(1)} %get-tuple-element.169) | copy-start | bytes 12292
  17.0 128.7 %copy-start.118 = (f32[1,1024]{1,0:T(1,128)}, f32[1,1024]{1,0:T(1,128)S(1)}, u32[]{:S(2)}) copy-start(f32[1,1024]{1,0:T(1,128)S(1)} %get-tuple-element.172) | copy-start | bytes 12292
  17.0 128.7 %copy-start.120 = (f32[1,1024]{1,0:T(1,128)}, f32[1,1024]{1,0:T(1,128)S(1)}, u32[]{:S(2)}) copy-start(f32[1,1024]{1,0:T(1,128)S(1)} %get-tuple-element.173) | copy-start | bytes 12292
  17.0 128.7 %copy-start.122 = (f32[1,1024]{1,0:T(1,128)}, f32[1,1024]{1,0:T(1,128)S(1)}, u32[]{:S(2)}) copy-start(f32[1,1024]{1,0:T(1,128)S(1)} %get-tuple-element.174) | copy-start | bytes 12292
  17.8 127.9 %copy-start.124 = (f32[1,1024]{1,0:T(1,128)}, f32[1,1024]{1,0:T(1,128)S(1)}, u32[]{:S(2)}) copy-start(f32[1,1024]{1,0:T(1,128)S(1)} %get-tuple-element.163) | copy-start | bytes 12292
  17.8 127.9 %copy-start.126 = (f32[1,1024]{1,0:T(1,128)}, f32[1,1024]{1,0:T(1,128)S(1)}, u32[]{:S(2)}) copy-start(f32[1,1024]{1,0:T(1,128)S(1)} %get-tuple-element.164) | copy-start | bytes 12292
  19.9 92.6 %copy-start.15 = (bf16[2,1024,768]{2,1,0:T(8,128)(2,1)S(1)}, bf16[2,1024,768]{2,1,0:T(8,128)(2,1)}, u32[]{:S(2)}) copy-start(bf16[2,1024,768]{2,1,0:T(8,128)(2,1)} %param.13) | copy-start | bytes 9437188
  19.9 92.6 %copy-start.161 = (f32[768]{0:T(1024)S(1)}, f32[768]{0:T(1024)}, u32[]{:S(2)}) copy-start(f32[768]{0:T(1024)} %param.16) | copy-start | bytes 9220
  132.6 98.9 %copy-start.74 = (f32[1,1024,24]{1,2,0:T(8,128)}, f32[1,1024,24]{1,2,0:T(8,128)S(1)}, u32[]{:S(2)}) copy-start(f32[1,1024,24]{1,2,0:T(8,128)S(1)} %get-tuple-element.108) | copy-start | bytes 294916
  231.7 299.8 %copy-start.65 = (f32[4,256,24]{1,2,0:T(8,128)}, f32[4,256,24]{1,2,0:T(8,128)S(1)}, u32[]{:S(2)}) copy-start(f32[4,256,24]{1,2,0:T(8,128)S(1)} %copy.337) | copy-start | bytes 294916
  311.3 95.7 %copy-start.95 = (f32[1024]{0:T(1024)}, f32[1024]{0:T(1024)S(1)}, u32[]{:S(2)}) copy-start(f32[1024]{0:T(1024)S(1)} %fusion.237) | copy-start | bytes 12292
  393.5 131.5 %copy-start.97 = (f32[1024]{0:T(1024)}, f32[1024]{0:T(1024)S(1)}, u32[]{:S(2)}) copy-start(f32[1024]{0:T(1024)S(1)} %fusion.239) | copy-start | bytes 12292
  531.4 42.7 %copy-start.33 = (f32[4,256,128]{2,1,0:T(8,128)S(1)}, f32[4,256,128]{2,1,0:T(8,128)}, u32[]{:S(2)}) copy-start(f32[4,256,128]{2,1,0:T(8,128)} %copy-done.32) | copy-start | bytes 1572868
  531.4 48.5 %copy-start.25 = (f32[4,256,128,1]{2,1,3,0:T(8,128)S(1)}, f32[4,256,128,1]{2,1,3,0:T(8,128)}, u32[]{:S(2)}) copy-start(f32[4,256,128,1]{2,1,3,0:T(8,128)} %copy-done.24) | copy-start | bytes 1572868
  531.4 493.7 %reduce-scatter.3.cloned.1.call-start = ((), (), s32[]{:S(2)}) async-start(), calls=%async_computation.4 | async-start | bytes 11280384 | tf_op jit(solution)/shard_map/reduce_scatter | solution.py:221
  531.5 44.5 %copy-start.29 = (f32[4,256,128]{2,1,0:T(8,128)S(1)}, f32[4,256,128]{2,1,0:T(8,128)}, u32[]{:S(2)}) copy-start(f32[4,256,128]{2,1,0:T(8,128)} %copy-done.28) | copy-start | bytes 1572868
  531.5 44.5 %copy-start.79 = (f32[4,256,128]{2,1,0:T(8,128)S(1)}, f32[4,256,128]{2,1,0:T(8,128)}, u32[]{:S(2)}) copy-start(f32[4,256,128]{2,1,0:T(8,128)} %fusion.173) | copy-start | bytes 1572868
  637.7 42.5 %copy-start.35 = (f32[4,256,128]{2,1,0:T(8,128)S(1)}, f32[4,256,128]{2,1,0:T(8,128)}, u32[]{:S(2)}) copy-start(f32[4,256,128]{2,1,0:T(8,128)} %copy-done.34) | copy-start | bytes 1572868
  637.8 44.4 %copy-start.31 = (f32[4,256,128]{2,1,0:T(8,128)S(1)}, f32[4,256,128]{2,1,0:T(8,128)}, u32[]{:S(2)}) copy-start(f32[4,256,128]{2,1,0:T(8,128)} %copy-done.30) | copy-start | bytes 1572868
  637.8 44.4 %copy-start.78 = (f32[4,256,128]{2,1,0:T(8,128)S(1)}, f32[4,256,128]{2,1,0:T(8,128)}, u32[]{:S(2)}) copy-start(f32[4,256,128]{2,1,0:T(8,128)} %fusion.172) | copy-start | bytes 1572868
  637.8 48.4 %copy-start.27 = (f32[4,256,128,1]{2,1,3,0:T(8,128)S(1)}, f32[4,256,128,1]{2,1,3,0:T(8,128)}, u32[]{:S(2)}) copy-start(f32[4,256,128,1]{2,1,3,0:T(8,128)} %copy-done.26) | copy-start | bytes 1572868
  735.8 60.9 %slice-start.8 = ((s8[7340032]{0:T(1024)(128)(4,1)}), s8[3145728]{0:T(1024)(128)(4,1)S(1)}, s32[]{:S(2)}) async-start(s8[7340032]{0:T(1024)(128)(4,1)} %bitcast.537), calls=%async_computation.15 | async-start | bytes 6291456
  905.6 169.6 %all-reduce.46.cloned.1.call-start = ((), (), s32[]{:S(2)}) async-start(), calls=%async_computation.6 | async-start | bytes 958464 | tf_op jit(solution)/shard_map/psum | solution.py:225
  941.9 85.1 %copy-start.165 = (f32[24]{0:T(128)S(1)}, f32[24]{0:T(128)}, u32[]{:S(2)}) copy-start(f32[24]{0:T(128)} %param.21) | copy-start | bytes 292
  942.0 85.1 %copy-start.140 = (f32[1536]{0:T(1024)S(1)}, f32[1536]{0:T(1024)}, u32[]{:S(2)}) copy-start(f32[1536]{0:T(1024)} %get-tuple-element.84) | copy-start | bytes 18436
  942.0 85.3 %copy-start.139 = (f32[1536]{0:T(1024)S(1)}, f32[1536]{0:T(1024)}, u32[]{:S(2)}) copy-start(f32[1536]{0:T(1024)} %get-tuple-element.157) | copy-start | bytes 18436
  942.0 85.5 %copy-start.137 = (f32[1536]{0:T(1024)S(1)}, f32[1536]{0:T(1024)}, u32[]{:S(2)}) copy-start(f32[1536]{0:T(1024)} %get-tuple-element.33) | copy-start | bytes 18436
  942.0 85.5 %copy-start.138 = (f32[1536]{0:T(1024)S(1)}, f32[1536]{0:T(1024)}, u32[]{:S(2)}) copy-start(f32[1536]{0:T(1024)} %get-tuple-element.160) | copy-start | bytes 18436
  942.0 85.5 %copy-start.141 = (f32[1792]{0:T(1024)S(1)}, f32[1792]{0:T(1024)}, u32[]{:S(2)}) copy-start(f32[1792]{0:T(1024)} %get-tuple-element.40) | copy-start | bytes 21508
  942.0 85.5 %copy-start.142 = (f32[1792]{0:T(1024)S(1)}, f32[1792]{0:T(1024)}, u32[]{:S(2)}) copy-start(f32[1792]{0:T(1024)} %get-tuple-element.35) | copy-start | bytes 21508
  946.3 127.0 %copy-start.54 = (bf16[1,1024,768]{2,1,0:T(8,128)(2,1)S(1)}, bf16[1,1024,768]{2,1,0:T(8,128)(2,1)}, u32[]{:S(2)}) copy-start(bf16[1,1024,768]{2,1,0:T(8,128)(2,1)} %fusion.101) | copy-start | bytes 4718596
  946.3 127.0 %copy-start.55 = (bf16[1,1024,768]{2,1,0:T(8,128)(2,1)S(1)}, bf16[1,1024,768]{2,1,0:T(8,128)(2,1)}, u32[]{:S(2)}) copy-start(bf16[1,1024,768]{2,1,0:T(8,128)(2,1)} %fusion.105) | copy-start | bytes 4718596
  (155 other events, 1856.2 us)
Sparse Core Ops, SparseCore 0:
  10.3 44.9 all-gather.4
  57.4 55.0 all-gather.2
  531.5 74.1 reduce-scatter.4
  905.8 119.3 reduce-scatter.2
  1028.5 27.4 all-reduce.45
where the time goes:
time: 1100 us; the launch traced here: 1090 us
  matrix products  418 us (38%)
  other arithmetic  249 us (23%)
  local copies, waits for them, and re-layouts  195 us (18%)
  waiting for transfers between devices  164 us (15%)
  blocking collectives  41.9 us (4%)
  between operations  17.2 us (2%)
    dot_general x6, matrix products, state_space(): jnp.einsum('skhij,skjhp->skihp', decay_mat * scores[:, :, None], x_scaled...  203 us
    reduce_scatter x1, waiting for transfers between devices, per_device(): lax.psum_scatter(acc_in, 'dp', scatter_dimension=0, tiled=True)  77.1 us
    dot_general x6, matrix products, state_space(): jnp.einsum('skin,skhpn->skihp', c_blocks, entering, precision=highest)  52.8 us
    all_gather x1, waiting for transfers between devices, per_device(): lax.all_gather(weight_in, 'dp', axis=0, tiled=True)  49.8 us
    dot_general x6, matrix products, state_space(): jnp.einsum('skjhp,skjn->skhpn', x_scaled * to_end[..., None], b_blocks, p...  45.3 us
    psum x1, blocking collectives, per_device(): lax.psum((acc_ngain, acc_cw, acc_cb, acc_dtb, acc_alog, acc_skip, acc_gga...  41.9 us
    reduce_sum x2, other arithmetic, causal_conv(): summed = jnp.zeros_like(padded[:, tap_count - 1:, :]) + conv_bias  38.4 us
    all_gather x1, waiting for transfers between devices, per_device(): lax.all_gather(weight_out, 'dp', axis=0, tiled=True)  35.4 us
  transfers between devices with their start and end apart: 5, of which 3 were waited for; matrix products, arithmetic and copies ran while one was open for 40% of the time, Pallas kernels for 0%

commit v1 on v0

v1 whole, which is shorter than its diff:
```python
import math

import jax
import jax.numpy as jnp
from jax import lax
from jax.experimental import pallas as pl
from jax.experimental.pallas import tpu as pltpu
from jax.sharding import PartitionSpec as P

f32 = jnp.float32
bf16 = jnp.bfloat16
Q = 128
LANES = 128
EPS = 1e-05
LOG2E = math.log2(math.e)
NEG = -1e30

NN = (((1,), (0,)), ((), ()))
NT = (((1,), (1,)), ((), ()))
TN = (((0,), (0,)), ((), ()))


def dot(a, b, dims=NN):
    return lax.dot_general(a, b, dims, preferred_element_type=f32)


def pair_split(v):
    return jnp.concatenate(split(v, 2), axis=1)


def twice(v, axis):
    return jnp.concatenate([v, v], axis=axis)


def dot_split(a, b):
    low = b[1]
    return dot(jnp.concatenate(a, axis=1), twice(b[0], 1), NT) + dot(a[0], low, NT)


def sigmoid(v):
    return 0.5 + 0.5 * jnp.tanh(0.5 * v)


def split(v, parts):
    out = []
    for _ in range(parts):
        low = v.astype(bf16)
        out.append(low)
        v = v - low.astype(f32)
    return out


def fold_rows(v):
    return jnp.sum(v.reshape(v.shape[0] // 8, 8, v.shape[1]), axis=0)


def wide(v, width):
    col = jnp.broadcast_to(v, (v.shape[0], LANES))
    return jnp.concatenate([col] * (width // LANES), axis=1)


def params(limit=None, **more):
    return pltpu.CompilerParams(vmem_limit_bytes=limit, **more)


def proj_kernel(tok_ref, gain_ref, wx_ref, normed_ref, xbc_ref, dt_ref):
    u = tok_ref[...].astype(f32)
    r = lax.rsqrt(jnp.mean(u * u, axis=-1, keepdims=True) + EPS)
    normed = (u * r * gain_ref[...]).astype(bf16)
    normed_ref[...] = normed
    out = dot(normed, wx_ref[...])
    ch = xbc_ref.shape[1]
    xbc_ref[...] = out[:, :ch]
    dt_ref[...] = out[:, ch:]


def project(tok, gain, wx, channels, tile=256):
    rows, width = tok.shape
    cols = wx.shape[1]
    return pl.pallas_call(
        proj_kernel,
        grid=(rows // tile,),
        in_specs=[
            pl.BlockSpec((tile, width), lambda i: (i, 0)),
            pl.BlockSpec((1, width), lambda i: (0, 0)),
            pl.BlockSpec((width, cols), lambda i: (0, 0)),
        ],
        out_specs=[
            pl.BlockSpec((tile, width), lambda i: (i, 0)),
            pl.BlockSpec((tile, channels), lambda i: (i, 0)),
            pl.BlockSpec((tile, cols - channels), lambda i: (i, 0)),
        ],
        out_shape=[
            jax.ShapeDtypeStruct((rows, width), bf16),
            jax.ShapeDtypeStruct((rows, channels), f32),
            jax.ShapeDtypeStruct((rows, cols - channels), f32),
        ],
        compiler_params=params(60 << 20),
        name="project",
    )(tok, gain, wx)


def table_columns(tab_ref):
    tab = tab_ref[...]
    reps = LANES // tab.shape[0]
    return tab, jnp.concatenate([tab] * reps, axis=0).T


def step_terms(dt, dtb, na2, tri, cols):
    raw = dt + dtb
    ts = jnp.maximum(raw, 0.0) + jnp.log1p(jnp.exp(-jnp.abs(raw)))
    cum = dot(jnp.concatenate([tri] * 3, axis=1), jnp.concatenate(split(ts * na2, 3), axis=0))
    start = jnp.exp2(cum) * wide(cols[:, 4:5], LANES)
    end = jnp.exp2(cum[Q - 1 : Q, :] - cum) * wide(cols[:, 5:6], LANES)
    return raw, ts, cum, start, end


def expand_operand(*terms):
    return jnp.concatenate([jnp.concatenate(split(t, 2), axis=1) for t in terms], axis=0)


def by_head(v, left):
    zero = jnp.zeros_like(v)
    return jnp.concatenate([jnp.where(left, v, zero), jnp.where(left, zero, v)], axis=0)


def fwd_kernel(
    tab_ref, xbc_ref, dt_ref, cw_ref, cb_ref, dtb_ref, na2_ref, skip_ref, e_ref, tri_ref,
    y_ref, s_ref, sin_ref, state, ext,
):
    inner = skip_ref.shape[1]
    channels = cb_ref.shape[1]
    b = pl.program_id(1)

    @pl.when(b == 0)
    def _():
        state[...] = jnp.zeros_like(state)
        ext[0:8, :] = jnp.zeros((8, channels), f32)

    @pl.when(b > 0)
    def _():
        ext[0:8, :] = ext[Q : Q + 8, :]

    ext[8 : 8 + Q, :] = xbc_ref[...]
    tab, cols = table_columns(tab_ref)
    m1, m2, m3 = (wide(cols[:, k : k + 1], 256) for k in (1, 2, 3))

    def conv(c):
        at = pl.ds(c, 256)
        s = cb_ref[:, at] + cw_ref[3:4, at] * ext[8 : 8 + Q, at]
        s += m1 * (cw_ref[2:3, at] * ext[7 : 7 + Q, at])
        s += m2 * (cw_ref[1:2, at] * ext[6 : 6 + Q, at])
        s += m3 * (cw_ref[0:1, at] * ext[5 : 5 + Q, at])
        s_ref[:, at] = s
        return s * sigmoid(s)

    bc, bc_rest = split(conv(inner), 2)
    bm, cm = bc[:, :LANES], bc[:, LANES:]
    bt = bm.T
    c_two = jnp.concatenate([cm, bc_rest[:, LANES:]], axis=1)
    _, ts, cum, start, end = step_terms(dt_ref[...], dtb_ref[...], na2_ref[...], tri_ref[...], cols)
    cum_t = cum.T
    grow = expand_operand(start, end, ts)
    row_i = lax.broadcasted_iota(jnp.int32, (Q, Q), 0)
    col_j = lax.broadcasted_iota(jnp.int32, (Q, Q), 1)
    same = wide(cols[:, 0:1], LANES) == tab[0:1, :]
    mask = jnp.where(same & (row_i >= col_j), 0.0, NEG)
    scores = dot_split((cm, bc_rest[:, LANES:]), (bm, bc_rest[:, :LANES]))
    left = col_j < LANES // 2

    for c in range(0, inner, 256):
        at = pl.ds(c, 256)
        x = conv(c)
        big = dot(grow, e_ref[:, at])
        s_e, e_e, t_e = big[:Q], big[Q : 2 * Q], big[2 * Q :]
        xs = x * t_e
        xs_low = xs.astype(bf16)
        st = state[:, at]
        st_low = st.astype(bf16)
        sin_ref[:, at] = st_low
        carried = dot(c_two, twice(st_low, 0))
        parts = []
        for p in range(2):
            mats = []
            for h in range(2):
                head = (c + p * LANES) // 64 + h
                gap = wide(cum[:, head : head + 1], LANES) - cum_t[head : head + 1, :] + mask
                mats.append((jnp.exp2(gap) * scores).astype(bf16))
            xp = xs_low[:, p * LANES : (p + 1) * LANES]
            parts.append(dot(jnp.concatenate(mats, axis=1), by_head(xp, left)))
        y = jnp.concatenate(parts, axis=1) + s_e * carried + skip_ref[:, at] * x
        y_ref[:, at] = y
        state[:, at] = st * s_e[Q - 1 : Q, :] + dot(bt, (xs * e_e).astype(bf16))


def fixed(shape):
    return pl.BlockSpec(shape, lambda *_: (0,) * len(shape))


def state_forward(tab, xbc, dt, cw, cb, dtb, na2, skip, e2, tri, seqs):
    rows, channels = xbc.shape
    inner = skip.shape[1]
    blocks = rows // seqs // Q
    at = lambda s, b: (s * blocks + b, 0)
    at3 = lambda s, b: (s * blocks + b, 0, 0)
    return pl.pallas_call(
        fwd_kernel,
        grid=(seqs, blocks),
        in_specs=[
            pl.BlockSpec((None, 16, LANES), at3),
            pl.BlockSpec((Q, channels), at),
            pl.BlockSpec((Q, LANES), at),
            fixed(cw.shape), fixed(cb.shape), fixed(dtb.shape), fixed(na2.shape), fixed(skip.shape),
            fixed(e2.shape), fixed(tri.shape),
        ],
        out_specs=[
            pl.BlockSpec((Q, inner), at),
            pl.BlockSpec((Q, channels), at),
            pl.BlockSpec((None, LANES, inner), at3),
        ],
        out_shape=[
            jax.ShapeDtypeStruct((rows, inner), f32),
            jax.ShapeDtypeStruct((rows, channels), f32),
            jax.ShapeDtypeStruct((seqs * blocks, LANES, inner), bf16),
        ],
        scratch_shapes=[pltpu.VMEM((LANES, inner), f32), pltpu.VMEM((Q + 8, channels), f32)],
        compiler_params=params(60 << 20),
        name="state_forward",
    )(tab, xbc, dt, cw, cb, dtb, na2, skip, e2, tri)


def gate_kernel(
    tok_ref, normed_ref, y_ref, cot_ref, wz_ref, wo_ref, gain_ref,
    gn_ref, out_ref, gz_ref, gm_ref, ggain_ref,
):
    z = dot(normed_ref[...], wz_ref[...])
    sg = sigmoid(z)
    sz = z * sg
    y = y_ref[...]
    gated = y * sz
    rstd = lax.rsqrt(jnp.mean(gated * gated, axis=-1, keepdims=True) + EPS)
    unit = gated * rstd
    gn = (unit * gain_ref[...]).astype(bf16)
    gn_ref[...] = gn
    out_ref[...] = (tok_ref[...].astype(f32) + dot(gn, wo_ref[...])).astype(bf16)
    g_gn = dot(cot_ref[...], wo_ref[...], NT)

    @pl.when(pl.program_id(0) == 0)
    def _():
        ggain_ref[...] = jnp.zeros_like(ggain_ref)

    ggain_ref[...] += fold_rows(unit * g_gn)
    q = g_gn * gain_ref[...]
    mean = jnp.mean(unit * q, axis=-1, keepdims=True)
    g_gated = rstd * (q - unit * mean)
    gm_ref[...] = g_gated * sz
    gz_ref[...] = (g_gated * y * (sg * (1.0 + z * (1.0 - sg)))).astype(bf16)


def gate(tok, normed, y, cot, wz, wo, gain, tile=256):
    rows, width = tok.shape
    inner = y.shape[1]
    at = lambda i: (i, 0)
    return pl.pallas_call(
        gate_kernel,
        grid=(rows // tile,),
        in_specs=[
            pl.BlockSpec((tile, width), at),
            pl.BlockSpec((tile, width), at),
            pl.BlockSpec((tile, inner), at),
            pl.BlockSpec((tile, width), at),
            fixed(wz.shape), fixed(wo.shape), fixed(gain.shape),
        ],
        out_specs=[
            pl.BlockSpec((tile, inner), at),
            pl.BlockSpec((tile, width), at),
            pl.BlockSpec((tile, inner), at),
            pl.BlockSpec((tile, inner), at),
            fixed((8, inner)),
        ],
        out_shape=[
            jax.ShapeDtypeStruct((rows, inner), bf16),
            jax.ShapeDtypeStruct((rows, width), bf16),
            jax.ShapeDtypeStruct((rows, inner), bf16),
            jax.ShapeDtypeStruct((rows, inner), f32),
            jax.ShapeDtypeStruct((8, inner), f32),
        ],
        compiler_params=params(60 << 20),
        name="gate",
    )(tok, normed, y, cot, wz, wo, gain)


def bwd_kernel(
    tab_ref, xbc_ref, dt_ref, s_ref, sin_ref, gm_ref, cw_ref, dtb_ref, na2_ref, na_ref, skip_ref,
    e_ref, et_ref, tri_ref, tail_ref, pair_ref,
    gx_ref, gcw_ref, gcb_ref, gskip_ref, galog_ref, gdtb_ref,
    adj, gext, da_rows, edge, spread, grad_b, grad_c, link,
):
    inner = skip_ref.shape[1]
    channels = s_ref.shape[1]
    heads = inner // 64
    b = pl.program_id(1)

    @pl.when((b == 0) & (pl.program_id(0) == 0))
    def _():
        for ref in (gcw_ref, gcb_ref, gskip_ref, galog_ref, gdtb_ref, da_rows):
            ref[...] = jnp.zeros_like(ref)

    @pl.when(b == 0)
    def _():
        adj[...] = jnp.zeros_like(adj)
        gext[Q : Q + 8, :] = jnp.zeros((8, channels), f32)

    @pl.when(b > 0)
    def _():
        gext[Q : Q + 8, :] = gext[0:8, :]

    tab, cols = table_columns(tab_ref)
    raw, ts, cum, start, end = step_terms(
        dt_ref[...], dtb_ref[...], na2_ref[...], tri_ref[...], cols
    )
    cum_t = cum.T
    grow = expand_operand(start, end, ts)

    def act(c):
        s = s_ref[:, pl.ds(c, 256)]
        sg = sigmoid(s)
        return s * sg, sg * (1.0 + s * (1.0 - sg))

    bc, slope_bc = act(inner)
    bc, bc_rest = split(bc, 2)
    bm, cm = bc[:, :LANES], bc[:, LANES:]
    ct = cm.T
    b_two = jnp.concatenate([bm, bc_rest[:, :LANES]], axis=1)
    c_two = jnp.concatenate([cm, bc_rest[:, LANES:]], axis=1)
    row_j = lax.broadcasted_iota(jnp.int32, (Q, Q), 0)
    col_i = lax.broadcasted_iota(jnp.int32, (Q, Q), 1)
    same = wide(cols[:, 0:1], LANES) == tab[0:1, :]
    mask = jnp.where(same & (col_i >= row_j), 0.0, NEG)
    before = (row_j < col_i).astype(f32)
    scores = dot_split((bm, bc_rest[:, :LANES]), (cm, bc_rest[:, LANES:]))
    left = col_i < LANES // 2
    grad_scores = jnp.zeros((Q, Q), f32)

    for c in range(0, inner, 256):
        at = pl.ds(c, 256)
        x, slope = act(c)
        big = dot(grow, e_ref[:, at])
        s_e, e_e, t_e = big[:Q], big[Q : 2 * Q], big[2 * Q :]
        xs = x * t_e
        xs_low, xs_rest = split(xs, 2)
        gm = gm_ref[:, at]
        gm_low, gm_rest = split(gm, 2)
        ad = adj[:, at]
        ad_low, ad_rest = split(ad, 2)
        st_low = sin_ref[:, at]
        into = dot(b_two, twice(ad_low, 0)) + dot(bm, ad_rest)
        carried = dot(c_two, twice(st_low, 0))
        parts = []
        for p in range(2):
            lanes = slice(p * LANES, (p + 1) * LANES)
            diag, diag_rest = by_head(gm_low[:, lanes], left), by_head(gm_rest[:, lanes], left)
            gmat = dot_split((xs_low[:, lanes], xs_rest[:, lanes]), (diag, diag_rest))
            mats, links = [], []
            for h in range(2):
                head = (c + p * LANES) // 64 + h
                gap = cum_t[head : head + 1, :] - wide(cum[:, head : head + 1], LANES) + mask
                decay = jnp.exp2(gap)
                mat = decay * scores
                grad = gmat[:, h * LANES : (h + 1) * LANES]
                grad_scores += decay * grad
                mats.append(split(mat, 2))
                links.append((mat * grad).astype(bf16))
            high = jnp.concatenate([mats[0][0], mats[1][0]], axis=1)
            rest = jnp.concatenate([mats[0][1], mats[1][1]], axis=1)
            parts.append(dot(high, diag) + dot(high, diag_rest) + dot(rest, diag))
            reach = dot(jnp.concatenate(links, axis=1), pair_ref[...])
            for h in range(2):
                head = (c + p * LANES) // 64 + h
                da_rows[head : head + 1, :] = jnp.sum(
                    reach[:, h * LANES : (h + 1) * LANES] * before, axis=0, keepdims=True
                )
        g_xs = jnp.concatenate(parts, axis=1) + e_e * into
        gext[0:Q, at] = (t_e * g_xs + skip_ref[:, at] * gm) * slope
        sums = jnp.concatenate(
            [pair_split(carried * gm), pair_split(x * into), pair_split(x * g_xs)], axis=0
        )
        sums = dot(sums, twice(et_ref[at, :], 0))
        s_gm = (s_e * gm).astype(bf16)
        part_c = dot(s_gm, st_low, NT)
        part_b = dot((e_e * xs).astype(bf16), ad_low, NT)
        if c == 0:
            spread[...] = sums
            grad_c[...] = part_c
            grad_b[...] = part_b
        else:
            spread[...] += sums
            grad_c[...] += part_c
            grad_b[...] += part_b
        gskip_ref[:, at] += fold_rows(gm * x)
        link[:, at] = fold_rows(st_low.astype(f32) * ad)
        adj[:, at] = ad * s_e[Q - 1 : Q, :] + dot(ct, s_gm)

    grad_low = grad_scores.astype(bf16)
    g_b = grad_b[...] + dot(grad_low, cm)
    g_c = grad_c[...] + dot(grad_low, bm, TN)
    gext[0:Q, pl.ds(inner, 256)] = jnp.concatenate([g_b, g_c], axis=1) * slope_bc

    phi = start * spread[0:Q]
    psi = end * ts * spread[Q : 2 * Q]
    through = jnp.sum(dot(jnp.concatenate(split(link[...], 2), axis=0), et_ref[...]), axis=0, keepdims=True)
    around = jnp.concatenate(split(phi, 2) + split(psi, 2), axis=0)
    da = da_rows[...].T + dot(tail_ref[...], around) + start[Q - 1 : Q, :] * through
    g_ts = spread[2 * Q :] + na_ref[...] * da
    galog_ref[...] += fold_rows(ts * na_ref[...] * da)
    g_dt = g_ts * sigmoid(raw)
    gdtb_ref[...] += fold_rows(g_dt)

    n1, n2, n3 = (wide(cols[:, k : k + 1], 256) for k in (6, 7, 8))
    for c in range(0, channels, 256):
        at = pl.ds(c, 256)
        x = xbc_ref[:, at]
        g0 = gext[0:Q, at]
        g1 = gext[1 : 1 + Q, at] * n1
        g2 = gext[2 : 2 + Q, at] * n2
        g3 = gext[3 : 3 + Q, at] * n3
        gx = cw_ref[3:4, at] * g0 + cw_ref[2:3, at] * g1 + cw_ref[1:2, at] * g2 + cw_ref[0:1, at] * g3
        gx_ref[:, at] = gx.astype(bf16)
        gcb_ref[:, at] += fold_rows(g0)
        gcw_ref[24:32, at] += fold_rows(g0 * x)
        gcw_ref[16:24, at] += fold_rows(g1 * x)
        gcw_ref[8:16, at] += fold_rows(g2 * x)
        gcw_ref[0:8, at] += fold_rows(g3 * x)
    gx_ref[:, channels:] = g_dt.astype(bf16)


def state_backward(tab, xbc, dt, s, sin, gm, cw, dtb, na2, na, skip, e2, et, tri, tail, pair, seqs):
    rows, channels = xbc.shape
    inner = skip.shape[1]
    blocks = rows // seqs // Q
    at = lambda s, b: (s * blocks + blocks - 1 - b, 0)
    at3 = lambda s, b: (s * blocks + blocks - 1 - b, 0, 0)
    return pl.pallas_call(
        bwd_kernel,
        grid=(seqs, blocks),
        in_specs=[
            pl.BlockSpec((None, 16, LANES), at3),
            pl.BlockSpec((Q, channels), at),
            pl.BlockSpec((Q, LANES), at),
            pl.BlockSpec((Q, channels), at),
            pl.BlockSpec((None, LANES, inner), at3),
            pl.BlockSpec((Q, inner), at),
        ]
        + [fixed(v.shape) for v in (cw, dtb, na2, na, skip, e2, et, tri, tail, pair)],
        out_specs=[
            pl.BlockSpec((Q, channels + LANES), at),
            fixed((32, channels)), fixed((8, channels)), fixed((8, inner)), fixed((8, LANES)), fixed((8, LANES)),
        ],
        out_shape=[
            jax.ShapeDtypeStruct((rows, channels + LANES), bf16),
            jax.ShapeDtypeStruct((32, channels), f32),
            jax.ShapeDtypeStruct((8, channels), f32),
            jax.ShapeDtypeStruct((8, inner), f32),
            jax.ShapeDtypeStruct((8, LANES), f32),
            jax.ShapeDtypeStruct((8, LANES), f32),
        ],
        scratch_shapes=[
            pltpu.VMEM((LANES, inner), f32),
            pltpu.VMEM((Q + 8, channels), f32),
            pltpu.VMEM((LANES, LANES), f32),
            pltpu.VMEM((8, LANES), f32),
            pltpu.VMEM((3 * Q, LANES), f32),
            pltpu.VMEM((Q, LANES), f32),
            pltpu.VMEM((Q, LANES), f32),
            pltpu.VMEM((8, inner), f32),
        ],
        compiler_params=params(60 << 20),
        name="state_backward",
    )(tab, xbc, dt, s, sin, gm, cw, dtb, na2, na, skip, e2, et, tri, tail, pair)


def token_kernel(tok_ref, cot_ref, gz_ref, gx_ref, wz_ref, wx_ref, gain_ref, out_ref, ggain_ref):
    g = dot(gz_ref[...], wz_ref[...], NT) + dot(gx_ref[...], wx_ref[...], NT)
    u = tok_ref[...].astype(f32)
    r = lax.rsqrt(jnp.mean(u * u, axis=-1, keepdims=True) + EPS)
    unit = u * r

    @pl.when(pl.program_id(0) == 0)
    def _():
        ggain_ref[...] = jnp.zeros_like(ggain_ref)

    ggain_ref[...] += fold_rows(unit * g)
    q = g * gain_ref[...]
    mean = jnp.mean(unit * q, axis=-1, keepdims=True)
    out_ref[...] = (cot_ref[...].astype(f32) + r * (q - unit * mean)).astype(bf16)


def token_grad(tok, cot, gz, gx, wz, wx, gain, tile=256):
    rows, width = tok.shape
    at = lambda i: (i, 0)
    return pl.pallas_call(
        token_kernel,
        grid=(rows // tile,),
        in_specs=[
            pl.BlockSpec((tile, width), at),
            pl.BlockSpec((tile, width), at),
            pl.BlockSpec((tile, gz.shape[1]), at),
            pl.BlockSpec((tile, gx.shape[1]), at),
            fixed(wz.shape), fixed(wx.shape), fixed(gain.shape),
        ],
        out_specs=[pl.BlockSpec((tile, width), at), fixed((8, width))],
        out_shape=[jax.ShapeDtypeStruct((rows, width), bf16), jax.ShapeDtypeStruct((8, width), f32)],
        compiler_params=params(60 << 20),
        name="token_grad",
    )(tok, cot, gz, gx, wz, wx, gain)


def segment_table(segments):
    seqs, length = segments.shape
    seg = segments.astype(f32)
    blocks = length // Q

    def earlier(k):
        return jnp.concatenate([jnp.full((seqs, k), -1.0, f32), seg[:, :-k]], axis=1)

    def later(k):
        return jnp.concatenate([seg[:, k:], jnp.full((seqs, k), -1.0, f32)], axis=1)

    by_block = seg.reshape(seqs, blocks, Q)
    last = by_block[:, :, -1]
    prev = jnp.concatenate([jnp.full((seqs, 1), -1.0, f32), last[:, :-1]], axis=1)
    rows = [seg]
    rows += [(earlier(k) == seg).astype(f32) for k in (1, 2, 3)]
    rows += [(by_block == prev[..., None]).astype(f32).reshape(seqs, length)]
    rows += [(by_block == last[..., None]).astype(f32).reshape(seqs, length)]
    rows += [(later(k) == seg).astype(f32) for k in (1, 2, 3)]
    rows += [jnp.zeros_like(seg)] * (16 - len(rows))
    return jnp.stack(rows, axis=0).reshape(16, seqs * blocks, Q).transpose(1, 0, 2)


def per_device(
    tokens, segments, cotangent, norm_gain, weight_in, conv_weight, conv_bias, dt_bias, a_log, skip_d,
    gate_gain, weight_out,
):
    seqs, length, width = tokens.shape
    rows = seqs * length
    inner = gate_gain.shape[0]
    channels = conv_bias.shape[0]
    heads = dt_bias.shape[0]
    tok = tokens.reshape(rows, width)
    cot = cotangent.reshape(rows, width)
    pad = LANES - heads

    local_x = jnp.pad(weight_in[:, inner:], ((0, 0), (0, pad)))
    wx = lax.all_gather(local_x, "dp", axis=0, tiled=True)
    wz = lax.all_gather(weight_in[:, :inner], "dp", axis=0, tiled=True)
    wo = lax.all_gather(weight_out, "dp", axis=0, tiled=True)

    def row(v):
        return jnp.pad(v, (0, pad)).reshape(1, LANES)

    tab = segment_table(segments)
    neg_rate = -jnp.exp(a_log)
    na, na2 = row(neg_rate), row(neg_rate * LOG2E)
    dtb = row(dt_bias)
    head_of = jnp.arange(inner) // (inner // heads)
    skip = skip_d[head_of].reshape(1, inner)
    et = (head_of[:, None] == jnp.arange(LANES)[None, :]).astype(bf16)
    e2 = jnp.concatenate([et.T, et.T], axis=0)
    pos = jnp.arange(Q)
    tri = (pos[:, None] >= pos[None, :]).astype(bf16)
    below = (pos[:, None] > pos[None, :]).astype(bf16)
    tail = jnp.concatenate([tri.T, tri.T, below, below], axis=1)
    pair = jnp.kron(jnp.eye(2, dtype=f32), tri.astype(f32)).astype(bf16)
    cb = conv_bias.reshape(1, channels)
    ngain = norm_gain.reshape(1, width)
    ggain = gate_gain.reshape(1, inner)

    normed, xbc, dt = project(tok, ngain, wx, channels)
    y, s, sin = state_forward(tab, xbc, dt, conv_weight, cb, dtb, na2, skip, e2, tri, seqs)
    gn, out, gz, gm, p_ggain = gate(tok, normed, y, cot, wz, wo, ggain)
    d_out = dot(gn, cot, TN).astype(bf16)
    d_z = dot(normed, gz, TN).astype(bf16)
    d_out = lax.psum_scatter(d_out, "dp", scatter_dimension=0, tiled=True)
    d_z = lax.psum_scatter(d_z, "dp", scatter_dimension=0, tiled=True)
    gx, p_cw, p_cb, p_skip, p_alog, p_dtb = state_backward(
        tab, xbc, dt, s, sin, gm, conv_weight, dtb, na2, na, skip, e2, et, tri, tail, pair, seqs
    )
    d_x = dot(normed, gx, TN).astype(bf16)
    d_x = lax.psum_scatter(d_x, "dp", scatter_dimension=0, tiled=True)
    g_tok, p_ngain = token_grad(tok, cot, gz, gx, wz, wx, ngain)

    d_in = jnp.concatenate([d_z, d_x], axis=1)
    d_in = lax.psum(d_in, "seq").astype(f32)[:, : weight_in.shape[1]]
    d_out = lax.psum(d_out, "seq").astype(f32)
    small = (
        jnp.sum(p_ngain, axis=0),
        jnp.sum(p_cw.reshape(4, 8, channels), axis=1),
        jnp.sum(p_cb, axis=0),
        jnp.sum(p_dtb, axis=0)[:heads],
        jnp.sum(p_alog, axis=0)[:heads],
        jnp.sum(p_skip.reshape(8, heads, inner // heads), axis=(0, 2)),
        jnp.sum(p_ggain, axis=0),
    )
    s_ngain, s_cw, s_cb, s_dtb, s_alog, s_skip, s_ggain = lax.psum(small, ("dp", "seq"))
    return (
        out.reshape(tokens.shape), g_tok.reshape(tokens.shape), s_ngain, d_in, s_cw, s_cb, s_dtb, s_alog,
        s_skip, s_ggain, d_out,
    )


def solution(mesh):
    data = P(("dp", "seq"), None, None)
    owned = P("dp", None)
    placed = (data, P(("dp", "seq"), None), data, P(), owned, P(), P(), P(), P(), P(), P(), owned)
    return jax.shard_map(
        per_device,
        mesh=mesh,
        in_specs=placed,
        out_specs=(data, data, P(), owned, P(), P(), P(), P(), P(), P(), owned),
        check_vma=False,
    )
```

time: 1100 us -> 503 us (0.46); the launches traced: 1090 us -> 502 us
  matrix products: 418 us -> 30.4 us
  other arithmetic: 249 us -> 28.1 us
  Pallas kernels: 0 us -> 204 us
  local copies, waits for them, and re-layouts: 195 us -> 15.9 us
    dot_general x36 -> x3, matrix products: 418 us -> 30.4 us  [dot(): return lax.dot_general(a, b, dims, preferred_element_type=f32)]
    pallas_call x0 -> x5, Pallas kernels: none -> 204 us  [the longest x1 93.3 us: state_backward(): pl.pallas_call(bwd_kernel, grid=(seqs, blocks), in_specs=[pl.BlockSpec((N...]
    reshape x27 -> x6, local copies, waits for them, and re-layouts: 108 us -> 6.14 us  [the longest x2 1.69 us: row(): return jnp.pad(v, (0, pad)).reshape(1, LANES)]
    reduce_sum x15 -> x8, other arithmetic: 98.9 us -> 1.03 us  [the longest x1 0.75 us: per_device(): jnp.sum(p_ngain, axis=0)]
    mul x18 -> x0, other arithmetic: 66.5 us -> none  [the longest x1 28 us: causal_conv(): return jax.nn.silu(summed)]
    reduce_scatter x2 -> x3, waiting for transfers between devices: 77.1 us -> 118 us  [the longest x1 64.7 us: per_device(): d_out = lax.psum_scatter(d_out, 'dp', scatter_dimension=0, tiled=True)]
    all_gather x2 -> x3, waiting for transfers between devices: 85.2 us -> 48.2 us  [the longest x1 33.5 us: per_device(): wo = lax.all_gather(weight_out, 'dp', axis=0, tiled=True)]
    concatenate x4 -> x3, other arithmetic: 31 us -> 3.37 us  [the longest x1 1.75 us: per_device(): d_in = jnp.concatenate([d_z, d_x], axis=1)]
  transfers between devices with their start and end apart: 5 -> 7, of which waited for: 3 -> 4; matrix products, arithmetic and copies ran while one was open for 40% -> 12% of each run, Pallas kernels for 0% -> 33%
where the time goes in v1:
time: 503 us; the launch traced here: 502 us
  Pallas kernels  204 us (41%)
  waiting for transfers between devices  167 us (33%)
  blocking collectives  41.8 us (8%)
  matrix products  30.4 us (6%)
  other arithmetic  28.1 us (6%)
  local copies, waits for them, and re-layouts  15.9 us (3%)
  between operations  14.4 us (3%)
    pallas_call x1, Pallas kernels, state_backward(): pl.pallas_call(bwd_kernel, grid=(seqs, blocks), in_specs=[pl.BlockSpec((N...  93.3 us
    reduce_scatter x1, waiting for transfers between devices, per_device(): d_out = lax.psum_scatter(d_out, 'dp', scatter_dimension=0, tiled=True)  64.7 us
    reduce_scatter x1, waiting for transfers between devices, per_device(): d_x = lax.psum_scatter(d_x, 'dp', scatter_dimension=0, tiled=True)  53.3 us
    psum x1, blocking collectives, per_device(): lax.psum(small, ('dp', 'seq'))  41.8 us
    pallas_call x1, Pallas kernels, state_forward(): pl.pallas_call(fwd_kernel, grid=(seqs, blocks), in_specs=[pl.BlockSpec((N...  40.8 us
    pallas_call x1, Pallas kernels, gate(): pl.pallas_call(gate_kernel, grid=(rows // tile,), in_specs=[pl.BlockSpec(...  37.2 us
    all_gather x1, waiting for transfers between devices, per_device(): wo = lax.all_gather(weight_out, 'dp', axis=0, tiled=True)  33.5 us
    dot_general x3, matrix products, dot(): return lax.dot_general(a, b, dims, preferred_element_type=f32)  30.4 us
  transfers between devices with their start and end apart: 7, of which 4 were waited for; matrix products, arithmetic and copies ran while one was open for 12% of the time, Pallas kernels for 33%

profile of v1, /device:TPU:0, one launch (start us, length us, event | category | flops | bytes accessed | tf_op | source)
XLA Modules:
  0.0 502.2 jit_solution(9734657612734336926)
XLA Ops:
  7.2 0.9 slice.42
  8.2 0.7 pad.21
  8.9 1.6 slice.51
  10.6 0.7 all-gather.8.cloned.1.call-update
  11.3 0.7 convert_bitcast_fusion
  12.3 0.8 compare_convert_fusion.2
  13.3 0.1 copy.26
  13.4 0.1 eq.93
  14.4 1.5 fusion.11
  15.9 2.1 fusion.10
  18.0 4.3 fusion.6
  22.4 10.8 %select_select_fusion = f32[1536]{0:T(1024)S(1)} fusion(pred[1536]{0:T(1024)(128)(4,1)S(1)} %compare_reduce_fusion, pred[1536]{0:T(1024)(128)(4,1)S(1)} %compare_reduce_fusion.1, pred[1536]{0:T(1024)(128)(4,1)S(1)} %compare_reduce_fusion.2, pred[1536]{0:T(1024)(128)(4,1)S(1)} %compare_reduce_fusion.3, pred[1536]{0:T(1024)(128)(4,1)S(1)} %compare_reduce_fusion.4, ...), kind=kLoop, calls=%fused_computation.61 | loop fusion | flops 26112 | bytes 38468 | tf_op jit(solution)/shard_map/gather | solution.py:567
  33.2 0.6 reshape.238.skip_ref
  33.8 1.3 reshape.233.gain_ref
  35.1 1.3 reshape.235.cb_ref
  36.3 1.3 reshape.240.gain_ref
  37.6 0.1 compare_convert_fusion
  37.8 1.4 stack.57
  39.2 1.2 pad_bitcast_fusion.2.dtb_ref
  40.4 0.7 exponential_negate_fusion
  41.0 0.5 pad_bitcast_fusion
  41.5 0.6 fusion.1.tri_ref
  42.2 0.1 iota_compare_fusion.1
  42.3 1.0 add_convert_fusion.e_ref
  43.2 14.7 %all-gather.4.cloned.1.call-done.wx_ref = bf16[768,1920]{1,0:T(8,128)(2,1)} async-done(((bf16[48,1920]{1,0:T(8,128)(2,1)}), bf16[768,1920]{1,0:T(8,128)(2,1)}) %all-gather.4.cloned.1.call-update) | async-done | bytes 2949136 | tf_op jit(solution)/shard_map/all_gather | solution.py:555
  57.9 12.8 %project.1 = (bf16[2048,768]{1,0:T(8,128)(2,1)}, f32[2048,1792]{1,0:T(8,128)}, f32[2048,128]{1,0:T(8,128)}) custom-call(bf16[2048,768]{1,0:T(8,128)(2,1)} %bitcast.59, f32[1,768]{1,0:T(1,128)} %reshape.233.gain_ref, bf16[768,1920]{1,0:T(8,128)(2,1)} %all-gather.4.cloned.1.call-done.wx_ref), custom_call_target="tpu_custom_call" | custom-call | tf_op jit(solution)/shard_map/project/pallas_call | solution.py:80
  70.7 40.8 %state_forward.1 = (f32[2048,1536]{1,0:T(8,128)}, f32[2048,1792]{1,0:T(8,128)}, bf16[16,128,1536]{2,1,0:T(8,128)(2,1)}) custom-call(f32[16,16,128]{2,1,0:T(8,128)} %bitcast.65, f32[2048,1792]{1,0:T(8,128)} %get-tuple-element.31.xbc_ref, f32[2048,128]{1,0:T(8,128)} %get-tuple-element.32.dt_ref, f32[4,1792]{1,0:T(4,128)} %cw_ref.3, ...), custom_call_target="tpu_custom_call" | custom-call | tf_op jit(solution)/shard_map/state_forward/pallas_call | solution.py:206
  111.5 33.5 %all-gather.8.cloned.1.call-done.wo_ref = bf16[1536,768]{1,0:T(8,128)(2,1)} async-done(((bf16[96,768]{1,0:T(8,128)(2,1)}), bf16[1536,768]{1,0:T(8,128)(2,1)}) %all-gather.8.cloned.1.call-update) | async-done | bytes 2359312 | tf_op jit(solution)/shard_map/all_gather | solution.py:557
  145.0 37.2 %gate.1 = (bf16[2048,1536]{1,0:T(8,128)(2,1)}, bf16[2048,768]{1,0:T(8,128)(2,1)}, bf16[2048,1536]{1,0:T(8,128)(2,1)}, f32[2048,1536]{1,0:T(8,128)}, f32[8,1536]{1,0:T(8,128)}) custom-call(bf16[2048,768]{1,0:T(8,128)(2,1)} %bitcast.60, bf16[2048,768]{1,0:T(8,128)(2,1)} %get-tuple-element.30.normed_ref, f32[2048,1536]{1,0:T(8,128)} %get-tuple-element.33.y_ref, ...), custom_call_target="tpu_custom_call" | custom-call | tf_op jit(solution)/shard_map/gate/pallas_call | solution.py:264
  182.3 9.2 %convolution_convert_fusion.2 = bf16[768,1536]{1,0:T(8,128)(2,1)} fusion(bf16[2048,768]{1,0:T(8,128)(2,1)S(1)} %copy-done.1, bf16[2048,1536]{1,0:T(8,128)(2,1)} %get-tuple-element.35.gz_ref), kind=kOutput, calls=%fused_computation.2 | convolution fusion | flops 4833017856 | bytes 11796480 | tf_op jit(solution)/shard_map/dot_general | solution.py:24
  191.5 0.2 reduce-scatter.6.cloned.1.call-start
  191.8 0.2 multiply_convert_fusion
  191.9 0.7 copy.31
  192.6 0.7 add_convert_fusion.1.tail_ref
  193.3 1.0 fusion.et_ref
  194.3 93.3 %state_backward.1 = (bf16[2048,1920]{1,0:T(8,128)(2,1)}, f32[32,1792]{1,0:T(8,128)}, f32[8,1792]{1,0:T(8,128)}, f32[8,1536]{1,0:T(8,128)}, f32[8,128]{1,0:T(8,128)}, /*index=5*/f32[8,128]{1,0:T(8,128)}) custom-call(f32[16,16,128]{2,1,0:T(8,128)} %bitcast.66, f32[2048,1792]{1,0:T(8,128)} %get-tuple-element.31.xbc_ref, f32[2048,128]{1,0:T(8,128)} %get-tuple-element.32.dt_ref, ...), custom_call_target="tpu_custom_call" | custom-call | tf_op jit(solution)/shard_map/state_backward/pallas_call | solution.py:443
  287.6 11.9 %convolution_convert_fusion = bf16[768,1920]{1,0:T(8,128)(2,1)} fusion(bf16[2048,768]{1,0:T(8,128)(2,1)} %get-tuple-element.30.normed_ref, bf16[2048,1920]{1,0:T(8,128)(2,1)} %get-tuple-element.39.gx_ref), kind=kOutput, calls=%fused_computation | convolution fusion | flops 6041272320 | bytes 13959168 | tf_op jit(solution)/shard_map/dot_general | solution.py:24
  299.6 9.2 %convolution_convert_fusion.1 = bf16[1536,768]{1,0:T(8,128)(2,1)} fusion(bf16[2048,1536]{1,0:T(8,128)(2,1)} %get-tuple-element.48, bf16[2048,768]{1,0:T(8,128)(2,1)S(1)} %bitcast.64), kind=kOutput, calls=%fused_computation.1 | convolution fusion | flops 4833017856 | bytes 11796480 | tf_op jit(solution)/shard_map/dot_general | solution.py:24
  308.8 0.3 all-reduce.15.cloned.1.call-start
  309.1 53.3 %reduce-scatter.6.cloned.1.call-done = bf16[48,1920]{1,0:T(8,128)(2,1)} async-done(((bf16[768,1920]{1,0:T(8,128)(2,1)}), bf16[48,1920]{1,0:T(8,128)(2,1)}) %reduce-scatter.6.cloned.1.call-update) | async-done | bytes 184336 | tf_op jit(solution)/shard_map/reduce_scatter | solution.py:590
  362.4 1.7 pad_maximum_fusion
  364.1 64.7 %reduce-scatter.8.cloned.1.call-done = bf16[96,768]{1,0:T(8,128)(2,1)} async-done(((bf16[1536,768]{1,0:T(8,128)(2,1)}), bf16[96,768]{1,0:T(8,128)(2,1)}) %reduce-scatter.8.cloned.1.call-update) | async-done | bytes 147472 | tf_op jit(solution)/shard_map/reduce_scatter | solution.py:584
  428.9 20.0 %token_grad.1 = (bf16[2048,768]{1,0:T(8,128)(2,1)}, f32[8,768]{1,0:T(8,128)}) custom-call(bf16[2048,768]{1,0:T(8,128)(2,1)} %bitcast.61, bf16[2048,768]{1,0:T(8,128)(2,1)} %bitcast.63, bf16[2048,1536]{1,0:T(8,128)(2,1)} %get-tuple-element.35.gz_ref, bf16[2048,1920]{1,0:T(8,128)(2,1)} %get-tuple-element.39.gx_ref, ...), custom_call_target="tpu_custom_call" | custom-call | tf_op jit(solution)/shard_map/token_grad/pallas_call | solution.py:501
  448.9 0.7 reduce_sum.70
  449.7 0.1 reduce_sum.77
  450.1 41.8 %all-reduce.11 = (f32[768]{0:T(1024)}, f32[4,1792]{1,0:T(4,128)}, f32[1792]{0:T(1024)}, f32[24]{0:T(128)}, f32[24]{0:T(128)}, /*index=5*/f32[24]{0:T(128)}, f32[1536]{0:T(1024)}) all-reduce(f32[768]{0:T(1024)S(1)} %reduce_sum.70, f32[4,1792]{1,0:T(4,128)S(1)} %bitcast_reduce_fusion, ...), channel_id=1, replica_groups=mesh['dp'=16,'seq'=2] {'dp','seq'}, use_global_device_ids=true, to_apply=%region_1.2 | all-reduce | flops 11336 | bytes 90688 | tf_op jit(solution)/shard_map/psum | solution.py:605
  491.8 1.9 slice_convert_fusion
  493.7 1.6 convert_element_type.92
  (75 shorter events, 2.1 us)
Async XLA Ops:
  7.2 50.8 %all-gather.4.cloned.1.call-start = ((), (), s32[]{:S(2)}) async-start(), calls=%async_computation.3 | async-start | bytes 3133440 | tf_op jit(solution)/shard_map/all_gather | solution.py:555
  8.9 102.6 %all-gather.6.cloned.1.call-start = ((), (), s32[]{:S(2)}) async-start(), calls=%async_computation.4 | async-start | bytes 2506752 | tf_op jit(solution)/shard_map/all_gather | solution.py:556
  10.5 134.5 %all-gather.8.cloned.1.call-start = ((), (), s32[]{:S(2)}) async-start(), calls=%async_computation.5 | async-start | bytes 2506752 | tf_op jit(solution)/shard_map/all_gather | solution.py:557
  11.3 297.9 %reduce-scatter.4.cloned.1.call-start = ((), (), s32[]{:S(2)}) async-start(), calls=%async_computation.6 | async-start | bytes 2506752 | tf_op jit(solution)/shard_map/reduce_scatter | solution.py:585
  145.0 37.2 %copy-start.1 = (bf16[2048,768]{1,0:T(8,128)(2,1)S(1)}, bf16[2048,768]{1,0:T(8,128)(2,1)}, u32[]{:S(2)}) copy-start(bf16[2048,768]{1,0:T(8,128)(2,1)} %get-tuple-element.30.normed_ref) | copy-start | bytes 9437188
  191.5 170.9 %reduce-scatter.6.cloned.1.call-start = ((), (), s32[]{:S(2)}) async-start(), calls=%async_computation.7 | async-start | bytes 3133440 | tf_op jit(solution)/shard_map/reduce_scatter | solution.py:590
  287.6 12.0 %copy-start = (bf16[2,1024,768]{2,1,0:T(8,128)(2,1)S(1)}, bf16[2,1024,768]{2,1,0:T(8,128)(2,1)}, u32[]{:S(2)}) copy-start(bf16[2,1024,768]{2,1,0:T(8,128)(2,1)} %param.14) | copy-start | bytes 9437188
  299.5 129.3 %reduce-scatter.8.cloned.1.call-start = ((), (), s32[]{:S(2)}) async-start(), calls=%async_computation.8 | async-start | bytes 2506752 | tf_op jit(solution)/shard_map/reduce_scatter | solution.py:584
  308.8 183.0 %all-reduce.15.cloned.1.call-start = ((), (), s32[]{:S(2)}) async-start(), calls=%async_computation.9 | async-start | bytes 958464 | tf_op jit(solution)/shard_map/psum | solution.py:594
  428.9 20.8 %copy-start.5 = (f32[8,1536]{1,0:T(8,128)S(1)}, f32[8,1536]{1,0:T(8,128)}, u32[]{:S(2)}) copy-start(f32[8,1536]{1,0:T(8,128)} %get-tuple-element.46) | copy-start | bytes 147460
  428.9 21.0 %copy-start.3 = (f32[8,1792]{1,0:T(8,128)S(1)}, f32[8,1792]{1,0:T(8,128)}, u32[]{:S(2)}) copy-start(f32[8,1792]{1,0:T(8,128)} %get-tuple-element.43) | copy-start | bytes 172036
  428.9 21.0 %copy-start.7 = (f32[8,128]{1,0:T(8,128)S(1)}, f32[8,128]{1,0:T(8,128)}, u32[]{:S(2)}) copy-start(f32[8,128]{1,0:T(8,128)} %get-tuple-element.44) | copy-start | bytes 12292
  428.9 21.0 %copy-start.6 = (f32[8,128]{1,0:T(8,128)S(1)}, f32[8,128]{1,0:T(8,128)}, u32[]{:S(2)}) copy-start(f32[8,128]{1,0:T(8,128)} %get-tuple-element.45) | copy-start | bytes 12292
  428.9 21.0 %copy-start.4 = (f32[8,1536]{1,0:T(8,128)S(1)}, f32[8,1536]{1,0:T(8,128)}, u32[]{:S(2)}) copy-start(f32[8,1536]{1,0:T(8,128)} %get-tuple-element.47) | copy-start | bytes 147460
  428.9 21.1 %copy-start.2 = (f32[32,1792]{1,0:T(8,128)S(1)}, f32[32,1792]{1,0:T(8,128)}, u32[]{:S(2)}) copy-start(f32[32,1792]{1,0:T(8,128)} %get-tuple-element.42) | copy-start | bytes 688132
Sparse Core Ops, SparseCore 0:
  10.7 47.1 all-gather.3
  60.8 40.8 all-gather.5
  104.0 41.0 all-gather.7
  191.6 61.9 reduce-scatter.3
  299.6 62.7 reduce-scatter.5
  366.6 62.1 reduce-scatter.7
  431.7 27.1 all-reduce.14

commit v2 on v1

--- a/solution.py
+++ b/solution.py
@@ -1,3 +1,4 @@
+import functools
 import math
 
 import jax
@@ -9,6 +10,7 @@
 
 f32 = jnp.float32
 bf16 = jnp.bfloat16
+HEAD = 64
 Q = 128
 LANES = 128
 EPS = 1e-05
@@ -100,10 +102,39 @@
     )(tok, gain, wx)
 
 
-def table_columns(tab_ref):
-    tab = tab_ref[...]
-    reps = LANES // tab.shape[0]
-    return tab, jnp.concatenate([tab] * reps, axis=0).T
+def segment_rows(seg_ref, block, blocks, at):
+    rows = seg_ref.shape[0]
+    none = jnp.full((1, LANES), -1.0, f32)
+    seg = seg_ref[pl.ds(at, 1), :]
+    prev = jnp.where(block > 0, seg_ref[pl.ds(jnp.maximum(at - 1, 0), 1), :], none)
+    after = jnp.where(block < blocks - 1, seg_ref[pl.ds(jnp.minimum(at + 1, rows - 1), 1), :], none)
+    lane = lax.broadcasted_iota(jnp.int32, (1, LANES), 1)
+
+    def same(other):
+        return (other == seg).astype(f32)
+
+    out = [seg]
+    for k in (1, 2, 3):
+        out.append(same(jnp.where(lane < k, pltpu.roll(prev, k, 1), pltpu.roll(seg, k, 1))))
+    out.append(same(jnp.broadcast_to(prev[:, LANES - 1 :], (1, LANES))))
+    out.append(same(jnp.broadcast_to(seg[:, LANES - 1 :], (1, LANES))))
+    for k in (1, 2, 3):
+        turn = LANES - k
+        out.append(same(jnp.where(lane >= turn, pltpu.roll(after, turn, 1), pltpu.roll(seg, turn, 1))))
+    tab = jnp.concatenate(out + [none] * (16 - len(out)), axis=0)
+    return seg, jnp.concatenate([tab] * (LANES // 16), axis=0).T
+
+
+def iota(shape, axis):
+    return lax.broadcasted_iota(jnp.int32, shape, axis)
+
+
+def ones_where(cond):
+    return jnp.where(cond, 1.0, 0.0).astype(bf16)
+
+
+def head_columns(heads_wide, inner, width):
+    return ones_where(iota((heads_wide, inner), 0) % LANES == iota((heads_wide, inner), 1) // width)
 
 
 def step_terms(dt, dtb, na2, tri, cols):
@@ -115,6 +146,20 @@
     return raw, ts, cum, start, end
 
 
+def head_terms(head_ref):
+    rate = head_ref[1:2, :]
+    return head_ref[0:1, :], rate, rate * LOG2E
+
+
+def fill_constants(e_ref, tri_ref, skip_ref, head_ref):
+    inner = e_ref.shape[1]
+    e_ref[...] = head_columns(e_ref.shape[0], inner, HEAD)
+    tri_ref[...] = ones_where(iota((Q, Q), 0) >= iota((Q, Q), 1))
+    skip = jnp.broadcast_to(head_ref[2:3, :], (8, LANES))
+    wide_skip = dot(jnp.concatenate(split(skip, 3), axis=1), head_columns(3 * LANES, inner, HEAD))
+    skip_ref[...] = wide_skip[0:1]
+
+
 def expand_operand(*terms):
     return jnp.concatenate([jnp.concatenate(split(t, 2), axis=1) for t in terms], axis=0)
 
@@ -125,12 +170,17 @@
 
 
 def fwd_kernel(
-    tab_ref, xbc_ref, dt_ref, cw_ref, cb_ref, dtb_ref, na2_ref, skip_ref, e_ref, tri_ref,
-    y_ref, s_ref, sin_ref, state, ext,
+    seg_ref, xbc_ref, dt_ref, cw_ref, cb_ref, head_ref,
+    y_ref, s_ref, sin_ref, state, ext, e_ref, tri_ref, skip_ref,
 ):
-    inner = skip_ref.shape[1]
+    inner = y_ref.shape[1]
     channels = cb_ref.shape[1]
-    b = pl.program_id(1)
+    b, blocks = pl.program_id(1), pl.num_programs(1)
+    dtb, _, na2 = head_terms(head_ref)
+
+    @pl.when((b == 0) & (pl.program_id(0) == 0))
+    def _():
+        fill_constants(e_ref, tri_ref, skip_ref, head_ref)
 
     @pl.when(b == 0)
     def _():
@@ -142,7 +192,7 @@
         ext[0:8, :] = ext[Q : Q + 8, :]
 
     ext[8 : 8 + Q, :] = xbc_ref[...]
-    tab, cols = table_columns(tab_ref)
+    seg, cols = segment_rows(seg_ref, b, blocks, pl.program_id(0) * blocks + b)
     m1, m2, m3 = (wide(cols[:, k : k + 1], 256) for k in (1, 2, 3))
 
     def conv(c):
@@ -158,15 +208,15 @@
     bm, cm = bc[:, :LANES], bc[:, LANES:]
     bt = bm.T
     c_two = jnp.concatenate([cm, bc_rest[:, LANES:]], axis=1)
-    _, ts, cum, start, end = step_terms(dt_ref[...], dtb_ref[...], na2_ref[...], tri_ref[...], cols)
+    _, ts, cum, start, end = step_terms(dt_ref[...], dtb, na2, tri_ref[...], cols)
     cum_t = cum.T
     grow = expand_operand(start, end, ts)
     row_i = lax.broadcasted_iota(jnp.int32, (Q, Q), 0)
     col_j = lax.broadcasted_iota(jnp.int32, (Q, Q), 1)
-    same = wide(cols[:, 0:1], LANES) == tab[0:1, :]
+    same = wide(cols[:, 0:1], LANES) == seg
     mask = jnp.where(same & (row_i >= col_j), 0.0, NEG)
     scores = dot_split((cm, bc_rest[:, LANES:]), (bm, bc_rest[:, :LANES]))
-    left = col_j < LANES // 2
+    left = col_j < HEAD
 
     for c in range(0, inner, 256):
         at = pl.ds(c, 256)
@@ -183,7 +233,7 @@
         for p in range(2):
             mats = []
             for h in range(2):
-                head = (c + p * LANES) // 64 + h
+                head = (c + p * LANES) // HEAD + h
                 gap = wide(cum[:, head : head + 1], LANES) - cum_t[head : head + 1, :] + mask
                 mats.append((jnp.exp2(gap) * scores).astype(bf16))
             xp = xs_low[:, p * LANES : (p + 1) * LANES]
@@ -197,9 +247,8 @@
     return pl.BlockSpec(shape, lambda *_: (0,) * len(shape))
 
 
-def state_forward(tab, xbc, dt, cw, cb, dtb, na2, skip, e2, tri, seqs):
+def state_forward(seg, xbc, dt, cw, cb, head, inner, seqs):
     rows, channels = xbc.shape
-    inner = skip.shape[1]
     blocks = rows // seqs // Q
     at = lambda s, b: (s * blocks + b, 0)
     at3 = lambda s, b: (s * blocks + b, 0, 0)
@@ -207,11 +256,10 @@
         fwd_kernel,
         grid=(seqs, blocks),
         in_specs=[
-            pl.BlockSpec((None, 16, LANES), at3),
+            fixed(seg.shape),
             pl.BlockSpec((Q, channels), at),
             pl.BlockSpec((Q, LANES), at),
-            fixed(cw.shape), fixed(cb.shape), fixed(dtb.shape), fixed(na2.shape), fixed(skip.shape),
-            fixed(e2.shape), fixed(tri.shape),
+            fixed(cw.shape), fixed(cb.shape), fixed(head.shape),
         ],
         out_specs=[
             pl.BlockSpec((Q, inner), at),
@@ -223,17 +271,42 @@
             jax.ShapeDtypeStruct((rows, channels), f32),
             jax.ShapeDtypeStruct((seqs * blocks, LANES, inner), bf16),
         ],
-        scratch_shapes=[pltpu.VMEM((LANES, inner), f32), pltpu.VMEM((Q + 8, channels), f32)],
+        scratch_shapes=[
+            pltpu.VMEM((LANES, inner), f32),
+            pltpu.VMEM((Q + 8, channels), f32),
+            pltpu.VMEM((2 * LANES, inner), bf16),
+            pltpu.VMEM((Q, Q), bf16),
+            pltpu.VMEM((1, inner), f32),
+        ],
         compiler_params=params(60 << 20),
         name="state_forward",
-    )(tab, xbc, dt, cw, cb, dtb, na2, skip, e2, tri)
+    )(seg, xbc, dt, cw, cb, head)
+
+
+def flat(ref):
+    v = ref[...]
+    return v.reshape(v.shape[0] * v.shape[1], v.shape[2])
+
+
+def slab_views(slab, own):
+    owners, _, width = slab.shape
+    if own % 16 == 0:
+        first = lambda *_: (0, 0, 0)
+        second = lambda *_: (0, 1, 0)
+        sizes = ((own, first), (own, second), (2 * own, second))
+        return [(slab, pl.BlockSpec((owners, n, width), index)) for n, index in sizes]
+    parts = [
+        v.reshape(1, -1, width) for v in (slab[:, :own], slab[:, own : 2 * own], slab[:, 2 * own :])
+    ]
+    return [(v, fixed(v.shape)) for v in parts]
 
 
 def gate_kernel(
-    tok_ref, normed_ref, y_ref, cot_ref, wz_ref, wo_ref, gain_ref,
+    tok_ref, normed_ref, y_ref, cot_ref, wa_ref, wb_ref, wo_ref, gain_ref,
     gn_ref, out_ref, gz_ref, gm_ref, ggain_ref,
 ):
-    z = dot(normed_ref[...], wz_ref[...])
+    normed, wo = normed_ref[...], flat(wo_ref)
+    z = jnp.concatenate([dot(normed, flat(wa_ref)), dot(normed, flat(wb_ref))], axis=1)
     sg = sigmoid(z)
     sz = z * sg
     y = y_ref[...]
@@ -242,8 +315,8 @@
     unit = gated * rstd
     gn = (unit * gain_ref[...]).astype(bf16)
     gn_ref[...] = gn
-    out_ref[...] = (tok_ref[...].astype(f32) + dot(gn, wo_ref[...])).astype(bf16)
-    g_gn = dot(cot_ref[...], wo_ref[...], NT)
+    out_ref[...] = (tok_ref[...].astype(f32) + dot(gn, wo)).astype(bf16)
+    g_gn = dot(cot_ref[...], wo, NT)
 
     @pl.when(pl.program_id(0) == 0)
     def _():
@@ -257,7 +330,7 @@
     gz_ref[...] = (g_gated * y * (sg * (1.0 + z * (1.0 - sg)))).astype(bf16)
 
 
-def gate(tok, normed, y, cot, wz, wo, gain, tile=256):
+def gate(tok, normed, y, cot, weights, gain, tile=256):
     rows, width = tok.shape
     inner = y.shape[1]
     at = lambda i: (i, 0)
@@ -269,7 +342,7 @@
             pl.BlockSpec((tile, width), at),
             pl.BlockSpec((tile, inner), at),
             pl.BlockSpec((tile, width), at),
-            fixed(wz.shape), fixed(wo.shape), fixed(gain.shape),
+            *[spec for _, spec in weights], fixed(gain.shape),
         ],
         out_specs=[
             pl.BlockSpec((tile, inner), at),
@@ -287,24 +360,30 @@
         ],
         compiler_params=params(60 << 20),
         name="gate",
-    )(tok, normed, y, cot, wz, wo, gain)
+    )(tok, normed, y, cot, *[v for v, _ in weights], gain)
 
 
 def bwd_kernel(
-    tab_ref, xbc_ref, dt_ref, s_ref, sin_ref, gm_ref, cw_ref, dtb_ref, na2_ref, na_ref, skip_ref,
-    e_ref, et_ref, tri_ref, tail_ref, pair_ref,
+    seg_ref, xbc_ref, dt_ref, s_ref, sin_ref, gm_ref, cw_ref, head_ref,
     gx_ref, gcw_ref, gcb_ref, gskip_ref, galog_ref, gdtb_ref,
-    adj, gext, da_rows, edge, spread, grad_b, grad_c, link,
+    adj, gext, da_rows, spread, grad_b, grad_c, link, e_ref, tri_ref, skip_ref, et_ref, tail_ref, pair_ref,
 ):
-    inner = skip_ref.shape[1]
+    inner = gm_ref.shape[1]
     channels = s_ref.shape[1]
-    heads = inner // 64
-    b = pl.program_id(1)
+    b, blocks = pl.program_id(1), pl.num_programs(1)
+    dtb, rate, na2 = head_terms(head_ref)
 
     @pl.when((b == 0) & (pl.program_id(0) == 0))
     def _():
         for ref in (gcw_ref, gcb_ref, gskip_ref, galog_ref, gdtb_ref, da_rows):
             ref[...] = jnp.zeros_like(ref)
+        fill_constants(e_ref, tri_ref, skip_ref, head_ref)
+        et_ref[...] = ones_where(iota((inner, LANES), 0) // HEAD == iota((inner, LANES), 1))
+        turned = ones_where(iota((Q, Q), 0) <= iota((Q, Q), 1))
+        below = ones_where(iota((Q, Q), 0) > iota((Q, Q), 1))
+        tail_ref[...] = jnp.concatenate([turned, turned, below, below], axis=1)
+        row, col = iota((2 * Q, 2 * Q), 0), iota((2 * Q, 2 * Q), 1)
+        pair_ref[...] = ones_where((row // Q == col // Q) & (row >= col))
 
     @pl.when(b == 0)
     def _():
@@ -315,10 +394,9 @@
     def _():
         gext[Q : Q + 8, :] = gext[0:8, :]
 
-    tab, cols = table_columns(tab_ref)
-    raw, ts, cum, start, end = step_terms(
-        dt_ref[...], dtb_ref[...], na2_ref[...], tri_ref[...], cols
-    )
+    turn = blocks - 1 - b
+    seg, cols = segment_rows(seg_ref, turn, blocks, pl.program_id(0) * blocks + turn)
+    raw, ts, cum, start, end = step_terms(dt_ref[...], dtb, na2, tri_ref[...], cols)
     cum_t = cum.T
     grow = expand_operand(start, end, ts)
 
@@ -335,11 +413,11 @@
     c_two = jnp.concatenate([cm, bc_rest[:, LANES:]], axis=1)
     row_j = lax.broadcasted_iota(jnp.int32, (Q, Q), 0)
     col_i = lax.broadcasted_iota(jnp.int32, (Q, Q), 1)
-    same = wide(cols[:, 0:1], LANES) == tab[0:1, :]
+    same = wide(cols[:, 0:1], LANES) == seg
     mask = jnp.where(same & (col_i >= row_j), 0.0, NEG)
     before = (row_j < col_i).astype(f32)
     scores = dot_split((bm, bc_rest[:, :LANES]), (cm, bc_rest[:, LANES:]))
-    left = col_i < LANES // 2
+    left = col_i < HEAD
     grad_scores = jnp.zeros((Q, Q), f32)
 
     for c in range(0, inner, 256):
@@ -363,7 +441,7 @@
             gmat = dot_split((xs_low[:, lanes], xs_rest[:, lanes]), (diag, diag_rest))
             mats, links = [], []
             for h in range(2):
-                head = (c + p * LANES) // 64 + h
+                head = (c + p * LANES) // HEAD + h
                 gap = cum_t[head : head + 1, :] - wide(cum[:, head : head + 1], LANES) + mask
                 decay = jnp.exp2(gap)
                 mat = decay * scores
@@ -376,7 +454,7 @@
             parts.append(dot(high, diag) + dot(high, diag_rest) + dot(rest, diag))
             reach = dot(jnp.concatenate(links, axis=1), pair_ref[...])
             for h in range(2):
-                head = (c + p * LANES) // 64 + h
+                head = (c + p * LANES) // HEAD + h
                 da_rows[head : head + 1, :] = jnp.sum(
                     reach[:, h * LANES : (h + 1) * LANES] * before, axis=0, keepdims=True
                 )
@@ -411,8 +489,8 @@
     through = jnp.sum(dot(jnp.concatenate(split(link[...], 2), axis=0), et_ref[...]), axis=0, keepdims=True)
     around = jnp.concatenate(split(phi, 2) + split(psi, 2), axis=0)
     da = da_rows[...].T + dot(tail_ref[...], around) + start[Q - 1 : Q, :] * through
-    g_ts = spread[2 * Q :] + na_ref[...] * da
-    galog_ref[...] += fold_rows(ts * na_ref[...] * da)
+    g_ts = spread[2 * Q :] + rate * da
+    galog_ref[...] += fold_rows(ts * rate * da)
     g_dt = g_ts * sigmoid(raw)
     gdtb_ref[...] += fold_rows(g_dt)
 
@@ -434,9 +512,9 @@
     gx_ref[:, channels:] = g_dt.astype(bf16)
 
 
-def state_backward(tab, xbc, dt, s, sin, gm, cw, dtb, na2, na, skip, e2, et, tri, tail, pair, seqs):
+def state_backward(seg, xbc, dt, s, sin, gm, cw, head, seqs):
     rows, channels = xbc.shape
-    inner = skip.shape[1]
+    inner = gm.shape[1]
     blocks = rows // seqs // Q
     at = lambda s, b: (s * blocks + blocks - 1 - b, 0)
     at3 = lambda s, b: (s * blocks + blocks - 1 - b, 0, 0)
@@ -444,14 +522,14 @@
         bwd_kernel,
         grid=(seqs, blocks),
         in_specs=[
-            pl.BlockSpec((None, 16, LANES), at3),
+            fixed(seg.shape),
             pl.BlockSpec((Q, channels), at),
             pl.BlockSpec((Q, LANES), at),
             pl.BlockSpec((Q, channels), at),
             pl.BlockSpec((None, LANES, inner), at3),
             pl.BlockSpec((Q, inner), at),
         ]
-        + [fixed(v.shape) for v in (cw, dtb, na2, na, skip, e2, et, tri, tail, pair)],
+        + [fixed(v.shape) for v in (cw, head)],
         out_specs=[
             pl.BlockSpec((Q, channels + LANES), at),
             fixed((32, channels)), fixed((8, channels)), fixed((8, inner)), fixed((8, LANES)), fixed((8, LANES)),
@@ -468,19 +546,26 @@
             pltpu.VMEM((LANES, inner), f32),
             pltpu.VMEM((Q + 8, channels), f32),
             pltpu.VMEM((LANES, LANES), f32),
-            pltpu.VMEM((8, LANES), f32),
             pltpu.VMEM((3 * Q, LANES), f32),
             pltpu.VMEM((Q, LANES), f32),
             pltpu.VMEM((Q, LANES), f32),
             pltpu.VMEM((8, inner), f32),
+            pltpu.VMEM((2 * LANES, inner), bf16),
+            pltpu.VMEM((Q, Q), bf16),
+            pltpu.VMEM((1, inner), f32),
+            pltpu.VMEM((inner, LANES), bf16),
+            pltpu.VMEM((Q, 4 * Q), bf16),
+            pltpu.VMEM((2 * Q, 2 * Q), bf16),
         ],
         compiler_params=params(60 << 20),
         name="state_backward",
-    )(tab, xbc, dt, s, sin, gm, cw, dtb, na2, na, skip, e2, et, tri, tail, pair)
-
-
-def token_kernel(tok_ref, cot_ref, gz_ref, gx_ref, wz_ref, wx_ref, gain_ref, out_ref, ggain_ref):
-    g = dot(gz_ref[...], wz_ref[...], NT) + dot(gx_ref[...], wx_ref[...], NT)
+    )(seg, xbc, dt, s, sin, gm, cw, head)
+
+
+def token_kernel(tok_ref, cot_ref, gz_ref, gx_ref, wa_ref, wb_ref, wx_ref, gain_ref, out_ref, ggain_ref):
+    half = gz_ref.shape[1] // 2
+    g = dot(gz_ref[:, :half], flat(wa_ref), NT) + dot(gz_ref[:, half:], flat(wb_ref), NT)
+    g += dot(gx_ref[...], wx_ref[...], NT)
     u = tok_ref[...].astype(f32)
     r = lax.rsqrt(jnp.mean(u * u, axis=-1, keepdims=True) + EPS)
     unit = u * r
@@ -495,7 +580,7 @@
     out_ref[...] = (cot_ref[...].astype(f32) + r * (q - unit * mean)).astype(bf16)
 
 
-def token_grad(tok, cot, gz, gx, wz, wx, gain, tile=256):
+def token_grad(tok, cot, gz, gx, weights, wx, gain, tile=256):
     rows, width = tok.shape
     at = lambda i: (i, 0)
     return pl.pallas_call(
@@ -506,40 +591,106 @@
             pl.BlockSpec((tile, width), at),
             pl.BlockSpec((tile, gz.shape[1]), at),
             pl.BlockSpec((tile, gx.shape[1]), at),
-            fixed(wz.shape), fixed(wx.shape), fixed(gain.shape),
+            *[spec for _, spec in weights], fixed(wx.shape), fixed(gain.shape),
         ],
         out_specs=[pl.BlockSpec((tile, width), at), fixed((8, width))],
         out_shape=[jax.ShapeDtypeStruct((rows, width), bf16), jax.ShapeDtypeStruct((8, width), f32)],
         compiler_params=params(60 << 20),
         name="token_grad",
-    )(tok, cot, gz, gx, wz, wx, gain)
-
-
-def segment_table(segments):
-    seqs, length = segments.shape
-    seg = segments.astype(f32)
-    blocks = length // Q
-
-    def earlier(k):
-        return jnp.concatenate([jnp.full((seqs, k), -1.0, f32), seg[:, :-k]], axis=1)
-
-    def later(k):
-        return jnp.concatenate([seg[:, k:], jnp.full((seqs, k), -1.0, f32)], axis=1)
-
-    by_block = seg.reshape(seqs, blocks, Q)
-    last = by_block[:, :, -1]
-    prev = jnp.concatenate([jnp.full((seqs, 1), -1.0, f32), last[:, :-1]], axis=1)
-    rows = [seg]
-    rows += [(earlier(k) == seg).astype(f32) for k in (1, 2, 3)]
-    rows += [(by_block == prev[..., None]).astype(f32).reshape(seqs, length)]
-    rows += [(by_block == last[..., None]).astype(f32).reshape(seqs, length)]
-    rows += [(later(k) == seg).astype(f32) for k in (1, 2, 3)]
-    rows += [jnp.zeros_like(seg)] * (16 - len(rows))
-    return jnp.stack(rows, axis=0).reshape(16, seqs * blocks, Q).transpose(1, 0, 2)
+    )(tok, cot, gz, gx, *[v for v, _ in weights], wx, gain)
+
+
+def partner(axis, bit):
+    me = lax.axis_index(axis)
+    return {axis: me + bit - 2 * bit * ((me // bit) % 2)}
+
+
+def finish_kernel(
+    steps, heads, cw_ref, cb_ref, ggain_ref, skip_ref, ngain_ref, alog_ref, dtb_ref, zo_ref, x_ref,
+    small_ref, din_ref, dout_ref, acc, got, zo_got, x_got, send, recv, big_send, big_recv,
+):
+    barrier = pltpu.get_barrier_semaphore()
+    for axis, bit in steps:
+        pl.semaphore_signal(barrier, inc=1, device_id=partner(axis, bit), device_id_type=pl.DeviceIdType.MESH)
+    pl.semaphore_wait(barrier, len(steps))
+
+    def exchange(src, dst, ssem, rsem, axis, bit):
+        copy = pltpu.make_async_remote_copy(
+            src_ref=src, dst_ref=dst, send_sem=ssem, recv_sem=rsem,
+            device_id=partner(axis, bit), device_id_type=pl.DeviceIdType.MESH,
+        )
+        copy.start()
+        return copy
+
+    axis, bit = steps[-1]
+    big = [
+        exchange(zo_ref, zo_got, big_send.at[0], big_recv.at[0], axis, bit),
+        exchange(x_ref, x_got, big_send.at[1], big_recv.at[1], axis, bit),
+    ]
+
+    inner, width = ggain_ref.shape[1], ngain_ref.shape[1]
+    channels = cb_ref.shape[1]
+    total = lambda v: jnp.sum(v, axis=0, keepdims=True)
+    acc[0] = jnp.zeros((8, channels), f32)
+    for k in range(4):
+        acc[0, k : k + 1, :] = total(cw_ref[8 * k : 8 * k + 8, :])
+    acc[0, 4:5, :] = total(cb_ref[...])
+    acc[0, 5:6, :inner] = total(ggain_ref[...])
+    acc[0, 6:7, :width] = total(ngain_ref[...])
+    acc[0, 6:7, width : width + LANES] = total(alog_ref[...])
+    acc[0, 6:7, width + LANES : width + 2 * LANES] = total(dtb_ref[...])
+    skip = jnp.concatenate(split(skip_ref[...], 3), axis=0)
+    by_head = ones_where(iota((inner, LANES), 0) // HEAD == iota((inner, LANES), 1))
+    acc[0, 6:7, width + 2 * LANES : width + 3 * LANES] = total(dot(skip, by_head))
+
+    for k, (axis, bit) in enumerate(steps):
+        exchange(acc.at[k], got.at[k], send.at[k], recv.at[k], axis, bit).wait()
+        acc[k + 1] = acc[k] + got[k]
+    small_ref[...] = acc[len(steps)]
+
+    for copy in big:
+        copy.wait()
+    own = din_ref.shape[0]
+    zo = zo_ref[...].astype(f32) + zo_got[...].astype(f32)
+    half = zo.shape[1]
+    din_ref[:, :half] = zo[:own]
+    din_ref[:, half : 2 * half] = zo[own : 2 * own]
+    dout_ref[...] = zo[2 * own :]
+    left = din_ref.shape[1] - 2 * half
+    din_ref[:, 2 * half :] = (x_ref[...].astype(f32) + x_got[...].astype(f32))[:, :left]
+
+
+def finish(p_cw, p_cb, p_ggain, p_skip, p_ngain, p_alog, p_dtb, d_zo, d_x, sizes, heads, proj):
+    steps = [(axis, 1 << i) for axis, n in sizes for i in range(n.bit_length() - 1)]
+    own, half = d_x.shape[0], d_zo.shape[1]
+    channels = p_cb.shape[1]
+    vmem = pl.BlockSpec(memory_space=pltpu.VMEM)
+    return pl.pallas_call(
+        functools.partial(finish_kernel, steps, heads),
+        in_specs=[vmem] * 9,
+        out_specs=[vmem] * 3,
+        out_shape=[
+            jax.ShapeDtypeStruct((8, channels), f32),
+            jax.ShapeDtypeStruct((own, proj), f32),
+            jax.ShapeDtypeStruct((2 * own, half), f32),
+        ],
+        scratch_shapes=[
+            pltpu.VMEM((len(steps) + 1, 8, channels), f32),
+            pltpu.VMEM((len(steps), 8, channels), f32),
+            pltpu.VMEM(d_zo.shape, bf16),
+            pltpu.VMEM(d_x.shape, bf16),
+            pltpu.SemaphoreType.DMA((len(steps),)),
+            pltpu.SemaphoreType.DMA((len(steps),)),
+            pltpu.SemaphoreType.DMA((2,)),
+            pltpu.SemaphoreType.DMA((2,)),
+        ],
+        compiler_params=params(48 << 20, collective_id=0, has_side_effects=True),
+        name="finish",
+    )(p_cw, p_cb, p_ggain, p_skip, p_ngain, p_alog, p_dtb, d_zo, d_x)
 
 
 def per_device(
-    tokens, segments, cotangent, norm_gain, weight_in, conv_weight, conv_bias, dt_bias, a_log, skip_d,
+    sizes, tokens, segments, cotangent, norm_gain, weight_in, conv_weight, conv_bias, dt_bias, a_log, skip_d,
     gate_gain, weight_out,
 ):
     seqs, length, width = tokens.shape
@@ -547,65 +698,57 @@
     inner = gate_gain.shape[0]
     channels = conv_bias.shape[0]
     heads = dt_bias.shape[0]
+    own = weight_in.shape[0]
+    owners = width // own
     tok = tokens.reshape(rows, width)
     cot = cotangent.reshape(rows, width)
     pad = LANES - heads
 
     local_x = jnp.pad(weight_in[:, inner:], ((0, 0), (0, pad)))
     wx = lax.all_gather(local_x, "dp", axis=0, tiled=True)
-    wz = lax.all_gather(weight_in[:, :inner], "dp", axis=0, tiled=True)
-    wo = lax.all_gather(weight_out, "dp", axis=0, tiled=True)
-
-    def row(v):
-        return jnp.pad(v, (0, pad)).reshape(1, LANES)
-
-    tab = segment_table(segments)
-    neg_rate = -jnp.exp(a_log)
-    na, na2 = row(neg_rate), row(neg_rate * LOG2E)
-    dtb = row(dt_bias)
-    head_of = jnp.arange(inner) // (inner // heads)
-    skip = skip_d[head_of].reshape(1, inner)
-    et = (head_of[:, None] == jnp.arange(LANES)[None, :]).astype(bf16)
-    e2 = jnp.concatenate([et.T, et.T], axis=0)
-    pos = jnp.arange(Q)
-    tri = (pos[:, None] >= pos[None, :]).astype(bf16)
-    below = (pos[:, None] > pos[None, :]).astype(bf16)
-    tail = jnp.concatenate([tri.T, tri.T, below, below], axis=1)
-    pair = jnp.kron(jnp.eye(2, dtype=f32), tri.astype(f32)).astype(bf16)
+    local_zo = jnp.concatenate([weight_in[:, :width], weight_in[:, width:inner], weight_out], axis=0)
+    slab = lax.all_gather(local_zo, "dp", axis=0, tiled=True).reshape(owners, 4 * own, width)
+    weights = slab_views(slab, own)
+
+    head = jnp.pad(jnp.stack([dt_bias, -jnp.exp(a_log), skip_d]), ((0, 5), (0, pad)))
+    seg = segments.astype(f32).reshape(rows // Q, Q)
     cb = conv_bias.reshape(1, channels)
     ngain = norm_gain.reshape(1, width)
     ggain = gate_gain.reshape(1, inner)
 
     normed, xbc, dt = project(tok, ngain, wx, channels)
-    y, s, sin = state_forward(tab, xbc, dt, conv_weight, cb, dtb, na2, skip, e2, tri, seqs)
-    gn, out, gz, gm, p_ggain = gate(tok, normed, y, cot, wz, wo, ggain)
+    y, s, sin = state_forward(seg, xbc, dt, conv_weight, cb, head, inner, seqs)
+    gn, out, gz, gm, p_ggain = gate(tok, normed, y, cot, weights, ggain)
+    d_z = dot(normed, gz, TN).astype(bf16)
     d_out = dot(gn, cot, TN).astype(bf16)
-    d_z = dot(normed, gz, TN).astype(bf16)
-    d_out = lax.psum_scatter(d_out, "dp", scatter_dimension=0, tiled=True)
-    d_z = lax.psum_scatter(d_z, "dp", scatter_dimension=0, tiled=True)
-    gx, p_cw, p_cb, p_skip, p_alog, p_dtb = state_backward(
-        tab, xbc, dt, s, sin, gm, conv_weight, dtb, na2, na, skip, e2, et, tri, tail, pair, seqs
-    )
+    d_zo = jnp.concatenate(
+        [
+            d_z[:, :width].reshape(owners, own, width),
+            d_z[:, width:].reshape(owners, own, width),
+            d_out.reshape(owners, 2 * own, width),
+        ],
+        axis=1,
+    ).reshape(owners * 4 * own, width)
+    d_zo = lax.psum_scatter(d_zo, "dp", scatter_dimension=0, tiled=True)
+    gx, p_cw, p_cb, p_skip, p_alog, p_dtb = state_backward(seg, xbc, dt, s, sin, gm, conv_weight, head, seqs)
     d_x = dot(normed, gx, TN).astype(bf16)
     d_x = lax.psum_scatter(d_x, "dp", scatter_dimension=0, tiled=True)
-    g_tok, p_ngain = token_grad(tok, cot, gz, gx, wz, wx, ngain)
-
-    d_in = jnp.concatenate([d_z, d_x], axis=1)
-    d_in = lax.psum(d_in, "seq").astype(f32)[:, : weight_in.shape[1]]
-    d_out = lax.psum(d_out, "seq").astype(f32)
-    small = (
-        jnp.sum(p_ngain, axis=0),
-        jnp.sum(p_cw.reshape(4, 8, channels), axis=1),
-        jnp.sum(p_cb, axis=0),
-        jnp.sum(p_dtb, axis=0)[:heads],
-        jnp.sum(p_alog, axis=0)[:heads],
-        jnp.sum(p_skip.reshape(8, heads, inner // heads), axis=(0, 2)),
-        jnp.sum(p_ggain, axis=0),
+    g_tok, p_ngain = token_grad(tok, cot, gz, gx, weights[:2], wx, ngain)
+    small, d_in, d_out = finish(
+        p_cw, p_cb, p_ggain, p_skip, p_ngain, p_alog, p_dtb, d_zo, d_x, sizes, heads, weight_in.shape[1]
     )
-    s_ngain, s_cw, s_cb, s_dtb, s_alog, s_skip, s_ggain = lax.psum(small, ("dp", "seq"))
     return (
-        out.reshape(tokens.shape), g_tok.reshape(tokens.shape), s_ngain, d_in, s_cw, s_cb, s_dtb, s_alog,
-        s_skip, s_ggain, d_out,
+        out.reshape(tokens.shape),
+        g_tok.reshape(tokens.shape),
+        small[6, :width],
+        d_in,
+        small[:4],
+        small[4],
+        small[6, width + LANES : width + LANES + heads],
+        small[6, width : width + heads],
+        small[6, width + 2 * LANES : width + 2 * LANES + heads],
+        small[5, :inner],
+        d_out,
     )
 
 
@@ -614,7 +757,7 @@
     owned = P("dp", None)
     placed = (data, P(("dp", "seq"), None), data, P(), owned, P(), P(), P(), P(), P(), P(), owned)
     return jax.shard_map(
-        per_device,
+        functools.partial(per_device, [(axis, mesh.shape[axis]) for axis in ("dp", "seq")]),
         mesh=mesh,
         in_specs=placed,
         out_specs=(data, data, P(), owned, P(), P(), P(), P(), P(), P(), owned),

time: 503 us -> 428 us (0.85)
  blocking collectives: 41.8 us -> 0 us
  waiting for transfers between devices: 167 us -> 140 us
  other arithmetic: 28.1 us -> 6.68 us
  Pallas kernels: 204 us -> 223 us
    psum x1 -> x0, blocking collectives: 41.8 us -> none  [per_device(): lax.psum(small, ('dp', 'seq'))]
    all_gather x2 -> x1, waiting for transfers between devices: 33.5 us -> 0.01 us  [per_device(): lax.all_gather(local_zo, 'dp', axis=0, tiled=True)]
    reduce_scatter x1, waiting for transfers between devices: 53.3 us -> 22.4 us  [per_device(): d_x = lax.psum_scatter(d_x, 'dp', scatter_dimension=0, tiled=True)]
    all_gather x1, waiting for transfers between devices: 14.7 us -> 39.1 us  [per_device(): wx = lax.all_gather(local_x, 'dp', axis=0, tiled=True)]
    pallas_call x2 -> x3, Pallas kernels: 134 us -> 153 us  [the longest x1 93.7 us: state_backward(): pl.pallas_call(bwd_kernel, grid=(seqs, blocks), in_specs=[fixed(seg.shape...]
    gather x19 -> x0, other arithmetic: 15.9 us -> none  [per_device(): skip = skip_d[head_of].reshape(1, inner)]
    reduce_scatter x2 -> x1, waiting for transfers between devices: 64.7 us -> 78.3 us  [per_device(): d_zo = lax.psum_scatter(d_zo, 'dp', scatter_dimension=0, tiled=True)]
    unnamed x19 -> x24, local copies, waits for them, and re-layouts: 0.8 us -> 6.07 us
  transfers between devices with their start and end apart: 7 -> 4, of which waited for: 4 -> 3; matrix products, arithmetic and copies ran while one was open for 12% -> 7% of each run, Pallas kernels for 33% -> 17%
where the time goes in v2:
time: 428 us; the launch traced here: 427 us
  Pallas kernels  223 us (52%)
  waiting for transfers between devices  140 us (33%)
  matrix products  27.2 us (6%)
  local copies, waits for them, and re-layouts  16.3 us (4%)
  between operations  13.9 us (3%)
  other arithmetic  6.68 us (2%)
    pallas_call x1, Pallas kernels, state_backward(): pl.pallas_call(bwd_kernel, grid=(seqs, blocks), in_specs=[fixed(seg.shape...  93.7 us
    reduce_scatter x1, waiting for transfers between devices, per_device(): d_zo = lax.psum_scatter(d_zo, 'dp', scatter_dimension=0, tiled=True)  78.3 us
    pallas_call x1, Pallas kernels, state_forward(): pl.pallas_call(fwd_kernel, grid=(seqs, blocks), in_specs=[fixed(seg.shape...  41.8 us
    all_gather x1, waiting for transfers between devices, per_device(): wx = lax.all_gather(local_x, 'dp', axis=0, tiled=True)  39.1 us
    pallas_call x1, Pallas kernels, gate(): pl.pallas_call(gate_kernel, grid=(rows // tile,), in_specs=[pl.BlockSpec(...  37.1 us
    dot_general x3, matrix products, dot(): return lax.dot_general(a, b, dims, preferred_element_type=f32)  27.2 us
    reduce_scatter x1, waiting for transfers between devices, per_device(): d_x = lax.psum_scatter(d_x, 'dp', scatter_dimension=0, tiled=True)  22.4 us
    pallas_call x1, Pallas kernels, token_grad(): pl.pallas_call(token_kernel, grid=(rows // tile,), in_specs=[pl.BlockSpec...  20 us
  transfers between devices with their start and end apart: 4, of which 3 were waited for; matrix products, arithmetic and copies ran while one was open for 7% of the time, Pallas kernels for 17%

profile of v2, /device:TPU:0, one launch (start us, length us, event | category | flops | bytes accessed | tf_op | source)
XLA Modules:
  0.0 426.8 jit_solution(1615136827710488101)
XLA Ops:
  7.2 0.0 all-gather.3.cloned.1.call-start
  7.2 0.9 slice.36
  8.2 0.7 pad.8
  8.9 0.0 all-gather.3.cloned.1.call-update
  8.9 0.0 all-gather.5.cloned.1.call-start
  8.9 0.9 fusion.1
  9.9 1.6 pad_maximum_fusion.1
  11.5 0.0 all-gather.5.cloned.1.call-update
  11.5 0.0 reduce-scatter.5.cloned.1.call-start
  11.6 1.3 reshape.62.gain_ref
  12.9 1.3 reshape.67.gain_ref
  14.2 1.3 reshape.64.cb_ref
  15.5 0.7 convert_element_type.16
  16.2 0.6 reshape.63.seg_ref
  16.8 0.7 negate_bitcast_fusion
  17.4 1.3 select_maximum_fusion.head_ref
  18.7 39.1 %all-gather.3.cloned.1.call-done.wx_ref = bf16[768,1920]{1,0:T(8,128)(2,1)} async-done(((bf16[48,1920]{1,0:T(8,128)(2,1)}), bf16[768,1920]{1,0:T(8,128)(2,1)}) %all-gather.3.cloned.1.call-update) | async-done | bytes 2949136 | tf_op jit(solution)/shard_map/all_gather | solution.py:708
  57.8 12.7 %project.1 = (bf16[2048,768]{1,0:T(8,128)(2,1)}, f32[2048,1792]{1,0:T(8,128)}, f32[2048,128]{1,0:T(8,128)}) custom-call(bf16[2048,768]{1,0:T(8,128)(2,1)} %bitcast.30, f32[1,768]{1,0:T(1,128)} %reshape.62.gain_ref, bf16[768,1920]{1,0:T(8,128)(2,1)} %all-gather.3.cloned.1.call-done.wx_ref), custom_call_target="tpu_custom_call" | custom-call | tf_op jit(solution)/shard_map/project/pallas_call | solution.py:82
  70.5 41.8 %state_forward.1 = (f32[2048,1536]{1,0:T(8,128)}, f32[2048,1792]{1,0:T(8,128)}, bf16[16,128,1536]{2,1,0:T(8,128)(2,1)}) custom-call(f32[16,128]{1,0:T(8,128)} %reshape.63.seg_ref, f32[2048,1792]{1,0:T(8,128)} %get-tuple-element.34.xbc_ref, f32[2048,128]{1,0:T(8,128)} %get-tuple-element.35.dt_ref, f32[4,1792]{1,0:T(4,128)} %cw_ref.3, ...), custom_call_target="tpu_custom_call" | custom-call | tf_op jit(solution)/shard_map/state_forward/pallas_call | solution.py:255
  112.3 0.0 all-gather.5.cloned.1.call-done
  112.3 37.1 %gate.1 = (bf16[2048,1536]{1,0:T(8,128)(2,1)}, bf16[2048,768]{1,0:T(8,128)(2,1)}, bf16[2048,1536]{1,0:T(8,128)(2,1)}, f32[2048,1536]{1,0:T(8,128)}, f32[8,1536]{1,0:T(8,128)}) custom-call(bf16[2048,768]{1,0:T(8,128)(2,1)} %bitcast.31, bf16[2048,768]{1,0:T(8,128)(2,1)} %get-tuple-element.33.normed_ref, f32[2048,1536]{1,0:T(8,128)} %get-tuple-element.36.y_ref, ...), custom_call_target="tpu_custom_call" | custom-call | tf_op jit(solution)/shard_map/gate/pallas_call | solution.py:337
  149.4 0.0 copy-start.10
  149.4 93.7 %state_backward.1 = (bf16[2048,1920]{1,0:T(8,128)(2,1)}, f32[32,1792]{1,0:T(8,128)}, f32[8,1792]{1,0:T(8,128)}, f32[8,1536]{1,0:T(8,128)}, f32[8,128]{1,0:T(8,128)}, /*index=5*/f32[8,128]{1,0:T(8,128)}) custom-call(f32[16,128]{1,0:T(8,128)} %reshape.63.seg_ref, f32[2048,1792]{1,0:T(8,128)} %get-tuple-element.34.xbc_ref, ...), custom_call_target="tpu_custom_call" | custom-call | tf_op jit(solution)/shard_map/state_backward/pallas_call | solution.py:521
  243.1 11.4 %convolution_convert_fusion = bf16[768,1920]{1,0:T(8,128)(2,1)} fusion(bf16[2048,768]{1,0:T(8,128)(2,1)S(1)} %copy-done.10, bf16[2048,1920]{1,0:T(8,128)(2,1)} %get-tuple-element.42.gx_ref), kind=kOutput, calls=%fused_computation.1 | convolution fusion | flops 6041272320 | bytes 13959168 | tf_op jit(solution)/shard_map/dot_general | solution.py:26
  254.5 0.0 reduce-scatter.5.cloned.1.call-update
  254.5 0.0 reduce-scatter.3.cloned.1.call-start
  254.5 8.3 %convolution_convert_fusion.2 = bf16[768,1536]{1,0:T(8,128)(2,1)S(1)} fusion(bf16[2048,768]{1,0:T(8,128)(2,1)S(1)} %copy-done.10, bf16[2048,1536]{1,0:T(8,128)(2,1)} %get-tuple-element.38.gz_ref), kind=kOutput, calls=%fused_computation.3 | convolution fusion | flops 4833017856 | bytes 11796480 | tf_op jit(solution)/shard_map/dot_general | solution.py:26
  262.9 0.0 copy-start.9
  262.9 0.2 fusion
  263.0 1.9 copy-done.9
  264.9 7.5 %convolution_convert_fusion.1 = bf16[1536,768]{1,0:T(8,128)(2,1)S(1)} fusion(bf16[2048,1536]{1,0:T(8,128)(2,1)} %get-tuple-element.51, bf16[2048,768]{1,0:T(8,128)(2,1)S(1)} %bitcast.36), kind=kOutput, calls=%fused_computation.2 | convolution fusion | flops 4833017856 | bytes 11796480 | tf_op jit(solution)/shard_map/dot_general | solution.py:26
  272.4 2.4 pad_maximum_fusion
  274.8 0.0 reduce-scatter.3.cloned.1.call-update
  274.8 0.0 copy-start.7
  274.9 20.0 %token_grad.1 = (bf16[2048,768]{1,0:T(8,128)(2,1)}, f32[8,768]{1,0:T(8,128)}) custom-call(bf16[2048,768]{1,0:T(8,128)(2,1)} %bitcast.32, bf16[2048,768]{1,0:T(8,128)(2,1)} %bitcast.35, bf16[2048,1536]{1,0:T(8,128)(2,1)} %get-tuple-element.38.gz_ref, bf16[2048,1920]{1,0:T(8,128)(2,1)} %get-tuple-element.42.gx_ref, bf16[16,192,768]{2,1,0:T(8,128)(2,1)} %bitcast.28, ...), custom_call_target="tpu_custom_call" | custom-call | tf_op jit(solution)/shard_map/token_grad/pallas_call | solution.py:586
  294.9 22.4 %reduce-scatter.5.cloned.1.call-done.x_ref = bf16[48,1920]{1,0:T(8,128)(2,1)} async-done(((bf16[768,1920]{1,0:T(8,128)(2,1)}), bf16[48,1920]{1,0:T(8,128)(2,1)}) %reduce-scatter.5.cloned.1.call-update) | async-done | bytes 184336 | tf_op jit(solution)/shard_map/reduce_scatter | solution.py:735
  317.3 78.3 %reduce-scatter.3.cloned.1.call-done.zo_ref = bf16[192,768]{1,0:T(8,128)(2,1)} async-done(((bf16[3072,768]{1,0:T(8,128)(2,1)}), bf16[192,768]{1,0:T(8,128)(2,1)}) %reduce-scatter.3.cloned.1.call-update) | async-done | bytes 294928 | tf_op jit(solution)/shard_map/reduce_scatter | solution.py:732
  395.6 1.0 copy-done
  396.6 0.9 copy-done.2
  397.5 0.7 copy-done.6
  398.3 17.5 %finish.1 = (f32[8,1792]{1,0:T(8,128)S(1)}, f32[48,3352]{1,0:T(8,128)S(1)}, f32[96,768]{1,0:T(8,128)S(1)}) custom-call(f32[32,1792]{1,0:T(8,128)S(1)} %copy-done.1, f32[8,1792]{1,0:T(8,128)S(1)} %copy-done.3, f32[8,1536]{1,0:T(8,128)S(1)} %copy-done.4, f32[8,1536]{1,0:T(8,128)S(1)} %copy-done.5, f32[8,768]{1,0:T(8,128)S(1)} %copy-done.6, ...), custom_call_target="tpu_custom_call" | custom-call | tf_op jit(solution)/shard_map/finish/pallas_call | solution.py:668
  415.7 0.5 slice_bitcast_fusion
  416.3 0.6 slice_reduce_fusion.2
  416.9 0.6 slice_reduce_fusion.1
  417.5 0.6 slice_reduce_fusion
  418.1 0.6 slice.42
  418.7 0.8 copy.25
  419.6 0.7 copy.26
  (15 shorter events, 0.0 us)
Async XLA Ops:
  7.2 50.6 %all-gather.3.cloned.1.call-start = ((), (), s32[]{:S(2)}) async-start(), calls=%async_computation.2 | async-start | bytes 3133440 | tf_op jit(solution)/shard_map/all_gather | solution.py:708
  8.9 103.4 %all-gather.5.cloned.1.call-start = ((), (), s32[]{:S(2)}) async-start(), calls=%async_computation.3 | async-start | bytes 5013504 | tf_op jit(solution)/shard_map/all_gather | solution.py:710
  11.5 305.8 %reduce-scatter.5.cloned.1.call-start = ((), (), s32[]{:S(2)}) async-start(), calls=%async_computation.5 | async-start | bytes 3133440 | tf_op jit(solution)/shard_map/reduce_scatter | solution.py:735
  149.4 93.7 %copy-start.10 = (bf16[2048,768]{1,0:T(8,128)(2,1)S(1)}, bf16[2048,768]{1,0:T(8,128)(2,1)}, u32[]{:S(2)}) copy-start(bf16[2048,768]{1,0:T(8,128)(2,1)} %get-tuple-element.33.normed_ref) | copy-start | bytes 9437188
  254.5 141.1 %reduce-scatter.3.cloned.1.call-start = ((), (), s32[]{:S(2)}) async-start(), calls=%async_computation.4 | async-start | bytes 5013504 | tf_op jit(solution)/shard_map/reduce_scatter | solution.py:732
  262.9 2.0 copy-start.9
  274.8 120.8 %copy-start.1 = (f32[32,1792]{1,0:T(8,128)S(1)}, f32[32,1792]{1,0:T(8,128)}, u32[]{:S(2)}) copy-start(f32[32,1792]{1,0:T(8,128)} %get-tuple-element.44.cw_ref) | copy-start | bytes 688132
  274.8 120.8 %copy-start.3 = (f32[8,1792]{1,0:T(8,128)S(1)}, f32[8,1792]{1,0:T(8,128)}, u32[]{:S(2)}) copy-start(f32[8,1792]{1,0:T(8,128)} %get-tuple-element.45.cb_ref) | copy-start | bytes 172036
  274.8 120.8 %copy-start.4 = (f32[8,1536]{1,0:T(8,128)S(1)}, f32[8,1536]{1,0:T(8,128)}, u32[]{:S(2)}) copy-start(f32[8,1536]{1,0:T(8,128)} %get-tuple-element.46.ggain_ref) | copy-start | bytes 147460
  274.8 120.8 %copy-start.5 = (f32[8,1536]{1,0:T(8,128)S(1)}, f32[8,1536]{1,0:T(8,128)}, u32[]{:S(2)}) copy-start(f32[8,1536]{1,0:T(8,128)} %get-tuple-element.47.skip_ref) | copy-start | bytes 147460
  274.8 120.8 %copy-start.7 = (f32[8,128]{1,0:T(8,128)S(1)}, f32[8,128]{1,0:T(8,128)}, u32[]{:S(2)}) copy-start(f32[8,128]{1,0:T(8,128)} %get-tuple-element.49.alog_ref) | copy-start | bytes 12292
  274.9 120.8 %copy-start.8 = (f32[8,128]{1,0:T(8,128)S(1)}, f32[8,128]{1,0:T(8,128)}, u32[]{:S(2)}) copy-start(f32[8,128]{1,0:T(8,128)} %get-tuple-element.50.dtb_ref) | copy-start | bytes 12292
  395.6 1.0 copy-start
  396.6 0.9 copy-start.2
  397.5 0.7 copy-start.6
Sparse Core Ops, SparseCore 0:
  10.7 47.0 all-gather.2
  60.7 51.4 all-gather.4
  254.6 62.6 reduce-scatter.4
  321.0 74.5 reduce-scatter.2

commit v3 on v2

--- a/solution.py
+++ b/solution.py
@@ -169,6 +169,13 @@
     return jnp.concatenate([jnp.where(left, v, zero), jnp.where(left, zero, v)], axis=0)
 
 
+def later_rows(v, k):
+    width = v.shape[1]
+    v = pltpu.roll(v.reshape(-1, 8, width), 8 - k, 1)
+    here = lax.broadcasted_iota(jnp.int32, (1, 8, width), 1) < 8 - k
+    return jnp.where(here, v[:-1], v[1:]).reshape(-1, width)
+
+
 def fwd_kernel(
     seg_ref, xbc_ref, dt_ref, cw_ref, cb_ref, head_ref,
     y_ref, s_ref, sin_ref, state, ext, e_ref, tri_ref, skip_ref,
@@ -197,10 +204,11 @@
 
     def conv(c):
         at = pl.ds(c, 256)
-        s = cb_ref[:, at] + cw_ref[3:4, at] * ext[8 : 8 + Q, at]
-        s += m1 * (cw_ref[2:3, at] * ext[7 : 7 + Q, at])
-        s += m2 * (cw_ref[1:2, at] * ext[6 : 6 + Q, at])
-        s += m3 * (cw_ref[0:1, at] * ext[5 : 5 + Q, at])
+        x = ext[:, at]
+        s = cb_ref[:, at] + cw_ref[3:4, at] * x[8:]
+        s += m1 * (cw_ref[2:3, at] * later_rows(x, 7))
+        s += m2 * (cw_ref[1:2, at] * later_rows(x, 6))
+        s += m3 * (cw_ref[0:1, at] * later_rows(x, 5))
         s_ref[:, at] = s
         return s * sigmoid(s)
 
@@ -498,10 +506,11 @@
     for c in range(0, channels, 256):
         at = pl.ds(c, 256)
         x = xbc_ref[:, at]
-        g0 = gext[0:Q, at]
-        g1 = gext[1 : 1 + Q, at] * n1
-        g2 = gext[2 : 2 + Q, at] * n2
-        g3 = gext[3 : 3 + Q, at] * n3
+        g = gext[:, at]
+        g0 = g[:Q]
+        g1 = later_rows(g, 1) * n1
+        g2 = later_rows(g, 2) * n2
+        g3 = later_rows(g, 3) * n3
         gx = cw_ref[3:4, at] * g0 + cw_ref[2:3, at] * g1 + cw_ref[1:2, at] * g2 + cw_ref[0:1, at] * g3
         gx_ref[:, at] = gx.astype(bf16)
         gcb_ref[:, at] += fold_rows(g0)
@@ -609,10 +618,12 @@
     steps, heads, cw_ref, cb_ref, ggain_ref, skip_ref, ngain_ref, alog_ref, dtb_ref, zo_ref, x_ref,
     small_ref, din_ref, dout_ref, acc, got, zo_got, x_got, send, recv, big_send, big_recv,
 ):
-    barrier = pltpu.get_barrier_semaphore()
+    if steps:
+        barrier = pltpu.get_barrier_semaphore()
     for axis, bit in steps:
         pl.semaphore_signal(barrier, inc=1, device_id=partner(axis, bit), device_id_type=pl.DeviceIdType.MESH)
-    pl.semaphore_wait(barrier, len(steps))
+    if steps:
+        pl.semaphore_wait(barrier, len(steps))
 
     def exchange(src, dst, ssem, rsem, axis, bit):
         copy = pltpu.make_async_remote_copy(
@@ -622,11 +633,10 @@
         copy.start()
         return copy
 
-    axis, bit = steps[-1]
-    big = [
-        exchange(zo_ref, zo_got, big_send.at[0], big_recv.at[0], axis, bit),
-        exchange(x_ref, x_got, big_send.at[1], big_recv.at[1], axis, bit),
-    ]
+    big = []
+    for axis, bit in steps[-1:]:
+        big.append(exchange(zo_ref, zo_got, big_send.at[0], big_recv.at[0], axis, bit))
+        big.append(exchange(x_ref, x_got, big_send.at[1], big_recv.at[1], axis, bit))
 
     inner, width = ggain_ref.shape[1], ngain_ref.shape[1]
     channels = cb_ref.shape[1]
@@ -676,15 +686,15 @@
         ],
         scratch_shapes=[
             pltpu.VMEM((len(steps) + 1, 8, channels), f32),
-            pltpu.VMEM((len(steps), 8, channels), f32),
+            pltpu.VMEM((max(len(steps), 1), 8, channels), f32),
             pltpu.VMEM(d_zo.shape, bf16),
             pltpu.VMEM(d_x.shape, bf16),
-            pltpu.SemaphoreType.DMA((len(steps),)),
-            pltpu.SemaphoreType.DMA((len(steps),)),
+            pltpu.SemaphoreType.DMA((max(len(steps), 1),)),
+            pltpu.SemaphoreType.DMA((max(len(steps), 1),)),
             pltpu.SemaphoreType.DMA((2,)),
             pltpu.SemaphoreType.DMA((2,)),
         ],
-        compiler_params=params(48 << 20, collective_id=0, has_side_effects=True),
+        compiler_params=params(48 << 20, collective_id=0 if steps else None, has_side_effects=True),
         name="finish",
     )(p_cw, p_cb, p_ggain, p_skip, p_ngain, p_alog, p_dtb, d_zo, d_x)
 
@@ -729,6 +739,7 @@
         ],
         axis=1,
     ).reshape(owners * 4 * own, width)
+    d_zo, gm = lax.optimization_barrier((d_zo, gm))
     d_zo = lax.psum_scatter(d_zo, "dp", scatter_dimension=0, tiled=True)
     gx, p_cw, p_cb, p_skip, p_alog, p_dtb = state_backward(seg, xbc, dt, s, sin, gm, conv_weight, head, seqs)
     d_x = dot(normed, gx, TN).astype(bf16)

time: 428 us -> 433 us (1.012)
  waiting for transfers between devices: 140 us -> 160 us
  Pallas kernels: 223 us -> 213 us
    reduce_scatter x1, waiting for transfers between devices: 22.4 us -> 42 us  [per_device(): d_x = lax.psum_scatter(d_x, 'dp', scatter_dimension=0, tiled=True)]
    pallas_call x1, Pallas kernels: 93.7 us -> 83.8 us  [state_backward(): pl.pallas_call(bwd_kernel, grid=(seqs, blocks), in_specs=[fixed(seg.shape...]
  transfers between devices with their start and end apart: 4 -> 4, of which waited for: 3 -> 4; matrix products, arithmetic and copies ran while one was open for 7% -> 2% of each run, Pallas kernels for 17% -> 17%
where the time goes in v3:
time: 433 us
  Pallas kernels  213 us (49%)
  waiting for transfers between devices  160 us (37%)
  matrix products  24.4 us (6%)
  local copies, waits for them, and re-layouts  14.4 us (3%)
  between operations  13.9 us (3%)
  other arithmetic  6.69 us (2%)
    pallas_call x1, Pallas kernels, state_backward(): pl.pallas_call(bwd_kernel, grid=(seqs, blocks), in_specs=[fixed(seg.shape...  83.8 us
    reduce_scatter x1, waiting for transfers between devices, per_device(): d_zo = lax.psum_scatter(d_zo, 'dp', scatter_dimension=0, tiled=True)  78.3 us
    reduce_scatter x1, waiting for transfers between devices, per_device(): d_x = lax.psum_scatter(d_x, 'dp', scatter_dimension=0, tiled=True)  42 us
    pallas_call x1, Pallas kernels, state_forward(): pl.pallas_call(fwd_kernel, grid=(seqs, blocks), in_specs=[fixed(seg.shape...  41.5 us
    all_gather x1, waiting for transfers between devices, per_device(): wx = lax.all_gather(local_x, 'dp', axis=0, tiled=True)  39.1 us
    pallas_call x1, Pallas kernels, gate(): pl.pallas_call(gate_kernel, grid=(rows // tile,), in_specs=[pl.BlockSpec(...  37.2 us
    dot_general x3, matrix products, dot(): return lax.dot_general(a, b, dims, preferred_element_type=f32)  24.4 us
    pallas_call x1, Pallas kernels, token_grad(): pl.pallas_call(token_kernel, grid=(rows // tile,), in_specs=[pl.BlockSpec...  20.2 us
  transfers between devices with their start and end apart: 4, of which 4 were waited for; matrix products, arithmetic and copies ran while one was open for 2% of the time, Pallas kernels for 17%

profile of v3, /device:TPU:0, one launch (start us, length us, event | category | flops | bytes accessed | tf_op | source)
XLA Modules:
  0.0 432.6 jit_solution(13980382756944163252)
XLA Ops:
  7.2 0.0 all-gather.3.cloned.1.call-start
  7.2 0.9 slice.36
  8.2 0.7 pad.8
  8.9 0.0 all-gather.3.cloned.1.call-update
  8.9 0.0 all-gather.5.cloned.1.call-start
  8.9 0.9 fusion.1
  9.9 1.6 pad_maximum_fusion.1
  11.5 0.0 all-gather.5.cloned.1.call-update
  11.5 0.0 reduce-scatter.5.cloned.1.call-start
  11.6 1.3 reshape.62.gain_ref
  12.9 1.3 reshape.67.gain_ref
  14.2 1.3 reshape.64.cb_ref
  15.5 0.7 convert_element_type.16
  16.2 0.6 reshape.63.seg_ref
  16.8 0.7 negate_bitcast_fusion
  17.4 1.3 select_maximum_fusion.head_ref
  18.7 39.1 %all-gather.3.cloned.1.call-done.wx_ref = bf16[768,1920]{1,0:T(8,128)(2,1)} async-done(((bf16[48,1920]{1,0:T(8,128)(2,1)}), bf16[768,1920]{1,0:T(8,128)(2,1)}) %all-gather.3.cloned.1.call-update) | async-done | bytes 2949136 | tf_op jit(solution)/shard_map/all_gather | solution.py:718
  57.8 12.7 %project.1 = (bf16[2048,768]{1,0:T(8,128)(2,1)}, f32[2048,1792]{1,0:T(8,128)}, f32[2048,128]{1,0:T(8,128)}) custom-call(bf16[2048,768]{1,0:T(8,128)(2,1)} %bitcast.30, f32[1,768]{1,0:T(1,128)} %reshape.62.gain_ref, bf16[768,1920]{1,0:T(8,128)(2,1)} %all-gather.3.cloned.1.call-done.wx_ref), custom_call_target="tpu_custom_call" | custom-call | tf_op jit(solution)/shard_map/project/pallas_call | solution.py:82
  70.5 41.5 %state_forward.1 = (f32[2048,1536]{1,0:T(8,128)}, f32[2048,1792]{1,0:T(8,128)}, bf16[16,128,1536]{2,1,0:T(8,128)(2,1)}) custom-call(f32[16,128]{1,0:T(8,128)} %reshape.63.seg_ref, f32[2048,1792]{1,0:T(8,128)} %get-tuple-element.36.xbc_ref, f32[2048,128]{1,0:T(8,128)} %get-tuple-element.37.dt_ref, f32[4,1792]{1,0:T(4,128)} %cw_ref.3, ...), custom_call_target="tpu_custom_call" | custom-call | tf_op jit(solution)/shard_map/state_forward/pallas_call | solution.py:263
  112.0 0.1 all-gather.5.cloned.1.call-done
  112.2 37.2 %gate.1 = (bf16[2048,1536]{1,0:T(8,128)(2,1)}, bf16[2048,768]{1,0:T(8,128)(2,1)}, bf16[2048,1536]{1,0:T(8,128)(2,1)}, f32[2048,1536]{1,0:T(8,128)}, f32[8,1536]{1,0:T(8,128)}) custom-call(bf16[2048,768]{1,0:T(8,128)(2,1)} %bitcast.31, bf16[2048,768]{1,0:T(8,128)(2,1)} %get-tuple-element.35.normed_ref, f32[2048,1536]{1,0:T(8,128)} %get-tuple-element.38.y_ref, ...), custom_call_target="tpu_custom_call" | custom-call | tf_op jit(solution)/shard_map/gate/pallas_call | solution.py:345
  149.3 0.0 copy-start.11
  149.4 7.4 %convolution_convert_fusion.1 = bf16[1536,768]{1,0:T(8,128)(2,1)S(1)} fusion(bf16[2048,1536]{1,0:T(8,128)(2,1)} %get-tuple-element.43, bf16[2048,768]{1,0:T(8,128)(2,1)S(1)} %bitcast.36), kind=kOutput, calls=%fused_computation.2 | convolution fusion | flops 4833017856 | bytes 11796480 | tf_op jit(solution)/shard_map/dot_general | solution.py:26
  156.8 5.6 %convolution_convert_fusion.2 = bf16[768,1536]{1,0:T(8,128)(2,1)S(1)} fusion(bf16[2048,768]{1,0:T(8,128)(2,1)S(1)} %copy-done.11, bf16[2048,1536]{1,0:T(8,128)(2,1)S(1)} %copy-done.10), kind=kOutput, calls=%fused_computation.3 | convolution fusion | flops 4833017856 | bytes 11796480 | tf_op jit(solution)/shard_map/dot_general | solution.py:26
  162.4 0.2 fusion
  162.6 2.4 pad_maximum_fusion
  165.0 83.8 %state_backward.1 = (bf16[2048,1920]{1,0:T(8,128)(2,1)}, f32[32,1792]{1,0:T(8,128)}, f32[8,1792]{1,0:T(8,128)}, f32[8,1536]{1,0:T(8,128)}, f32[8,128]{1,0:T(8,128)}, /*index=5*/f32[8,128]{1,0:T(8,128)}) custom-call(f32[16,128]{1,0:T(8,128)} %reshape.63.seg_ref, f32[2048,1792]{1,0:T(8,128)} %get-tuple-element.36.xbc_ref, ...), custom_call_target="tpu_custom_call" | custom-call | tf_op jit(solution)/shard_map/state_backward/pallas_call | solution.py:530
  248.8 11.4 %convolution_convert_fusion = bf16[768,1920]{1,0:T(8,128)(2,1)} fusion(bf16[2048,768]{1,0:T(8,128)(2,1)S(1)} %copy-done.12, bf16[2048,1920]{1,0:T(8,128)(2,1)} %get-tuple-element.46.gx_ref), kind=kOutput, calls=%fused_computation.1 | convolution fusion | flops 6041272320 | bytes 13959168 | tf_op jit(solution)/shard_map/dot_general | solution.py:26
  260.2 0.0 reduce-scatter.5.cloned.1.call-update
  260.2 0.0 reduce-scatter.3.cloned.1.call-start
  260.3 0.5 reduce-scatter.3.cloned.1.call-update
  260.8 0.0 copy-start.1
  260.8 0.0 copy-start.3
  260.8 0.0 copy-start.7
  260.9 20.2 %token_grad.1 = (bf16[2048,768]{1,0:T(8,128)(2,1)}, f32[8,768]{1,0:T(8,128)}) custom-call(bf16[2048,768]{1,0:T(8,128)(2,1)} %bitcast.32, bf16[2048,768]{1,0:T(8,128)(2,1)} %bitcast.35, bf16[2048,1536]{1,0:T(8,128)(2,1)} %get-tuple-element.40.gz_ref, bf16[2048,1920]{1,0:T(8,128)(2,1)} %get-tuple-element.46.gx_ref, bf16[16,192,768]{2,1,0:T(8,128)(2,1)} %bitcast.28, ...), custom_call_target="tpu_custom_call" | custom-call | tf_op jit(solution)/shard_map/token_grad/pallas_call | solution.py:595
  281.1 42.0 %reduce-scatter.5.cloned.1.call-done.x_ref = bf16[48,1920]{1,0:T(8,128)(2,1)} async-done(((bf16[768,1920]{1,0:T(8,128)(2,1)}), bf16[48,1920]{1,0:T(8,128)(2,1)}) %reduce-scatter.5.cloned.1.call-update) | async-done | bytes 184336 | tf_op jit(solution)/shard_map/reduce_scatter | solution.py:746
  323.1 78.3 %reduce-scatter.3.cloned.1.call-done.zo_ref = bf16[192,768]{1,0:T(8,128)(2,1)} async-done(((bf16[3072,768]{1,0:T(8,128)(2,1)}), bf16[192,768]{1,0:T(8,128)(2,1)}) %reduce-scatter.3.cloned.1.call-update) | async-done | bytes 294928 | tf_op jit(solution)/shard_map/reduce_scatter | solution.py:743
  401.4 1.0 copy-done
  402.3 0.9 copy-done.2
  403.3 0.7 copy-done.6
  404.0 17.5 %finish.1 = (f32[8,1792]{1,0:T(8,128)S(1)}, f32[48,3352]{1,0:T(8,128)S(1)}, f32[96,768]{1,0:T(8,128)S(1)}) custom-call(f32[32,1792]{1,0:T(8,128)S(1)} %copy-done.1, f32[8,1792]{1,0:T(8,128)S(1)} %copy-done.3, f32[8,1536]{1,0:T(8,128)S(1)} %copy-done.4, f32[8,1536]{1,0:T(8,128)S(1)} %copy-done.5, f32[8,768]{1,0:T(8,128)S(1)} %copy-done.6, ...), custom_call_target="tpu_custom_call" | custom-call | tf_op jit(solution)/shard_map/finish/pallas_call | solution.py:678
  421.5 0.5 slice_bitcast_fusion
  422.0 0.6 slice_reduce_fusion.2
  422.6 0.6 slice_reduce_fusion.1
  423.2 0.6 slice_reduce_fusion
  423.9 0.6 slice.42
  424.5 0.8 copy.25
  425.3 0.7 copy.26
  (19 shorter events, 0.0 us)
Async XLA Ops:
  7.2 50.6 %all-gather.3.cloned.1.call-start = ((), (), s32[]{:S(2)}) async-start(), calls=%async_computation.2 | async-start | bytes 3133440 | tf_op jit(solution)/shard_map/all_gather | solution.py:718
  8.9 103.3 %all-gather.5.cloned.1.call-start = ((), (), s32[]{:S(2)}) async-start(), calls=%async_computation.3 | async-start | bytes 5013504 | tf_op jit(solution)/shard_map/all_gather | solution.py:720
  11.5 311.5 %reduce-scatter.5.cloned.1.call-start = ((), (), s32[]{:S(2)}) async-start(), calls=%async_computation.5 | async-start | bytes 3133440 | tf_op jit(solution)/shard_map/reduce_scatter | solution.py:746
  112.2 37.2 %copy-start.9 = (bf16[2,1024,768]{2,1,0:T(8,128)(2,1)S(1)}, bf16[2,1024,768]{2,1,0:T(8,128)(2,1)}, u32[]{:S(2)}) copy-start(bf16[2,1024,768]{2,1,0:T(8,128)(2,1)} %param.14) | copy-start | bytes 9437188
  149.3 7.4 %copy-start.10 = (bf16[2048,1536]{1,0:T(8,128)(2,1)S(1)}, bf16[2048,1536]{1,0:T(8,128)(2,1)}, u32[]{:S(2)}) copy-start(bf16[2048,1536]{1,0:T(8,128)(2,1)} %get-tuple-element.40.gz_ref) | copy-start | bytes 18874372
  149.3 7.4 %copy-start.11 = (bf16[2048,768]{1,0:T(8,128)(2,1)S(1)}, bf16[2048,768]{1,0:T(8,128)(2,1)}, u32[]{:S(2)}) copy-start(bf16[2048,768]{1,0:T(8,128)(2,1)} %get-tuple-element.35.normed_ref) | copy-start | bytes 9437188
  165.0 83.8 %copy-start.12 = (bf16[2048,768]{1,0:T(8,128)(2,1)S(1)}, bf16[2048,768]{1,0:T(8,128)(2,1)}, u32[]{:S(2)}) copy-start(bf16[2048,768]{1,0:T(8,128)(2,1)} %get-tuple-element.35.normed_ref) | copy-start | bytes 9437188
  260.2 141.1 %reduce-scatter.3.cloned.1.call-start = ((), (), s32[]{:S(2)}) async-start(), calls=%async_computation.4 | async-start | bytes 5013504 | tf_op jit(solution)/shard_map/reduce_scatter | solution.py:743
  260.8 140.5 %copy-start.1 = (f32[32,1792]{1,0:T(8,128)S(1)}, f32[32,1792]{1,0:T(8,128)}, u32[]{:S(2)}) copy-start(f32[32,1792]{1,0:T(8,128)} %get-tuple-element.48.cw_ref) | copy-start | bytes 688132
  260.8 140.5 %copy-start.3 = (f32[8,1792]{1,0:T(8,128)S(1)}, f32[8,1792]{1,0:T(8,128)}, u32[]{:S(2)}) copy-start(f32[8,1792]{1,0:T(8,128)} %get-tuple-element.49.cb_ref) | copy-start | bytes 172036
  260.8 140.5 %copy-start.4 = (f32[8,1536]{1,0:T(8,128)S(1)}, f32[8,1536]{1,0:T(8,128)}, u32[]{:S(2)}) copy-start(f32[8,1536]{1,0:T(8,128)} %get-tuple-element.50.ggain_ref) | copy-start | bytes 147460
  260.8 140.5 %copy-start.5 = (f32[8,1536]{1,0:T(8,128)S(1)}, f32[8,1536]{1,0:T(8,128)}, u32[]{:S(2)}) copy-start(f32[8,1536]{1,0:T(8,128)} %get-tuple-element.51.skip_ref) | copy-start | bytes 147460
  260.8 140.5 %copy-start.7 = (f32[8,128]{1,0:T(8,128)S(1)}, f32[8,128]{1,0:T(8,128)}, u32[]{:S(2)}) copy-start(f32[8,128]{1,0:T(8,128)} %get-tuple-element.53.alog_ref) | copy-start | bytes 12292
  260.8 140.5 %copy-start.8 = (f32[8,128]{1,0:T(8,128)S(1)}, f32[8,128]{1,0:T(8,128)}, u32[]{:S(2)}) copy-start(f32[8,128]{1,0:T(8,128)} %get-tuple-element.54.dtb_ref) | copy-start | bytes 12292
  401.4 1.0 copy-start
  402.3 0.9 copy-start.2
  403.3 0.7 copy-start.6
Sparse Core Ops, SparseCore 0:
  10.7 47.0 all-gather.2
  60.7 51.4 all-gather.4
  260.3 62.6 reduce-scatter.4
  326.8 74.5 reduce-scatter.2

commit v4 on v3

--- a/solution.py
+++ b/solution.py
@@ -313,25 +313,27 @@
     tok_ref, normed_ref, y_ref, cot_ref, wa_ref, wb_ref, wo_ref, gain_ref,
     gn_ref, out_ref, gz_ref, gm_ref, ggain_ref,
 ):
-    normed, wo = normed_ref[...], flat(wo_ref)
-    z = jnp.concatenate([dot(normed, flat(wa_ref)), dot(normed, flat(wb_ref))], axis=1)
+    wa, wb, wo = flat(wa_ref), flat(wb_ref), flat(wo_ref)
+    gain = gain_ref[...]
+
+    @pl.when(pl.program_id(0) == 0)
+    def _():
+        ggain_ref[...] = jnp.zeros_like(ggain_ref)
+
+    normed = normed_ref[...]
+    z = jnp.concatenate([dot(normed, wa), dot(normed, wb)], axis=1)
+    g_gn = dot(cot_ref[...], wo, NT)
     sg = sigmoid(z)
     sz = z * sg
     y = y_ref[...]
     gated = y * sz
     rstd = lax.rsqrt(jnp.mean(gated * gated, axis=-1, keepdims=True) + EPS)
     unit = gated * rstd
-    gn = (unit * gain_ref[...]).astype(bf16)
+    gn = (unit * gain).astype(bf16)
     gn_ref[...] = gn
     out_ref[...] = (tok_ref[...].astype(f32) + dot(gn, wo)).astype(bf16)
-    g_gn = dot(cot_ref[...], wo, NT)
-
-    @pl.when(pl.program_id(0) == 0)
-    def _():
-        ggain_ref[...] = jnp.zeros_like(ggain_ref)
-
     ggain_ref[...] += fold_rows(unit * g_gn)
-    q = g_gn * gain_ref[...]
+    q = g_gn * gain
     mean = jnp.mean(unit * q, axis=-1, keepdims=True)
     g_gated = rstd * (q - unit * mean)
     gm_ref[...] = g_gated * sz
@@ -743,6 +745,7 @@
     d_zo = lax.psum_scatter(d_zo, "dp", scatter_dimension=0, tiled=True)
     gx, p_cw, p_cb, p_skip, p_alog, p_dtb = state_backward(seg, xbc, dt, s, sin, gm, conv_weight, head, seqs)
     d_x = dot(normed, gx, TN).astype(bf16)
+    d_x, d_zo = lax.optimization_barrier((d_x, d_zo))
     d_x = lax.psum_scatter(d_x, "dp", scatter_dimension=0, tiled=True)
     g_tok, p_ngain = token_grad(tok, cot, gz, gx, weights[:2], wx, ngain)
     small, d_in, d_out = finish(

time: 433 us -> 345 us (0.80)
  waiting for transfers between devices: 160 us -> 82 us
  Pallas kernels: 213 us -> 204 us
    reduce_scatter x1, waiting for transfers between devices: 78.3 us -> 0.01 us  [per_device(): d_zo = lax.psum_scatter(d_zo, 'dp', scatter_dimension=0, tiled=True)]
    pallas_call x1, Pallas kernels: 37.2 us -> 28.4 us  [gate(): pl.pallas_call(gate_kernel, grid=(rows // tile,), in_specs=[pl.BlockSpec(...]
  transfers between devices with their start and end apart: 4 -> 4, of which waited for: 4 -> 3; matrix products, arithmetic and copies ran while one was open for 2% -> 6% of each run, Pallas kernels for 17% -> 46%
where the time goes in v4:
time: 345 us; the launch traced here: 344 us
  Pallas kernels  204 us (59%)
  waiting for transfers between devices  82 us (24%)
  matrix products  24.2 us (7%)
  between operations  14 us (4%)
  local copies, waits for them, and re-layouts  13.4 us (4%)
  other arithmetic  6.69 us (2%)
    pallas_call x1, Pallas kernels, state_backward(): pl.pallas_call(bwd_kernel, grid=(seqs, blocks), in_specs=[fixed(seg.shape...  83.8 us
    reduce_scatter x1, waiting for transfers between devices, per_device(): d_x = lax.psum_scatter(d_x, 'dp', scatter_dimension=0, tiled=True)  42.7 us
    pallas_call x1, Pallas kernels, state_forward(): pl.pallas_call(fwd_kernel, grid=(seqs, blocks), in_specs=[fixed(seg.shape...  41.5 us
    all_gather x1, waiting for transfers between devices, per_device(): wx = lax.all_gather(local_x, 'dp', axis=0, tiled=True)  39.1 us
    pallas_call x1, Pallas kernels, gate(): pl.pallas_call(gate_kernel, grid=(rows // tile,), in_specs=[pl.BlockSpec(...  28.4 us
    dot_general x3, matrix products, dot(): return lax.dot_general(a, b, dims, preferred_element_type=f32)  24.2 us
    pallas_call x1, Pallas kernels, token_grad(): pl.pallas_call(token_kernel, grid=(rows // tile,), in_specs=[pl.BlockSpec...  20 us
    pallas_call x1, Pallas kernels, finish(): pl.pallas_call(functools.partial(finish_kernel, steps, heads), in_specs=[...  17.4 us
  transfers between devices with their start and end apart: 4, of which 3 were waited for; matrix products, arithmetic and copies ran while one was open for 6% of the time, Pallas kernels for 46%

profile of v4, /device:TPU:0, one launch (start us, length us, event | category | flops | bytes accessed | tf_op | source)
XLA Modules:
  0.0 344.5 jit_solution(80480049864273973)
XLA Ops:
  7.2 0.0 all-gather.3.cloned.1.call-start
  7.2 0.9 slice.36
  8.2 0.7 pad.8
  8.9 0.0 all-gather.3.cloned.1.call-update
  8.9 0.0 all-gather.5.cloned.1.call-start
  8.9 0.9 fusion.1
  9.9 1.6 pad_maximum_fusion.1
  11.5 0.0 all-gather.5.cloned.1.call-update
  11.5 0.0 reduce-scatter.3.cloned.1.call-start
  11.6 1.3 reshape.62.gain_ref
  12.9 1.3 reshape.67.gain_ref
  14.2 1.3 reshape.64.cb_ref
  15.5 0.7 convert_element_type.16
  16.2 0.6 reshape.63.seg_ref
  16.8 0.7 negate_bitcast_fusion
  17.4 1.3 select_maximum_fusion.head_ref
  18.7 39.1 %all-gather.3.cloned.1.call-done.wx_ref = bf16[768,1920]{1,0:T(8,128)(2,1)} async-done(((bf16[48,1920]{1,0:T(8,128)(2,1)}), bf16[768,1920]{1,0:T(8,128)(2,1)}) %all-gather.3.cloned.1.call-update) | async-done | bytes 2949136 | tf_op jit(solution)/shard_map/all_gather | solution.py:720
  57.8 12.7 %project.1 = (bf16[2048,768]{1,0:T(8,128)(2,1)}, f32[2048,1792]{1,0:T(8,128)}, f32[2048,128]{1,0:T(8,128)}) custom-call(bf16[2048,768]{1,0:T(8,128)(2,1)} %bitcast.30, f32[1,768]{1,0:T(1,128)} %reshape.62.gain_ref, bf16[768,1920]{1,0:T(8,128)(2,1)} %all-gather.3.cloned.1.call-done.wx_ref), custom_call_target="tpu_custom_call" | custom-call | tf_op jit(solution)/shard_map/project/pallas_call | solution.py:82
  70.5 41.5 %state_forward.1 = (f32[2048,1536]{1,0:T(8,128)}, f32[2048,1792]{1,0:T(8,128)}, bf16[16,128,1536]{2,1,0:T(8,128)(2,1)}) custom-call(f32[16,128]{1,0:T(8,128)} %reshape.63.seg_ref, f32[2048,1792]{1,0:T(8,128)} %get-tuple-element.38.xbc_ref, f32[2048,128]{1,0:T(8,128)} %get-tuple-element.39.dt_ref, f32[4,1792]{1,0:T(4,128)} %cw_ref.3, ...), custom_call_target="tpu_custom_call" | custom-call | tf_op jit(solution)/shard_map/state_forward/pallas_call | solution.py:263
  112.0 0.1 all-gather.5.cloned.1.call-done
  112.2 28.4 %gate.1 = (bf16[2048,1536]{1,0:T(8,128)(2,1)}, bf16[2048,768]{1,0:T(8,128)(2,1)}, bf16[2048,1536]{1,0:T(8,128)(2,1)}, f32[2048,1536]{1,0:T(8,128)}, f32[8,1536]{1,0:T(8,128)}) custom-call(bf16[2048,768]{1,0:T(8,128)(2,1)} %bitcast.31, bf16[2048,768]{1,0:T(8,128)(2,1)} %get-tuple-element.37.normed_ref, f32[2048,1536]{1,0:T(8,128)} %get-tuple-element.40.y_ref, ...), custom_call_target="tpu_custom_call" | custom-call | tf_op jit(solution)/shard_map/gate/pallas_call | solution.py:347
  140.6 0.0 copy-start.11
  140.6 7.4 %convolution_convert_fusion.1 = bf16[1536,768]{1,0:T(8,128)(2,1)S(1)} fusion(bf16[2048,1536]{1,0:T(8,128)(2,1)} %get-tuple-element.45, bf16[2048,768]{1,0:T(8,128)(2,1)S(1)} %bitcast.36), kind=kOutput, calls=%fused_computation.2 | convolution fusion | flops 4833017856 | bytes 11796480 | tf_op jit(solution)/shard_map/dot_general | solution.py:26
  148.0 5.4 %convolution_convert_fusion.2 = bf16[768,1536]{1,0:T(8,128)(2,1)S(1)} fusion(bf16[2048,768]{1,0:T(8,128)(2,1)S(1)} %copy-done.11, bf16[2048,1536]{1,0:T(8,128)(2,1)S(1)} %copy-done.10), kind=kOutput, calls=%fused_computation.3 | convolution fusion | flops 4833017856 | bytes 11796480 | tf_op jit(solution)/shard_map/dot_general | solution.py:26
  153.5 0.2 fusion
  153.6 2.4 pad_maximum_fusion
  156.0 0.0 reduce-scatter.3.cloned.1.call-update
  156.1 0.2 reduce-scatter.5.cloned.1.call-start
  156.3 0.0 copy-start.12
  156.3 83.8 %state_backward.1 = (bf16[2048,1920]{1,0:T(8,128)(2,1)}, f32[32,1792]{1,0:T(8,128)}, f32[8,1792]{1,0:T(8,128)}, f32[8,1536]{1,0:T(8,128)}, f32[8,128]{1,0:T(8,128)}, /*index=5*/f32[8,128]{1,0:T(8,128)}) custom-call(f32[16,128]{1,0:T(8,128)} %reshape.63.seg_ref, f32[2048,1792]{1,0:T(8,128)} %get-tuple-element.38.xbc_ref, ...), custom_call_target="tpu_custom_call" | custom-call | tf_op jit(solution)/shard_map/state_backward/pallas_call | solution.py:532
  240.2 11.4 %convolution_convert_fusion = bf16[768,1920]{1,0:T(8,128)(2,1)} fusion(bf16[2048,768]{1,0:T(8,128)(2,1)S(1)} %copy-done.12, bf16[2048,1920]{1,0:T(8,128)(2,1)} %get-tuple-element.48.gx_ref), kind=kOutput, calls=%fused_computation.1 | convolution fusion | flops 6041272320 | bytes 13959168 | tf_op jit(solution)/shard_map/dot_general | solution.py:26
  251.5 0.0 reduce-scatter.5.cloned.1.call-update
  251.5 0.0 copy-start
  251.5 0.0 copy-start.1
  251.6 0.0 copy-start.3
  251.6 0.0 copy-start.7
  251.6 20.0 %token_grad.1 = (bf16[2048,768]{1,0:T(8,128)(2,1)}, f32[8,768]{1,0:T(8,128)}) custom-call(bf16[2048,768]{1,0:T(8,128)(2,1)} %bitcast.32, bf16[2048,768]{1,0:T(8,128)(2,1)} %bitcast.35, bf16[2048,1536]{1,0:T(8,128)(2,1)} %get-tuple-element.42.gz_ref, bf16[2048,1920]{1,0:T(8,128)(2,1)} %get-tuple-element.48.gx_ref, bf16[16,192,768]{2,1,0:T(8,128)(2,1)} %bitcast.28, ...), custom_call_target="tpu_custom_call" | custom-call | tf_op jit(solution)/shard_map/token_grad/pallas_call | solution.py:597
  271.6 42.7 %reduce-scatter.5.cloned.1.call-done.x_ref = bf16[48,1920]{1,0:T(8,128)(2,1)} async-done(((bf16[768,1920]{1,0:T(8,128)(2,1)}), bf16[48,1920]{1,0:T(8,128)(2,1)}) %reduce-scatter.5.cloned.1.call-update) | async-done | bytes 184336 | tf_op jit(solution)/shard_map/reduce_scatter | solution.py:749
  314.4 0.9 copy-done.2
  315.3 0.7 copy-done.6
  316.1 17.4 %finish.1 = (f32[8,1792]{1,0:T(8,128)S(1)}, f32[48,3352]{1,0:T(8,128)S(1)}, f32[96,768]{1,0:T(8,128)S(1)}) custom-call(f32[32,1792]{1,0:T(8,128)S(1)} %copy-done.1, f32[8,1792]{1,0:T(8,128)S(1)} %copy-done.3, f32[8,1536]{1,0:T(8,128)S(1)} %copy-done.4, f32[8,1536]{1,0:T(8,128)S(1)} %copy-done.5, f32[8,768]{1,0:T(8,128)S(1)} %copy-done.6, ...), custom_call_target="tpu_custom_call" | custom-call | tf_op jit(solution)/shard_map/finish/pallas_call | solution.py:680
  333.4 0.5 slice_bitcast_fusion
  333.9 0.6 slice_reduce_fusion.2
  334.6 0.6 slice_reduce_fusion.1
  335.2 0.6 slice_reduce_fusion
  335.8 0.6 slice.42
  336.4 0.8 copy.25
  337.2 0.7 copy.26
  (19 shorter events, 0.0 us)
Async XLA Ops:
  7.2 50.6 %all-gather.3.cloned.1.call-start = ((), (), s32[]{:S(2)}) async-start(), calls=%async_computation.2 | async-start | bytes 3133440 | tf_op jit(solution)/shard_map/all_gather | solution.py:720
  8.9 103.3 %all-gather.5.cloned.1.call-start = ((), (), s32[]{:S(2)}) async-start(), calls=%async_computation.3 | async-start | bytes 5013504 | tf_op jit(solution)/shard_map/all_gather | solution.py:722
  11.5 240.0 %reduce-scatter.3.cloned.1.call-start = ((), (), s32[]{:S(2)}) async-start(), calls=%async_computation.4 | async-start | bytes 5013504 | tf_op jit(solution)/shard_map/reduce_scatter | solution.py:745
  112.2 28.4 %copy-start.9 = (bf16[2,1024,768]{2,1,0:T(8,128)(2,1)S(1)}, bf16[2,1024,768]{2,1,0:T(8,128)(2,1)}, u32[]{:S(2)}) copy-start(bf16[2,1024,768]{2,1,0:T(8,128)(2,1)} %param.14) | copy-start | bytes 9437188
  140.6 7.4 %copy-start.10 = (bf16[2048,1536]{1,0:T(8,128)(2,1)S(1)}, bf16[2048,1536]{1,0:T(8,128)(2,1)}, u32[]{:S(2)}) copy-start(bf16[2048,1536]{1,0:T(8,128)(2,1)} %get-tuple-element.42.gz_ref) | copy-start | bytes 18874372
  140.6 7.4 %copy-start.11 = (bf16[2048,768]{1,0:T(8,128)(2,1)S(1)}, bf16[2048,768]{1,0:T(8,128)(2,1)}, u32[]{:S(2)}) copy-start(bf16[2048,768]{1,0:T(8,128)(2,1)} %get-tuple-element.37.normed_ref) | copy-start | bytes 9437188
  156.1 158.3 %reduce-scatter.5.cloned.1.call-start = ((), (), s32[]{:S(2)}) async-start(), calls=%async_computation.5 | async-start | bytes 3133440 | tf_op jit(solution)/shard_map/reduce_scatter | solution.py:749
  156.3 83.9 %copy-start.12 = (bf16[2048,768]{1,0:T(8,128)(2,1)S(1)}, bf16[2048,768]{1,0:T(8,128)(2,1)}, u32[]{:S(2)}) copy-start(bf16[2048,768]{1,0:T(8,128)(2,1)} %get-tuple-element.37.normed_ref) | copy-start | bytes 9437188
  251.5 62.8 %copy-start = (bf16[192,768]{1,0:T(8,128)(2,1)S(1)}, bf16[192,768]{1,0:T(8,128)(2,1)}, u32[]{:S(2)}) copy-start(bf16[192,768]{1,0:T(8,128)(2,1)} %reduce-scatter.3.cloned.1.call-done.zo_ref) | copy-start | bytes 884740
  251.5 62.8 %copy-start.1 = (f32[32,1792]{1,0:T(8,128)S(1)}, f32[32,1792]{1,0:T(8,128)}, u32[]{:S(2)}) copy-start(f32[32,1792]{1,0:T(8,128)} %get-tuple-element.50.cw_ref) | copy-start | bytes 688132
  251.6 62.8 %copy-start.3 = (f32[8,1792]{1,0:T(8,128)S(1)}, f32[8,1792]{1,0:T(8,128)}, u32[]{:S(2)}) copy-start(f32[8,1792]{1,0:T(8,128)} %get-tuple-element.51.cb_ref) | copy-start | bytes 172036
  251.6 62.8 %copy-start.4 = (f32[8,1536]{1,0:T(8,128)S(1)}, f32[8,1536]{1,0:T(8,128)}, u32[]{:S(2)}) copy-start(f32[8,1536]{1,0:T(8,128)} %get-tuple-element.52.ggain_ref) | copy-start | bytes 147460
  251.6 62.8 %copy-start.5 = (f32[8,1536]{1,0:T(8,128)S(1)}, f32[8,1536]{1,0:T(8,128)}, u32[]{:S(2)}) copy-start(f32[8,1536]{1,0:T(8,128)} %get-tuple-element.53.skip_ref) | copy-start | bytes 147460
  251.6 62.8 %copy-start.7 = (f32[8,128]{1,0:T(8,128)S(1)}, f32[8,128]{1,0:T(8,128)}, u32[]{:S(2)}) copy-start(f32[8,128]{1,0:T(8,128)} %get-tuple-element.55.alog_ref) | copy-start | bytes 12292
  251.6 62.8 %copy-start.8 = (f32[8,128]{1,0:T(8,128)S(1)}, f32[8,128]{1,0:T(8,128)}, u32[]{:S(2)}) copy-start(f32[8,128]{1,0:T(8,128)} %get-tuple-element.56.dtb_ref) | copy-start | bytes 12292
  314.4 0.9 copy-start.2
  315.3 0.7 copy-start.6
Sparse Core Ops, SparseCore 0:
  10.7 47.0 all-gather.2
  60.7 51.4 all-gather.4
  156.2 74.1 reduce-scatter.2
  251.7 62.6 reduce-scatter.4

commit v5 on v4

--- a/solution.py
+++ b/solution.py
@@ -611,75 +611,217 @@
     )(tok, cot, gz, gx, *[v for v, _ in weights], wx, gain)
 
 
-def partner(axis, bit):
-    me = lax.axis_index(axis)
-    return {axis: me + bit - 2 * bit * ((me // bit) % 2)}
+MESH = pl.DeviceIdType.MESH
+
+
+def place(line):
+    me = lax.axis_index("dp")
+    index = lambda l, x, c: (l * 2 + x) * 2 + c
+    return me // 4, (me // 2) % 2, me % 2, index, lax.axis_index("seq")
+
+
+def meet(devices):
+    barrier = pltpu.get_barrier_semaphore()
+    for device in devices:
+        pl.semaphore_signal(barrier, inc=1, device_id=device, device_id_type=MESH)
+    pl.semaphore_wait(barrier, len(devices))
+
+
+def remote(src, dst, send, recv, device):
+    return pltpu.make_async_remote_copy(
+        src_ref=src, dst_ref=dst, send_sem=send, recv_sem=recv, device_id=device, device_id_type=MESH
+    )
+
+
+def gather_kernel(line, own_ref, out_ref, line_send, x_send, y_send, core_send, recv, local):
+    l, x, c, index, y = place(line)
+    others = [{"dp": index((l + k) % line, x, c)} for k in range(1, line)]
+    beside, sibling, across = {"dp": index(l, 1 - x, c)}, {"dp": index(l, x, 1 - c)}, {"seq": 1 - y}
+    meet(others + [beside, sibling, across])
+    started = []
+
+    def send(src, at, sem, device):
+        copy = remote(src, out_ref.at[at], sem, recv.at[at], device)
+        copy.start()
+        started.append(copy)
+
+    def arrived(at):
+        remote(out_ref.at[at], out_ref.at[at], local.at[1], recv.at[at], sibling).wait_recv()
+
+    mine = pltpu.make_async_copy(own_ref, out_ref.at[l, x, c], local.at[0])
+    mine.start()
+    for k in range(1, line):
+        send(own_ref.at[y], (l, x, c, y), line_send.at[k], others[k - 1])
+    send(own_ref.at[y], (l, x, c, y), x_send.at[0], beside)
+    for h in range(2):
+        send(own_ref.at[h], (l, x, c, h), core_send.at[0, h], sibling)
+    for k in range(1, line):
+        at = ((l + k) % line, x, c, y)
+        arrived(at)
+        send(out_ref.at[at], at, x_send.at[k], beside)
+        send(out_ref.at[at], at, y_send.at[k], across)
+        send(out_ref.at[at], at, core_send.at[k, 0], sibling)
+    for k in range(line):
+        at = ((l + k) % line, 1 - x, c, y)
+        arrived(at)
+        send(out_ref.at[at], at, y_send.at[line + k], across)
+        send(out_ref.at[at], at, core_send.at[line + k, 0], sibling)
+    for k in range(1, line):
+        at = ((l + k) % line, x, c, 1 - y)
+        arrived(at)
+        send(out_ref.at[at], at, core_send.at[k, 1], sibling)
+    for k in range(line):
+        at = ((l + k) % line, 1 - x, c, 1 - y)
+        arrived(at)
+        send(out_ref.at[at], at, core_send.at[line + k, 1], sibling)
+    for k in range(line):
+        for side in range(2):
+            for h in range(2):
+                arrived(((l + k) % line, side, 1 - c, h))
+    for copy in started:
+        copy.wait_send()
+    mine.wait()
+
+
+def gather(local, owners):
+    own, columns = local.shape
+    line = owners // 4
+    vmem = pl.BlockSpec(memory_space=pltpu.VMEM)
+    dma = pltpu.SemaphoreType.DMA
+    out = pl.pallas_call(
+        functools.partial(gather_kernel, line),
+        in_specs=[vmem],
+        out_specs=vmem,
+        out_shape=jax.ShapeDtypeStruct((line, 2, 2, 2, own // 2, columns), local.dtype),
+        scratch_shapes=[
+            dma((line,)), dma((line,)), dma((2 * line,)), dma((2 * line, 2)), dma((line, 2, 2, 2)), dma((2,)),
+        ],
+        compiler_params=params(48 << 20, collective_id=1, has_side_effects=True),
+        name="gather",
+    )(local.reshape(2, own // 2, columns))
+    return out.reshape(owners * own, columns)
+
+
+def pack_small(acc, cw_ref, cb_ref, ggain_ref, skip_ref, ngain_ref, alog_ref, dtb_ref):
+    inner, width = ggain_ref.shape[1], ngain_ref.shape[1]
+    total = lambda v: jnp.sum(v, axis=0, keepdims=True)
+    acc[...] = jnp.zeros(acc.shape, f32)
+    for k in range(4):
+        acc[k : k + 1, :] = total(cw_ref[8 * k : 8 * k + 8, :])
+    acc[4:5, :] = total(cb_ref[...])
+    acc[5:6, :inner] = total(ggain_ref[...])
+    acc[6:7, :width] = total(ngain_ref[...])
+    acc[6:7, width : width + LANES] = total(alog_ref[...])
+    acc[6:7, width + LANES : width + 2 * LANES] = total(dtb_ref[...])
+    skip = jnp.concatenate(split(skip_ref[...], 3), axis=0)
+    by_head = ones_where(iota((inner, LANES), 0) // HEAD == iota((inner, LANES), 1))
+    acc[6:7, width + 2 * LANES : width + 3 * LANES] = total(dot(skip, by_head))
 
 
 def finish_kernel(
-    steps, heads, cw_ref, cb_ref, ggain_ref, skip_ref, ngain_ref, alog_ref, dtb_ref, zo_ref, x_ref,
-    small_ref, din_ref, dout_ref, acc, got, zo_got, x_got, send, recv, big_send, big_recv,
+    line, bits, cw_ref, cb_ref, ggain_ref, skip_ref, ngain_ref, alog_ref, dtb_ref, zo_ref, zo_got_ref, d_ref,
+    small_ref, din_ref, dout_ref,
+    acc, got, core_got, one, two_got, two, three_got, three, line_got, last, last_got,
+    small_send, small_recv, core_send, core_recv, two_send, two_recv, three_send, three_recv,
+    line_send, line_recv, last_sem,
 ):
-    if steps:
-        barrier = pltpu.get_barrier_semaphore()
-    for axis, bit in steps:
-        pl.semaphore_signal(barrier, inc=1, device_id=partner(axis, bit), device_id_type=pl.DeviceIdType.MESH)
-    if steps:
-        pl.semaphore_wait(barrier, len(steps))
-
-    def exchange(src, dst, ssem, rsem, axis, bit):
-        copy = pltpu.make_async_remote_copy(
-            src_ref=src, dst_ref=dst, send_sem=ssem, recv_sem=rsem,
-            device_id=partner(axis, bit), device_id_type=pl.DeviceIdType.MESH,
-        )
+    l, x, c, index, y = place(line)
+    me = lax.axis_index("dp")
+    doubling = [{"dp": me + bit - 2 * bit * ((me // bit) % 2)} for bit in bits]
+    others = [{"dp": index((l + k) % line, x, c)} for k in range(1, line)]
+    beside, sibling, across = {"dp": index(l, 1 - x, c)}, {"dp": index(l, x, 1 - c)}, {"seq": 1 - y}
+    meet(doubling + others + [beside, sibling, across])
+    order = list(range(1, line)) + [0]
+    at = [(l + k) % line for k in order]
+
+    def plus(a, b):
+        return a.astype(f32) + b.astype(f32)
+
+    def launch(*args):
+        copy = remote(*args)
         copy.start()
         return copy
 
-    big = []
-    for axis, bit in steps[-1:]:
-        big.append(exchange(zo_ref, zo_got, big_send.at[0], big_recv.at[0], axis, bit))
-        big.append(exchange(x_ref, x_got, big_send.at[1], big_recv.at[1], axis, bit))
-
-    inner, width = ggain_ref.shape[1], ngain_ref.shape[1]
-    channels = cb_ref.shape[1]
-    total = lambda v: jnp.sum(v, axis=0, keepdims=True)
-    acc[0] = jnp.zeros((8, channels), f32)
-    for k in range(4):
-        acc[0, k : k + 1, :] = total(cw_ref[8 * k : 8 * k + 8, :])
-    acc[0, 4:5, :] = total(cb_ref[...])
-    acc[0, 5:6, :inner] = total(ggain_ref[...])
-    acc[0, 6:7, :width] = total(ngain_ref[...])
-    acc[0, 6:7, width : width + LANES] = total(alog_ref[...])
-    acc[0, 6:7, width + LANES : width + 2 * LANES] = total(dtb_ref[...])
-    skip = jnp.concatenate(split(skip_ref[...], 3), axis=0)
-    by_head = ones_where(iota((inner, LANES), 0) // HEAD == iota((inner, LANES), 1))
-    acc[0, 6:7, width + 2 * LANES : width + 3 * LANES] = total(dot(skip, by_head))
-
-    for k, (axis, bit) in enumerate(steps):
-        exchange(acc.at[k], got.at[k], send.at[k], recv.at[k], axis, bit).wait()
-        acc[k + 1] = acc[k] + got[k]
-    small_ref[...] = acc[len(steps)]
-
-    for copy in big:
-        copy.wait()
-    own = din_ref.shape[0]
-    zo = zo_ref[...].astype(f32) + zo_got[...].astype(f32)
-    half = zo.shape[1]
+    first = []
+    for i in range(line):
+        first.append(
+            launch(d_ref.at[at[i], :, 1 - c], core_got.at[i], core_send.at[i], core_recv.at[i], sibling)
+        )
+    pack_small(acc.at[0], cw_ref, cb_ref, ggain_ref, skip_ref, ngain_ref, alog_ref, dtb_ref)
+    smalls = doubling + [across]
+    second, third, fourth = [], [], []
+
+    def small_start(k):
+        return launch(acc.at[k], got.at[k], small_send.at[k], small_recv.at[k], smalls[k])
+
+    for t in range(max(line + 2, len(smalls))):
+        small = small_start(t) if t < len(smalls) else None
+        if t < line:
+            i = t
+            first[i].wait()
+            for a in range(2):
+                for h in range(2):
+                    one[i, a, h] = plus(d_ref[at[i], a, c, h], core_got[i, a, h]).astype(bf16)
+            src, device = (one.at[i, 1 - x], beside) if i % 2 == 0 else (one.at[i, :, 1 - y], across)
+            second.append(launch(src, two_got.at[i], two_send.at[i], two_recv.at[i], device))
+        if 1 <= t <= line:
+            i = t - 1
+            second[i].wait()
+            for j in range(2):
+                kept = one[i, x, j] if i % 2 == 0 else one[i, j, y]
+                two[i, j] = plus(kept, two_got[i, j]).astype(bf16)
+            src, device = (two.at[i, 1 - y], across) if i % 2 == 0 else (two.at[i, 1 - x], beside)
+            third.append(launch(src, three_got.at[i], three_send.at[i], three_recv.at[i], device))
+        if 2 <= t <= line + 1:
+            i = t - 2
+            third[i].wait()
+            kept = two[i, y] if i % 2 == 0 else two[i, x]
+            three[i] = plus(kept, three_got[i]).astype(bf16)
+            if order[i] > 0:
+                fourth.append(
+                    launch(three.at[i], line_got.at[l], line_send.at[i], line_recv.at[l], others[order[i] - 1])
+                )
+        if small is not None:
+            small.wait()
+            acc[t + 1] = acc[t] + got[t]
+
+    small_ref[...] = acc[len(smalls)]
+    own, half = din_ref.shape[0], zo_ref.shape[1]
+    zo = plus(zo_ref[...], zo_got_ref[...])
     din_ref[:, :half] = zo[:own]
     din_ref[:, half : 2 * half] = zo[own : 2 * own]
     dout_ref[...] = zo[2 * own :]
+
+    total = three[line - 1].astype(f32)
+    for k in range(1, line):
+        at_k = (l + k) % line
+        remote(three.at[0], line_got.at[at_k], last_sem.at[2], line_recv.at[at_k], sibling).wait_recv()
+        total += line_got[at_k].astype(f32)
+    last[...] = total.astype(bf16)
+    final = launch(last, last_got, last_sem.at[0], last_sem.at[1], across)
+    for copy in fourth:
+        copy.wait_send()
+    final.wait()
     left = din_ref.shape[1] - 2 * half
-    din_ref[:, 2 * half :] = (x_ref[...].astype(f32) + x_got[...].astype(f32))[:, :left]
-
-
-def finish(p_cw, p_cb, p_ggain, p_skip, p_ngain, p_alog, p_dtb, d_zo, d_x, sizes, heads, proj):
-    steps = [(axis, 1 << i) for axis, n in sizes for i in range(n.bit_length() - 1)]
-    own, half = d_x.shape[0], d_zo.shape[1]
-    channels = p_cb.shape[1]
+    kept, came = last[...].astype(f32), last_got[...].astype(f32)
+    lower = (y == 0).astype(f32)
+    din_ref[: own // 2, 2 * half :] = (kept * lower + came * (1.0 - lower))[:, :left]
+    din_ref[own // 2 :, 2 * half :] = (came * lower + kept * (1.0 - lower))[:, :left]
+
+
+def finish(smalls, d_zo, zo_got, d_x, own, proj):
+    owners = d_x.shape[0] // own
+    line, columns, half = owners // 4, d_x.shape[1], d_zo.shape[1]
+    bits = [1 << i for i in range(owners.bit_length() - 1)]
+    channels = smalls[1].shape[1]
     vmem = pl.BlockSpec(memory_space=pltpu.VMEM)
+    dma = pltpu.SemaphoreType.DMA
+    piece = (own // 2, columns)
+    steps = len(bits) + 1
+    low = lambda *dims: pltpu.VMEM(dims + piece, bf16)
     return pl.pallas_call(
-        functools.partial(finish_kernel, steps, heads),
-        in_specs=[vmem] * 9,
+        functools.partial(finish_kernel, line, bits),
+        in_specs=[vmem] * 10,
         out_specs=[vmem] * 3,
         out_shape=[
             jax.ShapeDtypeStruct((8, channels), f32),
@@ -687,18 +829,28 @@
             jax.ShapeDtypeStruct((2 * own, half), f32),
         ],
         scratch_shapes=[
-            pltpu.VMEM((len(steps) + 1, 8, channels), f32),
-            pltpu.VMEM((max(len(steps), 1), 8, channels), f32),
-            pltpu.VMEM(d_zo.shape, bf16),
-            pltpu.VMEM(d_x.shape, bf16),
-            pltpu.SemaphoreType.DMA((max(len(steps), 1),)),
-            pltpu.SemaphoreType.DMA((max(len(steps), 1),)),
-            pltpu.SemaphoreType.DMA((2,)),
-            pltpu.SemaphoreType.DMA((2,)),
-        ],
-        compiler_params=params(48 << 20, collective_id=0 if steps else None, has_side_effects=True),
+            pltpu.VMEM((steps + 1, 8, channels), f32),
+            pltpu.VMEM((steps, 8, channels), f32),
+            low(line, 2, 2), low(line, 2, 2), low(line, 2), low(line, 2), low(line), low(line), low(line), low(), low(),
+            dma((steps,)), dma((steps,)),
+        ]
+        + [dma((line,))] * 8
+        + [dma((3,))],
+        compiler_params=params(48 << 20, collective_id=0, has_side_effects=True),
         name="finish",
-    )(p_cw, p_cb, p_ggain, p_skip, p_ngain, p_alog, p_dtb, d_zo, d_x)
+    )(*smalls, d_zo, zo_got, d_x.reshape(line, 2, 2, 2, own // 2, columns))
+
+
+def finish_plain(smalls, d_zo, d_x, own, proj):
+    cw, cb, ggain, skip, ngain, alog, dtb = (v.reshape(-1, 8, v.shape[1]).sum(1) for v in smalls)
+    skip = jnp.pad(skip.reshape(1, -1, HEAD).sum(2), ((0, 0), (0, LANES - skip.shape[1] // HEAD)))
+    tail = jnp.concatenate([ngain, alog, dtb, skip], axis=1)
+    wide = lambda v: jnp.pad(v, ((0, 0), (0, cb.shape[1] - v.shape[1])))
+    small = lax.psum(jnp.concatenate([cw, cb, wide(ggain), wide(tail)], axis=0), ("dp", "seq"))
+    d_x = lax.psum_scatter(d_x, "dp", scatter_dimension=0, tiled=True)
+    d_zo, d_x = lax.psum((d_zo.astype(f32), d_x.astype(f32)), "seq")
+    d_in = jnp.concatenate([d_zo[:own], d_zo[own : 2 * own], d_x], axis=1)[:, :proj]
+    return small, d_in, d_zo[2 * own :]
 
 
 def per_device(
@@ -717,7 +869,9 @@
     pad = LANES - heads
 
     local_x = jnp.pad(weight_in[:, inner:], ((0, 0), (0, pad)))
-    wx = lax.all_gather(local_x, "dp", axis=0, tiled=True)
+    owned = sizes["dp"] % 4 == 0 and sizes["seq"] == 2
+    wx = gather(local_x, owners) if owned else lax.all_gather(local_x, "dp", axis=0, tiled=True)
+    wx, weight_out = lax.optimization_barrier((wx, weight_out))
     local_zo = jnp.concatenate([weight_in[:, :width], weight_in[:, width:inner], weight_out], axis=0)
     slab = lax.all_gather(local_zo, "dp", axis=0, tiled=True).reshape(owners, 4 * own, width)
     weights = slab_views(slab, own)
@@ -745,12 +899,13 @@
     d_zo = lax.psum_scatter(d_zo, "dp", scatter_dimension=0, tiled=True)
     gx, p_cw, p_cb, p_skip, p_alog, p_dtb = state_backward(seg, xbc, dt, s, sin, gm, conv_weight, head, seqs)
     d_x = dot(normed, gx, TN).astype(bf16)
-    d_x, d_zo = lax.optimization_barrier((d_x, d_zo))
-    d_x = lax.psum_scatter(d_x, "dp", scatter_dimension=0, tiled=True)
     g_tok, p_ngain = token_grad(tok, cot, gz, gx, weights[:2], wx, ngain)
-    small, d_in, d_out = finish(
-        p_cw, p_cb, p_ggain, p_skip, p_ngain, p_alog, p_dtb, d_zo, d_x, sizes, heads, weight_in.shape[1]
-    )
+    smalls = (p_cw, p_cb, p_ggain, p_skip, p_ngain, p_alog, p_dtb)
+    if owned:
+        zo_got = lax.ppermute(d_zo, "seq", [(0, 1), (1, 0)])
+        small, d_in, d_out = finish(smalls, d_zo, zo_got, d_x, own, weight_in.shape[1])
+    else:
+        small, d_in, d_out = finish_plain(smalls, d_zo, d_x, own, weight_in.shape[1])
     return (
         out.reshape(tokens.shape),
         g_tok.reshape(tokens.shape),
@@ -771,7 +926,7 @@
     owned = P("dp", None)
     placed = (data, P(("dp", "seq"), None), data, P(), owned, P(), P(), P(), P(), P(), P(), owned)
     return jax.shard_map(
-        functools.partial(per_device, [(axis, mesh.shape[axis]) for axis in ("dp", "seq")]),
+        functools.partial(per_device, dict(mesh.shape)),
         mesh=mesh,
         in_specs=placed,
         out_specs=(data, data, P(), owned, P(), P(), P(), P(), P(), P(), owned),

time: 345 us -> 302 us (0.88)
  waiting for transfers between devices: 82 us -> 0.05 us
  Pallas kernels: 204 us -> 247 us
    pallas_call x1 -> x2, Pallas kernels: 17.4 us -> 60.6 us  [the longest x1 31.3 us: finish(): pl.pallas_call(functools.partial(finish_kernel, line, bits), in_specs=[vm...]
    reduce_scatter x1 -> x0, waiting for transfers between devices: 42.7 us -> none  [per_device(): d_x = lax.psum_scatter(d_x, 'dp', scatter_dimension=0, tiled=True)]
    all_gather x1 -> x0, waiting for transfers between devices: 39.1 us -> none  [per_device(): wx = lax.all_gather(local_x, 'dp', axis=0, tiled=True)]
  transfers between devices with their start and end apart: 4 -> 3, of which waited for: 3 -> 0; matrix products, arithmetic and copies ran while one was open for 6% -> 5% of each run, Pallas kernels for 46% -> 52%
where the time goes in v5:
time: 302 us
  Pallas kernels  247 us (82%)
  matrix products  23.5 us (8%)
  between operations  14.4 us (5%)
  local copies, waits for them, and re-layouts  11.5 us (4%)
  other arithmetic  4.66 us (2%)
    pallas_call x1, Pallas kernels, state_backward(): pl.pallas_call(bwd_kernel, grid=(seqs, blocks), in_specs=[fixed(seg.shape...  83.9 us
    pallas_call x1, Pallas kernels, state_forward(): pl.pallas_call(fwd_kernel, grid=(seqs, blocks), in_specs=[fixed(seg.shape...  41.5 us
    pallas_call x1, Pallas kernels, finish(): pl.pallas_call(functools.partial(finish_kernel, line, bits), in_specs=[vm...  31.3 us
    pallas_call x1, Pallas kernels, gather(): pl.pallas_call(functools.partial(gather_kernel, line), in_specs=[vmem], o...  29.3 us
    pallas_call x1, Pallas kernels, gate(): pl.pallas_call(gate_kernel, grid=(rows // tile,), in_specs=[pl.BlockSpec(...  28.4 us
    dot_general x3, matrix products, dot(): return lax.dot_general(a, b, dims, preferred_element_type=f32)  23.5 us
    pallas_call x1, Pallas kernels, token_grad(): pl.pallas_call(token_kernel, grid=(rows // tile,), in_specs=[pl.BlockSpec...  20 us
    pallas_call x1, Pallas kernels, project(): pl.pallas_call(proj_kernel, grid=(rows // tile,), in_specs=[pl.BlockSpec(...  12.7 us
  transfers between devices with their start and end apart: 3, of which 0 were waited for; matrix products, arithmetic and copies ran while one was open for 5% of the time, Pallas kernels for 52%

profile of v5, /device:TPU:0, one launch (start us, length us, event | category | flops | bytes accessed | tf_op | source)
XLA Modules:
  0.0 301.8 jit_solution(7752865682818074651)
XLA Ops:
  7.2 0.0 all-gather.2.cloned.1.call-start
  7.3 0.9 fusion.1
  8.2 0.9 slice.36
  9.2 0.0 copy-start.18
  9.2 0.0 copy-start.16
  9.2 0.0 copy-start.17
  9.2 29.3 %gather.1 = bf16[4,2,2,2,24,1920]{5,4,3,2,1,0:T(8,128)(2,1)S(1)} custom-call(bf16[2,24,1920]{2,1,0:T(8,128)(2,1)S(1)} %bitcast.31), custom_call_target="tpu_custom_call" | custom-call | tf_op jit(solution)/shard_map/gather/pallas_call | solution.py:691
  38.5 1.7 copy-done
  40.2 1.6 pad_maximum_fusion.1
  41.9 0.0 all-gather.2.cloned.1.call-update
  41.9 0.0 reduce-scatter.2.cloned.1.call-start
  41.9 0.6 reshape.71.gain_ref
  42.5 0.6 reshape.78.gain_ref
  43.1 0.0 copy-done.14
  43.1 0.6 reshape.75.cb_ref
  43.7 0.6 reshape.74.seg_ref
  44.3 12.7 %project.1 = (bf16[2048,768]{1,0:T(8,128)(2,1)}, f32[2048,1792]{1,0:T(8,128)}, f32[2048,128]{1,0:T(8,128)}) custom-call(bf16[2048,768]{1,0:T(8,128)(2,1)} %bitcast.37, f32[1,768]{1,0:T(1,128)} %reshape.71.gain_ref, bf16[768,1920]{1,0:T(8,128)(2,1)} %bitcast.28), custom_call_target="tpu_custom_call" | custom-call | tf_op jit(solution)/shard_map/project/pallas_call | solution.py:82
  57.1 0.0 copy-done.18
  57.1 0.6 select_maximum_fusion.head_ref
  57.7 41.5 %state_forward.1 = (f32[2048,1536]{1,0:T(8,128)}, f32[2048,1792]{1,0:T(8,128)}, bf16[16,128,1536]{2,1,0:T(8,128)(2,1)}) custom-call(f32[16,128]{1,0:T(8,128)} %reshape.74.seg_ref, f32[2048,1792]{1,0:T(8,128)} %get-tuple-element.39.xbc_ref, f32[2048,128]{1,0:T(8,128)} %get-tuple-element.40.dt_ref, f32[4,1792]{1,0:T(4,128)} %cw_ref.3, ...), custom_call_target="tpu_custom_call" | custom-call | tf_op jit(solution)/shard_map/state_forward/pallas_call | solution.py:263
  99.2 0.0 all-gather.2.cloned.1.call-done
  99.2 0.0 copy-start.9
  99.2 28.4 %gate.1 = (bf16[2048,1536]{1,0:T(8,128)(2,1)}, bf16[2048,768]{1,0:T(8,128)(2,1)}, bf16[2048,1536]{1,0:T(8,128)(2,1)}, f32[2048,1536]{1,0:T(8,128)}, f32[8,1536]{1,0:T(8,128)}) custom-call(bf16[2048,768]{1,0:T(8,128)(2,1)} %bitcast.38, bf16[2048,768]{1,0:T(8,128)(2,1)} %get-tuple-element.38.normed_ref, f32[2048,1536]{1,0:T(8,128)} %get-tuple-element.41.y_ref, ...), custom_call_target="tpu_custom_call" | custom-call | tf_op jit(solution)/shard_map/gate/pallas_call | solution.py:347
  127.6 0.0 copy-start.11
  127.6 7.4 %convolution_convert_fusion.1 = bf16[1536,768]{1,0:T(8,128)(2,1)S(1)} fusion(bf16[2048,1536]{1,0:T(8,128)(2,1)} %get-tuple-element.47, bf16[2048,768]{1,0:T(8,128)(2,1)S(1)} %bitcast.43), kind=kOutput, calls=%fused_computation.2 | convolution fusion | flops 4833017856 | bytes 11796480 | tf_op jit(solution)/shard_map/dot_general | solution.py:26
  135.0 5.4 %convolution_convert_fusion.2 = bf16[768,1536]{1,0:T(8,128)(2,1)S(1)} fusion(bf16[2048,768]{1,0:T(8,128)(2,1)S(1)} %copy-done.11, bf16[2048,1536]{1,0:T(8,128)(2,1)S(1)} %copy-done.10), kind=kOutput, calls=%fused_computation.3 | convolution fusion | flops 4833017856 | bytes 11796480 | tf_op jit(solution)/shard_map/dot_general | solution.py:26
  140.5 0.2 fusion
  140.7 2.4 pad_maximum_fusion
  143.1 0.0 reduce-scatter.2.cloned.1.call-update
  143.1 83.9 %state_backward.1 = (bf16[2048,1920]{1,0:T(8,128)(2,1)}, f32[32,1792]{1,0:T(8,128)}, f32[8,1792]{1,0:T(8,128)}, f32[8,1536]{1,0:T(8,128)}, f32[8,128]{1,0:T(8,128)}, /*index=5*/f32[8,128]{1,0:T(8,128)}) custom-call(f32[16,128]{1,0:T(8,128)} %reshape.74.seg_ref, f32[2048,1792]{1,0:T(8,128)} %get-tuple-element.39.xbc_ref, ...), custom_call_target="tpu_custom_call" | custom-call | tf_op jit(solution)/shard_map/state_backward/pallas_call | solution.py:532
  226.9 0.0 reduce-scatter.2.cloned.1.call-done.zo_ref
  227.0 0.5 collective-permute-start
  227.5 10.7 %convolution_convert_fusion = bf16[768,1920]{1,0:T(8,128)(2,1)S(1)} fusion(bf16[2048,768]{1,0:T(8,128)(2,1)} %get-tuple-element.38.normed_ref, bf16[2048,1920]{1,0:T(8,128)(2,1)} %get-tuple-element.50.gx_ref), kind=kOutput, calls=%fused_computation.1 | convolution fusion | flops 6041272320 | bytes 13959168 | tf_op jit(solution)/shard_map/dot_general | solution.py:26
  238.2 0.0 copy-start.2
  238.2 0.0 copy-start.3
  238.2 0.0 copy-start.7
  238.2 20.0 %token_grad.1 = (bf16[2048,768]{1,0:T(8,128)(2,1)}, f32[8,768]{1,0:T(8,128)}) custom-call(bf16[2048,768]{1,0:T(8,128)(2,1)} %bitcast.39, bf16[2048,768]{1,0:T(8,128)(2,1)} %bitcast.42, bf16[2048,1536]{1,0:T(8,128)(2,1)} %get-tuple-element.44.gz_ref, bf16[2048,1920]{1,0:T(8,128)(2,1)} %get-tuple-element.50.gx_ref, bf16[16,192,768]{2,1,0:T(8,128)(2,1)} %bitcast.35, ...), custom_call_target="tpu_custom_call" | custom-call | tf_op jit(solution)/shard_map/token_grad/pallas_call | solution.py:597
  258.3 0.0 collective-permute-done.zo_got_ref
  258.3 0.0 copy-start.6
  258.4 0.7 copy-done.6
  259.1 31.3 %finish.1 = (f32[8,1792]{1,0:T(8,128)S(1)}, f32[48,3352]{1,0:T(8,128)S(1)}, f32[96,768]{1,0:T(8,128)S(1)}) custom-call(f32[32,1792]{1,0:T(8,128)S(1)} %copy-done.2, f32[8,1792]{1,0:T(8,128)S(1)} %copy-done.3, f32[8,1536]{1,0:T(8,128)S(1)} %copy-done.4, f32[8,1536]{1,0:T(8,128)S(1)} %copy-done.5, f32[8,768]{1,0:T(8,128)S(1)} %copy-done.6, ...), custom_call_target="tpu_custom_call" | custom-call | tf_op jit(solution)/shard_map/finish/pallas_call | solution.py:822
  290.4 0.5 slice_bitcast_fusion
  290.9 0.6 slice_reduce_fusion.2
  291.6 0.6 slice_reduce_fusion.1
  292.2 0.6 slice_reduce_fusion
  292.8 0.6 slice.42
  293.4 0.8 copy.25
  294.2 0.7 copy.26
  (28 shorter events, 0.1 us)
Async XLA Ops:
  7.2 34.8 %copy-start.15 = (f32[768]{0:T(1024)S(1)}, f32[768]{0:T(1024)}, u32[]{:S(2)}) copy-start(f32[768]{0:T(1024)} %param.15) | copy-start | bytes 9220
  7.2 35.3 %copy-start.12 = (f32[1536]{0:T(1024)S(1)}, f32[1536]{0:T(1024)}, u32[]{:S(2)}) copy-start(f32[1536]{0:T(1024)} %param.22) | copy-start | bytes 18436
  7.2 35.9 %copy-start.14 = (f32[1792]{0:T(1024)S(1)}, f32[1792]{0:T(1024)}, u32[]{:S(2)}) copy-start(f32[1792]{0:T(1024)} %param.18) | copy-start | bytes 21508
  7.2 36.5 %copy-start.13 = (s32[2,1024]{1,0:T(2,128)S(1)}, s32[2,1024]{1,0:T(2,128)}, u32[]{:S(2)}) copy-start(s32[2,1024]{1,0:T(2,128)} %param.13) | copy-start | bytes 24580
  7.2 92.0 %all-gather.2.cloned.1.call-start = ((), (), s32[]{:S(2)}) async-start(), calls=%async_computation.1 | async-start | bytes 5013504 | tf_op jit(solution)/shard_map/all_gather | solution.py:876
  9.2 47.9 %copy-start.18 = (f32[24]{0:T(128)S(1)}, f32[24]{0:T(128)}, u32[]{:S(2)}) copy-start(f32[24]{0:T(128)} %param.20) | copy-start | bytes 292
  9.2 47.9 %copy-start.16 = (f32[24]{0:T(128)S(1)}, f32[24]{0:T(128)}, u32[]{:S(2)}) copy-start(f32[24]{0:T(128)} %param.21) | copy-start | bytes 292
  9.2 47.9 %copy-start.17 = (f32[24]{0:T(128)S(1)}, f32[24]{0:T(128)}, u32[]{:S(2)}) copy-start(f32[24]{0:T(128)} %param.19) | copy-start | bytes 292
  38.5 1.7 copy-start
  41.9 185.1 %reduce-scatter.2.cloned.1.call-start = ((), (), s32[]{:S(2)}) async-start(), calls=%async_computation.2 | async-start | bytes 5013504 | tf_op jit(solution)/shard_map/reduce_scatter | solution.py:899
  99.2 28.4 %copy-start.9 = (bf16[2,1024,768]{2,1,0:T(8,128)(2,1)S(1)}, bf16[2,1024,768]{2,1,0:T(8,128)(2,1)}, u32[]{:S(2)}) copy-start(bf16[2,1024,768]{2,1,0:T(8,128)(2,1)} %param.14) | copy-start | bytes 9437188
  127.6 7.4 %copy-start.10 = (bf16[2048,1536]{1,0:T(8,128)(2,1)S(1)}, bf16[2048,1536]{1,0:T(8,128)(2,1)}, u32[]{:S(2)}) copy-start(bf16[2048,1536]{1,0:T(8,128)(2,1)} %get-tuple-element.44.gz_ref) | copy-start | bytes 18874372
  127.6 7.4 %copy-start.11 = (bf16[2048,768]{1,0:T(8,128)(2,1)S(1)}, bf16[2048,768]{1,0:T(8,128)(2,1)}, u32[]{:S(2)}) copy-start(bf16[2048,768]{1,0:T(8,128)(2,1)} %get-tuple-element.38.normed_ref) | copy-start | bytes 9437188
  227.0 31.3 %collective-permute-start = (bf16[192,768]{1,0:T(8,128)(2,1)}, bf16[192,768]{1,0:T(8,128)(2,1)S(1)}, u32[]{:S(2)}, u32[]{:S(2)}) collective-permute-start(bf16[192,768]{1,0:T(8,128)(2,1)} %reduce-scatter.2.cloned.1.call-done.zo_ref), channel_id=1, source_target_pairs={{0,1},{1,0},{2,3},{3,2},{4,5},{5,4},{6,7},{7,6},{8,9},{9,8},{10,11... | collective-permute-start | bytes 884744 | tf_op jit(solution)/shard_map/ppermute | solution.py:905
  238.2 20.1 %copy-start.1 = (bf16[192,768]{1,0:T(8,128)(2,1)S(1)}, bf16[192,768]{1,0:T(8,128)(2,1)}, u32[]{:S(2)}) copy-start(bf16[192,768]{1,0:T(8,128)(2,1)} %reduce-scatter.2.cloned.1.call-done.zo_ref) | copy-start | bytes 884740
  238.2 20.1 %copy-start.2 = (f32[32,1792]{1,0:T(8,128)S(1)}, f32[32,1792]{1,0:T(8,128)}, u32[]{:S(2)}) copy-start(f32[32,1792]{1,0:T(8,128)} %get-tuple-element.52.cw_ref) | copy-start | bytes 688132
  238.2 20.1 %copy-start.3 = (f32[8,1792]{1,0:T(8,128)S(1)}, f32[8,1792]{1,0:T(8,128)}, u32[]{:S(2)}) copy-start(f32[8,1792]{1,0:T(8,128)} %get-tuple-element.53.cb_ref) | copy-start | bytes 172036
  238.2 20.1 %copy-start.4 = (f32[8,1536]{1,0:T(8,128)S(1)}, f32[8,1536]{1,0:T(8,128)}, u32[]{:S(2)}) copy-start(f32[8,1536]{1,0:T(8,128)} %get-tuple-element.54.ggain_ref) | copy-start | bytes 147460
  238.2 20.1 %copy-start.5 = (f32[8,1536]{1,0:T(8,128)S(1)}, f32[8,1536]{1,0:T(8,128)}, u32[]{:S(2)}) copy-start(f32[8,1536]{1,0:T(8,128)} %get-tuple-element.55.skip_ref) | copy-start | bytes 147460
  238.2 20.1 %copy-start.7 = (f32[8,128]{1,0:T(8,128)S(1)}, f32[8,128]{1,0:T(8,128)}, u32[]{:S(2)}) copy-start(f32[8,128]{1,0:T(8,128)} %get-tuple-element.57.alog_ref) | copy-start | bytes 12292
  238.2 20.1 %copy-start.8 = (f32[8,128]{1,0:T(8,128)S(1)}, f32[8,128]{1,0:T(8,128)}, u32[]{:S(2)}) copy-start(f32[8,128]{1,0:T(8,128)} %get-tuple-element.58.dtb_ref) | copy-start | bytes 12292
  258.3 0.7 copy-start.6
Sparse Core Ops, SparseCore 0:
  42.0 52.7 all-gather.1
  143.2 75.2 reduce-scatter.1

commit v6 on v5

--- a/solution.py
+++ b/solution.py
@@ -702,15 +702,14 @@
     return out.reshape(owners * own, columns)
 
 
-def pack_small(acc, cw_ref, cb_ref, ggain_ref, skip_ref, ngain_ref, alog_ref, dtb_ref):
-    inner, width = ggain_ref.shape[1], ngain_ref.shape[1]
+def pack_small(acc, width, cw_ref, cb_ref, ggain_ref, skip_ref, alog_ref, dtb_ref):
+    inner = ggain_ref.shape[1]
     total = lambda v: jnp.sum(v, axis=0, keepdims=True)
     acc[...] = jnp.zeros(acc.shape, f32)
     for k in range(4):
         acc[k : k + 1, :] = total(cw_ref[8 * k : 8 * k + 8, :])
     acc[4:5, :] = total(cb_ref[...])
     acc[5:6, :inner] = total(ggain_ref[...])
-    acc[6:7, :width] = total(ngain_ref[...])
     acc[6:7, width : width + LANES] = total(alog_ref[...])
     acc[6:7, width + LANES : width + 2 * LANES] = total(dtb_ref[...])
     skip = jnp.concatenate(split(skip_ref[...], 3), axis=0)
@@ -719,130 +718,225 @@
 
 
 def finish_kernel(
-    line, bits, cw_ref, cb_ref, ggain_ref, skip_ref, ngain_ref, alog_ref, dtb_ref, zo_ref, zo_got_ref, d_ref,
-    small_ref, din_ref, dout_ref,
-    acc, got, core_got, one, two_got, two, three_got, three, line_got, last, last_got,
-    small_send, small_recv, core_send, core_recv, two_send, two_recv, three_send, three_recv,
-    line_send, line_recv, last_sem,
+    line, bits, tile, starts, own,
+    cw_ref, cb_ref, ggain_ref, skip_ref, alog_ref, dtb_ref, zo_ref, zo_got_ref, d_ref, gain_ref,
+    tok_ref, cot_ref, gz_ref, gx_ref, wa_ref, wb_ref, wx_ref,
+    small_ref, din_ref, dout_ref, gtok_ref,
+    acc, got, gain_acc, gain_got, core_got, one, two_got, two, three_got, three, line_got, last, last_got,
+    tok, cot, gz, gx, wa, wb, wx, gtok, gain_rows,
+    small_send, small_recv, gain_send, gain_recv, core_send, core_recv, two_send, two_recv,
+    three_send, three_recv, line_send, line_recv, last_sem, tile_sem, out_sem, weight_sem,
 ):
     l, x, c, index, y = place(line)
     me = lax.axis_index("dp")
     doubling = [{"dp": me + bit - 2 * bit * ((me // bit) % 2)} for bit in bits]
     others = [{"dp": index((l + k) % line, x, c)} for k in range(1, line)]
     beside, sibling, across = {"dp": index(l, 1 - x, c)}, {"dp": index(l, x, 1 - c)}, {"seq": 1 - y}
-    meet(doubling + others + [beside, sibling, across])
     order = list(range(1, line)) + [0]
     at = [(l + k) % line for k in order]
+    tiles = tok.shape[0]
+    width = gain_ref.shape[1]
+
+    def fetches(i):
+        rows = pl.ds(pl.multiple_of(i * tile, tile), tile)
+        pairs = ((tok_ref, tok), (cot_ref, cot), (gz_ref, gz), (gx_ref, gx))
+        return [pltpu.make_async_copy(src.at[rows], dst.at[i], tile_sem.at[i, n]) for n, (src, dst) in enumerate(pairs)]
+
+    def stored(i):
+        rows = pl.ds(pl.multiple_of(i * tile, tile), tile)
+        return pltpu.make_async_copy(gtok.at[i], gtok_ref.at[rows], out_sem.at[i])
+
+    weights = [
+        pltpu.make_async_copy(src.at[:, pl.ds(start, dst.shape[1])], dst, weight_sem.at[n])
+        for n, (src, dst, start) in enumerate(((wa_ref, wa, starts[0]), (wb_ref, wb, starts[1])))
+    ] + [pltpu.make_async_copy(wx_ref, wx, weight_sem.at[2])]
+    for copy in weights:
+        copy.start()
+    for i in range(tiles):
+        for copy in fetches(i):
+            copy.start()
+
+    meet(doubling + others + [beside, sibling, across])
 
     def plus(a, b):
         return a.astype(f32) + b.astype(f32)
 
-    def launch(*args):
-        copy = remote(*args)
-        copy.start()
-        return copy
-
-    first = []
+    smalls = doubling + [across]
+
+    def first(i):
+        return remote(d_ref.at[at[i], :, 1 - c], core_got.at[i], core_send.at[i], core_recv.at[i], sibling)
+
+    def second(i):
+        src, device = (one.at[i, 1 - x], beside) if i % 2 == 0 else (one.at[i, :, 1 - y], across)
+        return remote(src, two_got.at[i], two_send.at[i], two_recv.at[i], device)
+
+    def third(i):
+        src, device = (two.at[i, 1 - y], across) if i % 2 == 0 else (two.at[i, 1 - x], beside)
+        return remote(src, three_got.at[i], three_send.at[i], three_recv.at[i], device)
+
+    def fourth(i):
+        return remote(three.at[i], line_got.at[l], line_send.at[i], line_recv.at[l], others[order[i] - 1])
+
+    def small(k):
+        return remote(acc.at[k], got.at[k], small_send.at[k], small_recv.at[k], smalls[k])
+
+    def gains(k):
+        return remote(gain_acc.at[k], gain_got.at[k], gain_send.at[k], gain_recv.at[k], smalls[k])
+
+    def after_first(i):
+        first(i).wait()
+        for a in range(2):
+            for h in range(2):
+                one[i, a, h] = plus(d_ref[at[i], a, c, h], core_got[i, a, h]).astype(bf16)
+        second(i).start()
+
+    def after_second(i):
+        second(i).wait()
+        for j in range(2):
+            kept = one[i, x, j] if i % 2 == 0 else one[i, j, y]
+            two[i, j] = plus(kept, two_got[i, j]).astype(bf16)
+        third(i).start()
+
+    def after_third(i):
+        third(i).wait()
+        kept = two[i, y] if i % 2 == 0 else two[i, x]
+        three[i] = plus(kept, three_got[i]).astype(bf16)
+        if order[i] > 0:
+            fourth(i).start()
+
+    def after_small(k):
+        small(k).wait()
+        acc[k + 1] = acc[k] + got[k]
+        if k + 1 < len(smalls):
+            small(k + 1).start()
+
+    plan = [[] for _ in range(tiles)]
     for i in range(line):
-        first.append(
-            launch(d_ref.at[at[i], :, 1 - c], core_got.at[i], core_send.at[i], core_recv.at[i], sibling)
-        )
-    pack_small(acc.at[0], cw_ref, cb_ref, ggain_ref, skip_ref, ngain_ref, alog_ref, dtb_ref)
-    smalls = doubling + [across]
-    second, third, fourth = [], [], []
-
-    def small_start(k):
-        return launch(acc.at[k], got.at[k], small_send.at[k], small_recv.at[k], smalls[k])
-
-    for t in range(max(line + 2, len(smalls))):
-        small = small_start(t) if t < len(smalls) else None
-        if t < line:
-            i = t
-            first[i].wait()
-            for a in range(2):
-                for h in range(2):
-                    one[i, a, h] = plus(d_ref[at[i], a, c, h], core_got[i, a, h]).astype(bf16)
-            src, device = (one.at[i, 1 - x], beside) if i % 2 == 0 else (one.at[i, :, 1 - y], across)
-            second.append(launch(src, two_got.at[i], two_send.at[i], two_recv.at[i], device))
-        if 1 <= t <= line:
-            i = t - 1
-            second[i].wait()
-            for j in range(2):
-                kept = one[i, x, j] if i % 2 == 0 else one[i, j, y]
-                two[i, j] = plus(kept, two_got[i, j]).astype(bf16)
-            src, device = (two.at[i, 1 - y], across) if i % 2 == 0 else (two.at[i, 1 - x], beside)
-            third.append(launch(src, three_got.at[i], three_send.at[i], three_recv.at[i], device))
-        if 2 <= t <= line + 1:
-            i = t - 2
-            third[i].wait()
-            kept = two[i, y] if i % 2 == 0 else two[i, x]
-            three[i] = plus(kept, three_got[i]).astype(bf16)
-            if order[i] > 0:
-                fourth.append(
-                    launch(three.at[i], line_got.at[l], line_send.at[i], line_recv.at[l], others[order[i] - 1])
-                )
-        if small is not None:
-            small.wait()
-            acc[t + 1] = acc[t] + got[t]
-
-    small_ref[...] = acc[len(smalls)]
-    own, half = din_ref.shape[0], zo_ref.shape[1]
-    zo = plus(zo_ref[...], zo_got_ref[...])
-    din_ref[:, :half] = zo[:own]
-    din_ref[:, half : 2 * half] = zo[own : 2 * own]
-    dout_ref[...] = zo[2 * own :]
-
+        plan[min(i * 2 // line, tiles - 1)].append((after_first, i))
+    for i in range(line):
+        plan[min(2 + i * 3 // line, tiles - 1)].append((after_second, i))
+    for i in range(line):
+        plan[min(4 + i * 4 // line, tiles - 1)].append((after_third, i))
+    for k in range(len(smalls)):
+        plan[min(k + 1, tiles - 1)].append((after_small, k))
+
+    for i in range(line):
+        first(i).start()
+    pack_small(acc.at[0], width, cw_ref, cb_ref, ggain_ref, skip_ref, alog_ref, dtb_ref)
+    small(0).start()
+    gain_rows[...] = jnp.zeros_like(gain_rows)
+    for copy in weights:
+        copy.wait()
+    half = zo_ref.shape[1]
+
+    @pl.loop(0, tiles)
+    def _(i):
+        for t, work in enumerate(plan):
+            if work:
+
+                @pl.when(i == t)
+                def _():
+                    for step, n in work:
+                        step(n)
+
+        for copy in fetches(i):
+            copy.wait()
+        g = dot(gz[i, :, :half], flat(wa), NT) + dot(gz[i, :, half:], flat(wb), NT)
+        g += dot(gx[i], wx[...], NT)
+        u = tok[i].astype(f32)
+        r = lax.rsqrt(jnp.mean(u * u, axis=-1, keepdims=True) + EPS)
+        unit = u * r
+        gain_rows[...] += fold_rows(unit * g)
+        q = g * gain_ref[...]
+        mean = jnp.mean(unit * q, axis=-1, keepdims=True)
+        gtok[i] = (cot[i].astype(f32) + r * (q - unit * mean)).astype(bf16)
+        stored(i).start()
+
+    gain_acc[0] = jnp.sum(gain_rows[...], axis=0, keepdims=True)
+    gains(0).start()
     total = three[line - 1].astype(f32)
     for k in range(1, line):
         at_k = (l + k) % line
         remote(three.at[0], line_got.at[at_k], last_sem.at[2], line_recv.at[at_k], sibling).wait_recv()
         total += line_got[at_k].astype(f32)
     last[...] = total.astype(bf16)
-    final = launch(last, last_got, last_sem.at[0], last_sem.at[1], across)
-    for copy in fourth:
-        copy.wait_send()
+    final = remote(last, last_got, last_sem.at[0], last_sem.at[1], across)
+    final.start()
+
+    zo = plus(zo_ref[...], zo_got_ref[...])
+    din_ref[:, :half] = zo[:own]
+    din_ref[:, half : 2 * half] = zo[own : 2 * own]
+    dout_ref[...] = zo[2 * own :]
+    for k in range(len(smalls)):
+        gains(k).wait()
+        gain_acc[k + 1] = gain_acc[k] + gain_got[k]
+        if k + 1 < len(smalls):
+            gains(k + 1).start()
+    small_ref[...] = acc[len(smalls)]
+    small_ref[6:7, :width] = gain_acc[len(smalls)]
+
+    for i in range(line):
+        if order[i] > 0:
+            fourth(i).wait_send()
     final.wait()
     left = din_ref.shape[1] - 2 * half
     kept, came = last[...].astype(f32), last_got[...].astype(f32)
     lower = (y == 0).astype(f32)
     din_ref[: own // 2, 2 * half :] = (kept * lower + came * (1.0 - lower))[:, :left]
     din_ref[own // 2 :, 2 * half :] = (came * lower + kept * (1.0 - lower))[:, :left]
-
-
-def finish(smalls, d_zo, zo_got, d_x, own, proj):
+    for i in range(tiles):
+        stored(i).wait()
+
+
+def finish(smalls, d_zo, zo_got, d_x, own, proj, gain, tok, cot, gz, gx, weights, wx, tile=256):
     owners = d_x.shape[0] // own
     line, columns, half = owners // 4, d_x.shape[1], d_zo.shape[1]
     bits = [1 << i for i in range(owners.bit_length() - 1)]
     channels = smalls[1].shape[1]
+    rows, width = tok.shape
+    tiles = rows // tile
     vmem = pl.BlockSpec(memory_space=pltpu.VMEM)
+    away = pl.BlockSpec(memory_space=pl.ANY)
     dma = pltpu.SemaphoreType.DMA
     piece = (own // 2, columns)
     steps = len(bits) + 1
     low = lambda *dims: pltpu.VMEM(dims + piece, bf16)
+    held = lambda *dims: pltpu.VMEM(dims, bf16)
+    shared = own % 16 == 0
+    arrays = [v for v, _ in weights]
+    part = (owners, own, half) if shared else arrays[0].shape
     return pl.pallas_call(
-        functools.partial(finish_kernel, line, bits),
-        in_specs=[vmem] * 10,
-        out_specs=[vmem] * 3,
+        functools.partial(finish_kernel, line, bits, tile, (0, own) if shared else (0, 0), own),
+        in_specs=[vmem] * 10 + [away] * 7,
+        out_specs=[vmem] * 3 + [away],
         out_shape=[
             jax.ShapeDtypeStruct((8, channels), f32),
             jax.ShapeDtypeStruct((own, proj), f32),
             jax.ShapeDtypeStruct((2 * own, half), f32),
+            jax.ShapeDtypeStruct((rows, width), bf16),
         ],
         scratch_shapes=[
             pltpu.VMEM((steps + 1, 8, channels), f32),
             pltpu.VMEM((steps, 8, channels), f32),
+            pltpu.VMEM((steps + 1, 1, width), f32),
+            pltpu.VMEM((steps, 1, width), f32),
             low(line, 2, 2), low(line, 2, 2), low(line, 2), low(line, 2), low(line), low(line), low(line), low(), low(),
-            dma((steps,)), dma((steps,)),
+            held(tiles, tile, width), held(tiles, tile, width), held(tiles, tile, gz.shape[1]),
+            held(tiles, tile, columns), held(*part), held(*part), held(*wx.shape), held(tiles, tile, width),
+            pltpu.VMEM((8, width), f32),
+            dma((steps,)), dma((steps,)), dma((steps,)), dma((steps,)),
         ]
         + [dma((line,))] * 8
-        + [dma((3,))],
-        compiler_params=params(48 << 20, collective_id=0, has_side_effects=True),
+        + [dma((3,)), dma((tiles, 4)), dma((tiles,)), dma((3,))],
+        compiler_params=params(64000 << 10, collective_id=0, has_side_effects=True),
         name="finish",
-    )(*smalls, d_zo, zo_got, d_x.reshape(line, 2, 2, 2, own // 2, columns))
+    )(
+        *smalls, d_zo, zo_got, d_x.reshape(line, 2, 2, 2, own // 2, columns), gain, tok, cot, gz, gx, *arrays, wx
+    )
 
 
 def finish_plain(smalls, d_zo, d_x, own, proj):
-    cw, cb, ggain, skip, ngain, alog, dtb = (v.reshape(-1, 8, v.shape[1]).sum(1) for v in smalls)
+    cw, cb, ggain, skip, alog, dtb, ngain = (v.reshape(-1, 8, v.shape[1]).sum(1) for v in smalls)
     skip = jnp.pad(skip.reshape(1, -1, HEAD).sum(2), ((0, 0), (0, LANES - skip.shape[1] // HEAD)))
     tail = jnp.concatenate([ngain, alog, dtb, skip], axis=1)
     wide = lambda v: jnp.pad(v, ((0, 0), (0, cb.shape[1] - v.shape[1])))
@@ -899,13 +993,15 @@
     d_zo = lax.psum_scatter(d_zo, "dp", scatter_dimension=0, tiled=True)
     gx, p_cw, p_cb, p_skip, p_alog, p_dtb = state_backward(seg, xbc, dt, s, sin, gm, conv_weight, head, seqs)
     d_x = dot(normed, gx, TN).astype(bf16)
-    g_tok, p_ngain = token_grad(tok, cot, gz, gx, weights[:2], wx, ngain)
-    smalls = (p_cw, p_cb, p_ggain, p_skip, p_ngain, p_alog, p_dtb)
+    smalls = (p_cw, p_cb, p_ggain, p_skip, p_alog, p_dtb)
     if owned:
         zo_got = lax.ppermute(d_zo, "seq", [(0, 1), (1, 0)])
-        small, d_in, d_out = finish(smalls, d_zo, zo_got, d_x, own, weight_in.shape[1])
+        small, d_in, d_out, g_tok = finish(
+            smalls, d_zo, zo_got, d_x, own, weight_in.shape[1], ngain, tok, cot, gz, gx, weights[:2], wx
+        )
     else:
-        small, d_in, d_out = finish_plain(smalls, d_zo, d_x, own, weight_in.shape[1])
+        g_tok, p_ngain = token_grad(tok, cot, gz, gx, weights[:2], wx, ngain)
+        small, d_in, d_out = finish_plain(smalls + (p_ngain,), d_zo, d_x, own, weight_in.shape[1])
     return (
         out.reshape(tokens.shape),
         g_tok.reshape(tokens.shape),

time: 302 us -> 313 us (1.036)
  local copies, waits for them, and re-layouts: 11.5 us -> 19.2 us
    unnamed x40 -> x33, local copies, waits for them, and re-layouts: 4.11 us -> 7.86 us
    pallas_call x2 -> x1, Pallas kernels: 51.4 us -> 53.7 us  [finish(): pl.pallas_call(functools.partial(finish_kernel, line, bits, tile, (0, own...]
  transfers between devices with their start and end apart: 3 -> 3, of which waited for: 0 -> 0; matrix products, arithmetic and copies ran while one was open for 5% -> 5% of each run, Pallas kernels for 52% -> 44%
where the time goes in v6:
time: 313 us
  Pallas kernels  250 us (80%)
  matrix products  24.2 us (8%)
  local copies, waits for them, and re-layouts  19.2 us (6%)
  between operations  14.3 us (5%)
  other arithmetic  4.67 us (1%)
    pallas_call x1, Pallas kernels, state_backward(): pl.pallas_call(bwd_kernel, grid=(seqs, blocks), in_specs=[fixed(seg.shape...  84 us
    pallas_call x1, Pallas kernels, finish(): pl.pallas_call(functools.partial(finish_kernel, line, bits, tile, (0, own...  53.7 us
    pallas_call x1, Pallas kernels, state_forward(): pl.pallas_call(fwd_kernel, grid=(seqs, blocks), in_specs=[fixed(seg.shape...  41.5 us
    pallas_call x1, Pallas kernels, gather(): pl.pallas_call(functools.partial(gather_kernel, line), in_specs=[vmem], o...  29.3 us
    pallas_call x1, Pallas kernels, gate(): pl.pallas_call(gate_kernel, grid=(rows // tile,), in_specs=[pl.BlockSpec(...  28.4 us
    dot_general x3, matrix products, dot(): return lax.dot_general(a, b, dims, preferred_element_type=f32)  24.2 us
    pallas_call x1, Pallas kernels, project(): pl.pallas_call(proj_kernel, grid=(rows // tile,), in_specs=[pl.BlockSpec(...  12.7 us
    unnamed x33, local copies, waits for them, and re-layouts  7.86 us
  transfers between devices with their start and end apart: 3, of which 0 were waited for; matrix products, arithmetic and copies ran while one was open for 5% of the time, Pallas kernels for 44%

profile of v6, /device:TPU:0, one launch (start us, length us, event | category | flops | bytes accessed | tf_op | source)
XLA Modules:
  0.0 312.6 jit_solution(3753718360519479151)
XLA Ops:
  7.2 0.0 copy-start.11
  7.2 0.0 copy-start.8
  7.2 0.0 copy-start.10
  7.2 0.0 all-gather.2.cloned.1.call-start
  7.3 0.9 fusion.1
  8.2 0.9 slice.36
  9.2 0.0 copy-start.14
  9.2 0.0 copy-start.12
  9.2 0.0 copy-start.13
  9.2 29.3 %gather.1 = bf16[4,2,2,2,24,1920]{5,4,3,2,1,0:T(8,128)(2,1)S(1)} custom-call(bf16[2,24,1920]{2,1,0:T(8,128)(2,1)S(1)} %bitcast.30), custom_call_target="tpu_custom_call" | custom-call | tf_op jit(solution)/shard_map/gather/pallas_call | solution.py:691
  38.5 1.8 copy-done
  40.2 1.6 pad_maximum_fusion.1
  41.9 0.0 all-gather.2.cloned.1.call-update
  41.9 0.0 reduce-scatter.2.cloned.1.call-start
  42.0 0.0 copy-done.11
  42.0 0.6 reshape.71.gain_ref
  42.6 0.6 reshape.78.gain_ref
  43.2 0.6 reshape.75.cb_ref
  43.8 0.6 reshape.74.seg_ref
  44.4 12.7 %project.1 = (bf16[2048,768]{1,0:T(8,128)(2,1)}, f32[2048,1792]{1,0:T(8,128)}, f32[2048,128]{1,0:T(8,128)}) custom-call(bf16[2048,768]{1,0:T(8,128)(2,1)} %bitcast.36, f32[1,768]{1,0:T(1,128)} %reshape.71.gain_ref, bf16[768,1920]{1,0:T(8,128)(2,1)} %bitcast.28), custom_call_target="tpu_custom_call" | custom-call | tf_op jit(solution)/shard_map/project/pallas_call | solution.py:82
  57.1 0.6 select_maximum_fusion.head_ref
  57.7 41.5 %state_forward.1 = (f32[2048,1536]{1,0:T(8,128)}, f32[2048,1792]{1,0:T(8,128)}, bf16[16,128,1536]{2,1,0:T(8,128)(2,1)}) custom-call(f32[16,128]{1,0:T(8,128)} %reshape.74.seg_ref, f32[2048,1792]{1,0:T(8,128)} %get-tuple-element.38.xbc_ref, f32[2048,128]{1,0:T(8,128)} %get-tuple-element.39.dt_ref, f32[4,1792]{1,0:T(4,128)} %cw_ref.3, ...), custom_call_target="tpu_custom_call" | custom-call | tf_op jit(solution)/shard_map/state_forward/pallas_call | solution.py:263
  99.2 0.0 all-gather.2.cloned.1.call-done
  99.3 0.0 copy-start.1
  99.3 28.4 %gate.1 = (bf16[2048,1536]{1,0:T(8,128)(2,1)}, bf16[2048,768]{1,0:T(8,128)(2,1)}, bf16[2048,1536]{1,0:T(8,128)(2,1)}, f32[2048,1536]{1,0:T(8,128)}, f32[8,1536]{1,0:T(8,128)}) custom-call(bf16[2048,768]{1,0:T(8,128)(2,1)} %bitcast.37, bf16[2048,768]{1,0:T(8,128)(2,1)} %get-tuple-element.37.normed_ref, f32[2048,1536]{1,0:T(8,128)} %get-tuple-element.40.y_ref, ...), custom_call_target="tpu_custom_call" | custom-call | tf_op jit(solution)/shard_map/gate/pallas_call | solution.py:347
  127.7 0.0 copy-done.1
  127.7 0.0 copy-start.2
  127.7 0.0 copy-start.3
  127.7 7.4 %convolution_convert_fusion.1 = bf16[1536,768]{1,0:T(8,128)(2,1)S(1)} fusion(bf16[2048,1536]{1,0:T(8,128)(2,1)} %get-tuple-element.46, bf16[2048,768]{1,0:T(8,128)(2,1)S(1)} %bitcast.42), kind=kOutput, calls=%fused_computation.2 | convolution fusion | flops 4833017856 | bytes 11796480 | tf_op jit(solution)/shard_map/dot_general | solution.py:26
  135.1 5.5 %convolution_convert_fusion.2 = bf16[768,1536]{1,0:T(8,128)(2,1)S(1)} fusion(bf16[2048,768]{1,0:T(8,128)(2,1)S(1)} %copy-done.3, bf16[2048,1536]{1,0:T(8,128)(2,1)S(1)} %copy-done.2), kind=kOutput, calls=%fused_computation.3 | convolution fusion | flops 4833017856 | bytes 11796480 | tf_op jit(solution)/shard_map/dot_general | solution.py:26
  140.6 0.2 fusion
  140.8 2.4 pad_maximum_fusion
  143.2 0.0 reduce-scatter.2.cloned.1.call-update
  143.2 0.0 copy-start.4
  143.2 84.0 %state_backward.1 = (bf16[2048,1920]{1,0:T(8,128)(2,1)}, f32[32,1792]{1,0:T(8,128)}, f32[8,1792]{1,0:T(8,128)}, f32[8,1536]{1,0:T(8,128)}, f32[8,128]{1,0:T(8,128)}, /*index=5*/f32[8,128]{1,0:T(8,128)}) custom-call(f32[16,128]{1,0:T(8,128)} %reshape.74.seg_ref, f32[2048,1792]{1,0:T(8,128)} %get-tuple-element.38.xbc_ref, ...), custom_call_target="tpu_custom_call" | custom-call | tf_op jit(solution)/shard_map/state_backward/pallas_call | solution.py:532
  227.2 0.5 collective-permute-start
  227.8 11.3 %convolution_convert_fusion = bf16[768,1920]{1,0:T(8,128)(2,1)} fusion(bf16[2048,768]{1,0:T(8,128)(2,1)S(1)} %copy-done.4, bf16[2048,1920]{1,0:T(8,128)(2,1)} %get-tuple-element.56.gx_ref), kind=kOutput, calls=%fused_computation.1 | convolution fusion | flops 6041272320 | bytes 13959168 | tf_op jit(solution)/shard_map/dot_general | solution.py:26
  239.1 0.0 collective-permute-done.zo_got_ref
  239.1 0.7 copy-done.7
  239.8 53.7 %finish.1 = (f32[8,1792]{1,0:T(8,128)}, f32[48,3352]{1,0:T(8,128)}, f32[96,768]{1,0:T(8,128)}, bf16[2048,768]{1,0:T(8,128)(2,1)}) custom-call(f32[32,1792]{1,0:T(8,128)} %get-tuple-element.49.cw_ref, f32[8,1792]{1,0:T(8,128)} %get-tuple-element.50.cb_ref, f32[8,1536]{1,0:T(8,128)} %get-tuple-element.51.ggain_ref, f32[8,1536]{1,0:T(8,128)} %get-tuple-element.52.skip_ref, ...), custom_call_target="tpu_custom_call" | custom-call | tf_op jit(solution)/shard_map/finish/pallas_call | solution.py:908
  293.5 1.3 slice_bitcast_fusion
  294.8 1.3 slice_reduce_fusion.2
  296.1 1.4 slice_reduce_fusion.1
  297.5 1.4 slice_reduce_fusion
  299.0 1.4 slice.42
  300.4 3.8 %copy.26 = bf16[2,1024,768]{2,1,0:T(8,128)(2,1)} copy(bf16[2,1024,768]{2,1,0:T(8,128)(2,1)} %bitcast.45) | data formatting | bytes 6291456
  304.2 0.8 copy.27
  305.0 0.7 copy.28
  (20 shorter events, 0.1 us)
Async XLA Ops:
  7.2 34.8 %copy-start.11 = (f32[768]{0:T(1024)S(1)}, f32[768]{0:T(1024)}, u32[]{:S(2)}) copy-start(f32[768]{0:T(1024)} %param.15) | copy-start | bytes 9220
  7.2 35.4 %copy-start.8 = (f32[1536]{0:T(1024)S(1)}, f32[1536]{0:T(1024)}, u32[]{:S(2)}) copy-start(f32[1536]{0:T(1024)} %param.22) | copy-start | bytes 18436
  7.2 36.0 %copy-start.10 = (f32[1792]{0:T(1024)S(1)}, f32[1792]{0:T(1024)}, u32[]{:S(2)}) copy-start(f32[1792]{0:T(1024)} %param.18) | copy-start | bytes 21508
  7.2 36.6 %copy-start.9 = (s32[2,1024]{1,0:T(2,128)S(1)}, s32[2,1024]{1,0:T(2,128)}, u32[]{:S(2)}) copy-start(s32[2,1024]{1,0:T(2,128)} %param.13) | copy-start | bytes 24580
  7.2 92.0 %all-gather.2.cloned.1.call-start = ((), (), s32[]{:S(2)}) async-start(), calls=%async_computation.1 | async-start | bytes 5013504 | tf_op jit(solution)/shard_map/all_gather | solution.py:970
  9.2 47.9 %copy-start.14 = (f32[24]{0:T(128)S(1)}, f32[24]{0:T(128)}, u32[]{:S(2)}) copy-start(f32[24]{0:T(128)} %param.20) | copy-start | bytes 292
  9.2 47.9 %copy-start.12 = (f32[24]{0:T(128)S(1)}, f32[24]{0:T(128)}, u32[]{:S(2)}) copy-start(f32[24]{0:T(128)} %param.21) | copy-start | bytes 292
  9.2 47.9 %copy-start.13 = (f32[24]{0:T(128)S(1)}, f32[24]{0:T(128)}, u32[]{:S(2)}) copy-start(f32[24]{0:T(128)} %param.19) | copy-start | bytes 292
  38.5 1.8 copy-start
  41.9 185.3 %reduce-scatter.2.cloned.1.call-start = ((), (), s32[]{:S(2)}) async-start(), calls=%async_computation.2 | async-start | bytes 5013504 | tf_op jit(solution)/shard_map/reduce_scatter | solution.py:993
  99.3 28.4 %copy-start.1 = (bf16[2,1024,768]{2,1,0:T(8,128)(2,1)S(1)}, bf16[2,1024,768]{2,1,0:T(8,128)(2,1)}, u32[]{:S(2)}) copy-start(bf16[2,1024,768]{2,1,0:T(8,128)(2,1)} %param.14) | copy-start | bytes 9437188
  127.7 7.4 %copy-start.2 = (bf16[2048,1536]{1,0:T(8,128)(2,1)S(1)}, bf16[2048,1536]{1,0:T(8,128)(2,1)}, u32[]{:S(2)}) copy-start(bf16[2048,1536]{1,0:T(8,128)(2,1)} %get-tuple-element.45.gz_ref) | copy-start | bytes 18874372
  127.7 7.4 %copy-start.3 = (bf16[2048,768]{1,0:T(8,128)(2,1)S(1)}, bf16[2048,768]{1,0:T(8,128)(2,1)}, u32[]{:S(2)}) copy-start(bf16[2048,768]{1,0:T(8,128)(2,1)} %get-tuple-element.37.normed_ref) | copy-start | bytes 9437188
  143.2 84.6 %copy-start.4 = (bf16[2048,768]{1,0:T(8,128)(2,1)S(1)}, bf16[2048,768]{1,0:T(8,128)(2,1)}, u32[]{:S(2)}) copy-start(bf16[2048,768]{1,0:T(8,128)(2,1)} %get-tuple-element.37.normed_ref) | copy-start | bytes 9437188
  227.2 11.9 %collective-permute-start = (bf16[192,768]{1,0:T(8,128)(2,1)}, bf16[192,768]{1,0:T(8,128)(2,1)S(1)}, u32[]{:S(2)}, u32[]{:S(2)}) collective-permute-start(bf16[192,768]{1,0:T(8,128)(2,1)} %reduce-scatter.2.cloned.1.call-done.zo_ref), channel_id=1, source_target_pairs={{0,1},{1,0},{2,3},{3,2},{4,5},{5,4},{6,7},{7,6},{8,9},{9,8},{10,11... | collective-permute-start | bytes 884744 | tf_op jit(solution)/shard_map/ppermute | solution.py:998
  239.1 0.7 copy-start.7
  293.5 10.7 %copy-start.5 = (f32[48,3352]{1,0:T(8,128)S(1)}, f32[48,3352]{1,0:T(8,128)}, u32[]{:S(2)}) copy-start(f32[48,3352]{1,0:T(8,128)} %get-tuple-element.82) | copy-start | bytes 1930756
  293.5 11.5 %copy-start.6 = (f32[96,768]{1,0:T(8,128)S(1)}, f32[96,768]{1,0:T(8,128)}, u32[]{:S(2)}) copy-start(f32[96,768]{1,0:T(8,128)} %get-tuple-element.89) | copy-start | bytes 884740
Sparse Core Ops, SparseCore 0:
  42.0 52.7 all-gather.1
  143.3 75.2 reduce-scatter.1

commit v7 on v5

--- a/solution.py
+++ b/solution.py
@@ -180,26 +180,44 @@
     seg_ref, xbc_ref, dt_ref, cw_ref, cb_ref, head_ref,
     y_ref, s_ref, sin_ref, state, ext, e_ref, tri_ref, skip_ref,
 ):
-    inner = y_ref.shape[1]
+    seqs, _, inner = y_ref.shape
     channels = cb_ref.shape[1]
-    b, blocks = pl.program_id(1), pl.num_programs(1)
-    dtb, _, na2 = head_terms(head_ref)
-
-    @pl.when((b == 0) & (pl.program_id(0) == 0))
+    b = pl.program_id(0)
+
+    @pl.when(b == 0)
     def _():
         fill_constants(e_ref, tri_ref, skip_ref, head_ref)
 
     @pl.when(b == 0)
     def _():
         state[...] = jnp.zeros_like(state)
-        ext[0:8, :] = jnp.zeros((8, channels), f32)
+        ext[:, 0:8, :] = jnp.zeros((seqs, 8, channels), f32)
 
     @pl.when(b > 0)
     def _():
-        ext[0:8, :] = ext[Q : Q + 8, :]
-
+        ext[:, 0:8, :] = ext[:, Q : Q + 8, :]
+
+    alternate(
+        [
+            fwd_block(
+                q, seg_ref, xbc_ref.at[q], dt_ref.at[q], cw_ref, cb_ref, head_ref,
+                *[r.at[q] for r in (y_ref, s_ref, sin_ref, state, ext)], e_ref, tri_ref, skip_ref,
+            )
+            for q in range(seqs)
+        ],
+        2,
+    )
+
+
+def fwd_block(
+    q, seg_ref, xbc_ref, dt_ref, cw_ref, cb_ref, head_ref,
+    y_ref, s_ref, sin_ref, state, ext, e_ref, tri_ref, skip_ref,
+):
+    inner = y_ref.shape[1]
+    b, blocks = pl.program_id(0), pl.num_programs(0)
+    dtb, _, na2 = head_terms(head_ref)
     ext[8 : 8 + Q, :] = xbc_ref[...]
-    seg, cols = segment_rows(seg_ref, b, blocks, pl.program_id(0) * blocks + b)
+    seg, cols = segment_rows(seg_ref, b, blocks, q * blocks + b)
     m1, m2, m3 = (wide(cols[:, k : k + 1], 256) for k in (1, 2, 3))
 
     def conv(c):
@@ -225,6 +243,7 @@
     mask = jnp.where(same & (row_i >= col_j), 0.0, NEG)
     scores = dot_split((cm, bc_rest[:, LANES:]), (bm, bc_rest[:, :LANES]))
     left = col_j < HEAD
+    yield
 
     for c in range(0, inner, 256):
         at = pl.ds(c, 256)
@@ -249,6 +268,7 @@
         y = jnp.concatenate(parts, axis=1) + s_e * carried + skip_ref[:, at] * x
         y_ref[:, at] = y
         state[:, at] = st * s_e[Q - 1 : Q, :] + dot(bt, (xs * e_e).astype(bf16))
+        yield
 
 
 def fixed(shape):
@@ -258,37 +278,38 @@
 def state_forward(seg, xbc, dt, cw, cb, head, inner, seqs):
     rows, channels = xbc.shape
     blocks = rows // seqs // Q
-    at = lambda s, b: (s * blocks + b, 0)
-    at3 = lambda s, b: (s * blocks + b, 0, 0)
-    return pl.pallas_call(
+    at = lambda b: (0, b, 0)
+    tiled = lambda v: v.reshape(seqs, rows // seqs, v.shape[1])
+    y, s, sin = pl.pallas_call(
         fwd_kernel,
-        grid=(seqs, blocks),
+        grid=(blocks,),
         in_specs=[
             fixed(seg.shape),
-            pl.BlockSpec((Q, channels), at),
-            pl.BlockSpec((Q, LANES), at),
+            pl.BlockSpec((seqs, Q, channels), at),
+            pl.BlockSpec((seqs, Q, LANES), at),
             fixed(cw.shape), fixed(cb.shape), fixed(head.shape),
         ],
         out_specs=[
-            pl.BlockSpec((Q, inner), at),
-            pl.BlockSpec((Q, channels), at),
-            pl.BlockSpec((None, LANES, inner), at3),
+            pl.BlockSpec((seqs, Q, inner), at),
+            pl.BlockSpec((seqs, Q, channels), at),
+            pl.BlockSpec((seqs, None, LANES, inner), lambda b: (0, b, 0, 0)),
         ],
         out_shape=[
-            jax.ShapeDtypeStruct((rows, inner), f32),
-            jax.ShapeDtypeStruct((rows, channels), f32),
-            jax.ShapeDtypeStruct((seqs * blocks, LANES, inner), bf16),
+            jax.ShapeDtypeStruct((seqs, rows // seqs, inner), f32),
+            jax.ShapeDtypeStruct((seqs, rows // seqs, channels), f32),
+            jax.ShapeDtypeStruct((seqs, blocks, LANES, inner), bf16),
         ],
         scratch_shapes=[
-            pltpu.VMEM((LANES, inner), f32),
-            pltpu.VMEM((Q + 8, channels), f32),
+            pltpu.VMEM((seqs, LANES, inner), f32),
+            pltpu.VMEM((seqs, Q + 8, channels), f32),
             pltpu.VMEM((2 * LANES, inner), bf16),
             pltpu.VMEM((Q, Q), bf16),
             pltpu.VMEM((1, inner), f32),
         ],
         compiler_params=params(60 << 20),
         name="state_forward",
-    )(seg, xbc, dt, cw, cb, head)
+    )(seg, tiled(xbc), tiled(dt), cw, cb, head)
+    return y.reshape(rows, inner), s.reshape(rows, channels), sin
 
 
 def flat(ref):
@@ -378,12 +399,11 @@
     gx_ref, gcw_ref, gcb_ref, gskip_ref, galog_ref, gdtb_ref,
     adj, gext, da_rows, spread, grad_b, grad_c, link, e_ref, tri_ref, skip_ref, et_ref, tail_ref, pair_ref,
 ):
-    inner = gm_ref.shape[1]
-    channels = s_ref.shape[1]
-    b, blocks = pl.program_id(1), pl.num_programs(1)
-    dtb, rate, na2 = head_terms(head_ref)
-
-    @pl.when((b == 0) & (pl.program_id(0) == 0))
+    seqs, _, inner = gm_ref.shape
+    channels = s_ref.shape[2]
+    b = pl.program_id(0)
+
+    @pl.when(b == 0)
     def _():
         for ref in (gcw_ref, gcb_ref, gskip_ref, galog_ref, gdtb_ref, da_rows):
             ref[...] = jnp.zeros_like(ref)
@@ -398,17 +418,49 @@
     @pl.when(b == 0)
     def _():
         adj[...] = jnp.zeros_like(adj)
-        gext[Q : Q + 8, :] = jnp.zeros((8, channels), f32)
+        gext[:, Q : Q + 8, :] = jnp.zeros((seqs, 8, channels), f32)
 
     @pl.when(b > 0)
     def _():
-        gext[Q : Q + 8, :] = gext[0:8, :]
-
+        gext[:, Q : Q + 8, :] = gext[:, 0:8, :]
+
+    alternate(
+        [
+            bwd_block(
+                q, seg_ref, *[r.at[q] for r in (xbc_ref, dt_ref, s_ref, sin_ref, gm_ref)], cw_ref, head_ref,
+                gx_ref.at[q], gcw_ref, gcb_ref, gskip_ref, galog_ref, gdtb_ref,
+                *[r.at[q] for r in (adj, gext, da_rows, spread, grad_b, grad_c, link)],
+                e_ref, tri_ref, skip_ref, et_ref, tail_ref, pair_ref,
+            )
+            for q in range(seqs)
+        ],
+        26,
+    )
+
+
+def alternate(blocks, lead):
+    for _ in range(lead):
+        next(blocks[0], None)
+    live = list(blocks)
+    while live:
+        live = [block for block in reversed(live) if next(block, live) is not live][::-1]
+
+
+def bwd_block(
+    q, seg_ref, xbc_ref, dt_ref, s_ref, sin_ref, gm_ref, cw_ref, head_ref,
+    gx_ref, gcw_ref, gcb_ref, gskip_ref, galog_ref, gdtb_ref,
+    adj, gext, da_rows, spread, grad_b, grad_c, link, e_ref, tri_ref, skip_ref, et_ref, tail_ref, pair_ref,
+):
+    inner = gm_ref.shape[1]
+    channels = s_ref.shape[1]
+    b, blocks = pl.program_id(0), pl.num_programs(0)
+    dtb, rate, na2 = head_terms(head_ref)
     turn = blocks - 1 - b
-    seg, cols = segment_rows(seg_ref, turn, blocks, pl.program_id(0) * blocks + turn)
+    seg, cols = segment_rows(seg_ref, turn, blocks, q * blocks + turn)
     raw, ts, cum, start, end = step_terms(dt_ref[...], dtb, na2, tri_ref[...], cols)
     cum_t = cum.T
     grow = expand_operand(start, end, ts)
+    yield
 
     def act(c):
         s = s_ref[:, pl.ds(c, 256)]
@@ -429,8 +481,9 @@
     scores = dot_split((bm, bc_rest[:, :LANES]), (cm, bc_rest[:, LANES:]))
     left = col_i < HEAD
     grad_scores = jnp.zeros((Q, Q), f32)
-
-    for c in range(0, inner, 256):
+    yield
+
+    def enter(c):
         at = pl.ds(c, 256)
         x, slope = act(c)
         big = dot(grow, e_ref[:, at])
@@ -439,35 +492,53 @@
         xs_low, xs_rest = split(xs, 2)
         gm = gm_ref[:, at]
         gm_low, gm_rest = split(gm, 2)
-        ad = adj[:, at]
-        ad_low, ad_rest = split(ad, 2)
+        ad_low, ad_rest = split(adj[:, at], 2)
         st_low = sin_ref[:, at]
         into = dot(b_two, twice(ad_low, 0)) + dot(bm, ad_rest)
         carried = dot(c_two, twice(st_low, 0))
-        parts = []
+        diags, gmats = [], []
         for p in range(2):
             lanes = slice(p * LANES, (p + 1) * LANES)
-            diag, diag_rest = by_head(gm_low[:, lanes], left), by_head(gm_rest[:, lanes], left)
-            gmat = dot_split((xs_low[:, lanes], xs_rest[:, lanes]), (diag, diag_rest))
+            diags.append((by_head(gm_low[:, lanes], left), by_head(gm_rest[:, lanes], left)))
+            tall = dot(jnp.concatenate([xs_low[:, lanes], xs_rest[:, lanes]], axis=0), diags[p][0], NT)
+            gmats.append(tall[:Q] + tall[Q:] + dot(xs_low[:, lanes], diags[p][1], NT))
+        return x, slope, s_e, e_e, t_e, xs, gm, ad_low, st_low, into, carried, diags, gmats
+
+    def within(c, held):
+        diags, gmats = held[-2:]
+        parts, joined = [], []
+        extra = jnp.zeros((Q, Q), f32)
+        for p in range(2):
+            diag, diag_rest = diags[p]
             mats, links = [], []
             for h in range(2):
                 head = (c + p * LANES) // HEAD + h
                 gap = cum_t[head : head + 1, :] - wide(cum[:, head : head + 1], LANES) + mask
                 decay = jnp.exp2(gap)
                 mat = decay * scores
-                grad = gmat[:, h * LANES : (h + 1) * LANES]
-                grad_scores += decay * grad
+                grad = gmats[p][:, h * LANES : (h + 1) * LANES]
+                extra += decay * grad
                 mats.append(split(mat, 2))
                 links.append((mat * grad).astype(bf16))
             high = jnp.concatenate([mats[0][0], mats[1][0]], axis=1)
             rest = jnp.concatenate([mats[0][1], mats[1][1]], axis=1)
-            parts.append(dot(high, diag) + dot(high, diag_rest) + dot(rest, diag))
-            reach = dot(jnp.concatenate(links, axis=1), pair_ref[...])
-            for h in range(2):
-                head = (c + p * LANES) // HEAD + h
-                da_rows[head : head + 1, :] = jnp.sum(
-                    reach[:, h * LANES : (h + 1) * LANES] * before, axis=0, keepdims=True
-                )
+            both = dot(jnp.concatenate([high, rest], axis=0), diag)
+            parts.append(both[:Q] + both[Q:] + dot(high, diag_rest))
+            joined.append(jnp.concatenate(links, axis=1))
+            yield
+        reach = dot(jnp.concatenate(joined, axis=0), pair_ref[...])
+        for n in range(4):
+            p, h = n // 2, n % 2
+            head = c // HEAD + n
+            da_rows[head : head + 1, :] = jnp.sum(
+                reach[p * Q : (p + 1) * Q, h * LANES : (h + 1) * LANES] * before, axis=0, keepdims=True
+            )
+        return parts, extra
+
+    def leave(c, held, parts):
+        at = pl.ds(c, 256)
+        x, slope, s_e, e_e, t_e, xs, gm, ad_low, st_low, into, carried = held[:-2]
+        ad = adj[:, at]
         g_xs = jnp.concatenate(parts, axis=1) + e_e * into
         gext[0:Q, at] = (t_e * g_xs + skip_ref[:, at] * gm) * slope
         sums = jnp.concatenate(
@@ -489,6 +560,18 @@
         link[:, at] = fold_rows(st_low.astype(f32) * ad)
         adj[:, at] = ad * s_e[Q - 1 : Q, :] + dot(ct, s_gm)
 
+    starts = list(range(0, inner, 256))
+    held, inside = {}, {}
+    for step in range(len(starts) + 1):
+        if step < len(starts):
+            held[step] = enter(starts[step])
+            yield
+        if 0 <= step - 1:
+            parts, extra = yield from within(starts[step - 1], held[step - 1])
+            grad_scores += extra
+            leave(starts[step - 1], held.pop(step - 1), parts)
+        yield
+
     grad_low = grad_scores.astype(bf16)
     g_b = grad_b[...] + dot(grad_low, cm)
     g_c = grad_c[...] + dot(grad_low, bm, TN)
@@ -500,6 +583,7 @@
     around = jnp.concatenate(split(phi, 2) + split(psi, 2), axis=0)
     da = da_rows[...].T + dot(tail_ref[...], around) + start[Q - 1 : Q, :] * through
     g_ts = spread[2 * Q :] + rate * da
+    yield
     galog_ref[...] += fold_rows(ts * rate * da)
     g_dt = g_ts * sigmoid(raw)
     gdtb_ref[...] += fold_rows(g_dt)
@@ -520,6 +604,7 @@
         gcw_ref[16:24, at] += fold_rows(g1 * x)
         gcw_ref[8:16, at] += fold_rows(g2 * x)
         gcw_ref[0:8, at] += fold_rows(g3 * x)
+        yield
     gx_ref[:, channels:] = g_dt.astype(bf16)
 
 
@@ -527,26 +612,26 @@
     rows, channels = xbc.shape
     inner = gm.shape[1]
     blocks = rows // seqs // Q
-    at = lambda s, b: (s * blocks + blocks - 1 - b, 0)
-    at3 = lambda s, b: (s * blocks + blocks - 1 - b, 0, 0)
-    return pl.pallas_call(
+    at = lambda b: (0, blocks - 1 - b, 0)
+    tiled = lambda v: v.reshape(seqs, rows // seqs, v.shape[1])
+    out = pl.pallas_call(
         bwd_kernel,
-        grid=(seqs, blocks),
+        grid=(blocks,),
         in_specs=[
             fixed(seg.shape),
-            pl.BlockSpec((Q, channels), at),
-            pl.BlockSpec((Q, LANES), at),
-            pl.BlockSpec((Q, channels), at),
-            pl.BlockSpec((None, LANES, inner), at3),
-            pl.BlockSpec((Q, inner), at),
+            pl.BlockSpec((seqs, Q, channels), at),
+            pl.BlockSpec((seqs, Q, LANES), at),
+            pl.BlockSpec((seqs, Q, channels), at),
+            pl.BlockSpec((seqs, None, LANES, inner), lambda b: (0, blocks - 1 - b, 0, 0)),
+            pl.BlockSpec((seqs, Q, inner), at),
         ]
         + [fixed(v.shape) for v in (cw, head)],
         out_specs=[
-            pl.BlockSpec((Q, channels + LANES), at),
+            pl.BlockSpec((seqs, Q, channels + LANES), at),
             fixed((32, channels)), fixed((8, channels)), fixed((8, inner)), fixed((8, LANES)), fixed((8, LANES)),
         ],
         out_shape=[
-            jax.ShapeDtypeStruct((rows, channels + LANES), bf16),
+            jax.ShapeDtypeStruct((seqs, rows // seqs, channels + LANES), bf16),
             jax.ShapeDtypeStruct((32, channels), f32),
             jax.ShapeDtypeStruct((8, channels), f32),
             jax.ShapeDtypeStruct((8, inner), f32),
@@ -554,13 +639,13 @@
             jax.ShapeDtypeStruct((8, LANES), f32),
         ],
         scratch_shapes=[
-            pltpu.VMEM((LANES, inner), f32),
-            pltpu.VMEM((Q + 8, channels), f32),
-            pltpu.VMEM((LANES, LANES), f32),
-            pltpu.VMEM((3 * Q, LANES), f32),
-            pltpu.VMEM((Q, LANES), f32),
-            pltpu.VMEM((Q, LANES), f32),
-            pltpu.VMEM((8, inner), f32),
+            pltpu.VMEM((seqs, LANES, inner), f32),
+            pltpu.VMEM((seqs, Q + 8, channels), f32),
+            pltpu.VMEM((seqs, LANES, LANES), f32),
+            pltpu.VMEM((seqs, 3 * Q, LANES), f32),
+            pltpu.VMEM((seqs, Q, LANES), f32),
+            pltpu.VMEM((seqs, Q, LANES), f32),
+            pltpu.VMEM((seqs, 8, inner), f32),
             pltpu.VMEM((2 * LANES, inner), bf16),
             pltpu.VMEM((Q, Q), bf16),
             pltpu.VMEM((1, inner), f32),
@@ -570,7 +655,10 @@
         ],
         compiler_params=params(60 << 20),
         name="state_backward",
-    )(seg, xbc, dt, s, sin, gm, cw, head)
+    )(
+        seg, tiled(xbc), tiled(dt), tiled(s), sin.reshape(seqs, blocks, LANES, inner), tiled(gm), cw, head
+    )
+    return out[0].reshape(rows, channels + LANES), *out[1:]
 
 
 def token_kernel(tok_ref, cot_ref, gz_ref, gx_ref, wa_ref, wb_ref, wx_ref, gain_ref, out_ref, ggain_ref):
@@ -650,21 +738,22 @@
 
     mine = pltpu.make_async_copy(own_ref, out_ref.at[l, x, c], local.at[0])
     mine.start()
+    send(own_ref.at[y], (l, x, c, y), x_send.at[0], beside)
     for k in range(1, line):
-        send(own_ref.at[y], (l, x, c, y), line_send.at[k], others[k - 1])
-    send(own_ref.at[y], (l, x, c, y), x_send.at[0], beside)
+        send(own_ref.at[y], (l, x, c, y), line_send.at[k, 0], others[k - 1])
+    for k in range(1, line):
+        send(own_ref.at[1 - y], (l, x, c, 1 - y), line_send.at[k, 1], others[k - 1])
     for h in range(2):
         send(own_ref.at[h], (l, x, c, h), core_send.at[0, h], sibling)
     for k in range(1, line):
         at = ((l + k) % line, x, c, y)
         arrived(at)
         send(out_ref.at[at], at, x_send.at[k], beside)
-        send(out_ref.at[at], at, y_send.at[k], across)
         send(out_ref.at[at], at, core_send.at[k, 0], sibling)
     for k in range(line):
         at = ((l + k) % line, 1 - x, c, y)
         arrived(at)
-        send(out_ref.at[at], at, y_send.at[line + k], across)
+        send(out_ref.at[at], at, y_send.at[k], across)
         send(out_ref.at[at], at, core_send.at[line + k, 0], sibling)
     for k in range(1, line):
         at = ((l + k) % line, x, c, 1 - y)
@@ -694,7 +783,7 @@
         out_specs=vmem,
         out_shape=jax.ShapeDtypeStruct((line, 2, 2, 2, own // 2, columns), local.dtype),
         scratch_shapes=[
-            dma((line,)), dma((line,)), dma((2 * line,)), dma((2 * line, 2)), dma((line, 2, 2, 2)), dma((2,)),
+            dma((line, 2)), dma((line,)), dma((line,)), dma((2 * line, 2)), dma((line, 2, 2, 2)), dma((2,)),
         ],
         compiler_params=params(48 << 20, collective_id=1, has_side_effects=True),
         name="gather",
@@ -871,8 +960,8 @@
     local_x = jnp.pad(weight_in[:, inner:], ((0, 0), (0, pad)))
     owned = sizes["dp"] % 4 == 0 and sizes["seq"] == 2
     wx = gather(local_x, owners) if owned else lax.all_gather(local_x, "dp", axis=0, tiled=True)
-    wx, weight_out = lax.optimization_barrier((wx, weight_out))
     local_zo = jnp.concatenate([weight_in[:, :width], weight_in[:, width:inner], weight_out], axis=0)
+    wx, local_zo = lax.optimization_barrier((wx, local_zo))
     slab = lax.all_gather(local_zo, "dp", axis=0, tiled=True).reshape(owners, 4 * own, width)
     weights = slab_views(slab, own)
 

time: 302 us -> 298 us (0.987)
  Pallas kernels: 247 us -> 242 us
    pallas_call x2, Pallas kernels: 125 us -> 121 us  [the longest x1 80.9 us: state_backward(): pl.pallas_call(bwd_kernel, grid=(blocks,), in_specs=[fixed(seg.shape), pl...]
where the time goes in v7:
time: 298 us; the launch traced here: 297 us
  Pallas kernels  242 us (81%)
  matrix products  23.7 us (8%)
  between operations  14.4 us (5%)
  local copies, waits for them, and re-layouts  11.5 us (4%)
  other arithmetic  4.66 us (2%)
    pallas_call x1, Pallas kernels, state_backward(): pl.pallas_call(bwd_kernel, grid=(blocks,), in_specs=[fixed(seg.shape), pl...  80.9 us
    pallas_call x1, Pallas kernels, state_forward(): pl.pallas_call(fwd_kernel, grid=(blocks,), in_specs=[fixed(seg.shape), pl...  39.6 us
    pallas_call x1, Pallas kernels, finish(): pl.pallas_call(functools.partial(finish_kernel, line, bits), in_specs=[vm...  33.5 us
    pallas_call x1, Pallas kernels, gate(): pl.pallas_call(gate_kernel, grid=(rows // tile,), in_specs=[pl.BlockSpec(...  28.4 us
    pallas_call x1, Pallas kernels, gather(): pl.pallas_call(functools.partial(gather_kernel, line), in_specs=[vmem], o...  26.6 us
    dot_general x3, matrix products, dot(): return lax.dot_general(a, b, dims, preferred_element_type=f32)  23.7 us
    pallas_call x1, Pallas kernels, token_grad(): pl.pallas_call(token_kernel, grid=(rows // tile,), in_specs=[pl.BlockSpec...  20 us
    pallas_call x1, Pallas kernels, project(): pl.pallas_call(proj_kernel, grid=(rows // tile,), in_specs=[pl.BlockSpec(...  12.7 us
  transfers between devices with their start and end apart: 3, of which 0 were waited for; matrix products, arithmetic and copies ran while one was open for 5% of the time, Pallas kernels for 52%

profile of v7, /device:TPU:0, one launch (start us, length us, event | category | flops | bytes accessed | tf_op | source)
XLA Modules:
  0.0 297.4 jit_solution(433851243711257150)
XLA Ops:
  7.2 0.0 all-gather.2.cloned.1.call-start
  7.3 0.9 fusion.1
  8.2 0.9 slice.36
  9.2 0.0 copy-start.18
  9.2 0.0 copy-start.16
  9.2 0.0 copy-start.17
  9.2 26.6 %gather.1 = bf16[4,2,2,2,24,1920]{5,4,3,2,1,0:T(8,128)(2,1)S(1)} custom-call(bf16[2,24,1920]{2,1,0:T(8,128)(2,1)S(1)} %bitcast.36), custom_call_target="tpu_custom_call" | custom-call | tf_op jit(solution)/shard_map/gather/pallas_call | solution.py:780
  35.8 1.7 copy-done
  37.5 1.6 pad_maximum_fusion.1
  39.2 0.0 all-gather.2.cloned.1.call-update
  39.2 0.0 reduce-scatter.2.cloned.1.call-start
  39.2 0.0 copy-done.15
  39.3 0.6 reshape.88.gain_ref
  39.8 0.6 reshape.98.gain_ref
  40.4 0.6 reshape.94.cb_ref
  41.0 0.6 reshape.91.seg_ref
  41.7 12.7 %project.1 = (bf16[2048,768]{1,0:T(8,128)(2,1)}, f32[2048,1792]{1,0:T(8,128)}, f32[2048,128]{1,0:T(8,128)}) custom-call(bf16[2048,768]{1,0:T(8,128)(2,1)} %bitcast.44, f32[1,768]{1,0:T(1,128)} %reshape.88.gain_ref, bf16[768,1920]{1,0:T(8,128)(2,1)} %bitcast.33), custom_call_target="tpu_custom_call" | custom-call | tf_op jit(solution)/shard_map/project/pallas_call | solution.py:82
  54.4 0.6 select_maximum_fusion.head_ref
  55.0 39.6 %state_forward.1 = (f32[2,1024,1536]{2,1,0:T(8,128)}, f32[2,1024,1792]{2,1,0:T(8,128)}, bf16[2,8,128,1536]{3,2,1,0:T(8,128)(2,1)}) custom-call(f32[16,128]{1,0:T(8,128)} %reshape.91.seg_ref, f32[2,1024,1792]{2,1,0:T(8,128)} %bitcast.42, f32[2,1024,128]{2,1,0:T(8,128)} %bitcast.57, f32[4,1792]{1,0:T(4,128)} %cw_ref.3, f32[1,1792]{1,0:T(1,128)} %reshape.94.cb_ref, ...), custom_call_target="tpu_custom_call" | custom-call | tf_op jit(solution)/shard_map/state_forward/pallas_call | solution.py:283
  94.6 28.4 %gate.1 = (bf16[2048,1536]{1,0:T(8,128)(2,1)}, bf16[2048,768]{1,0:T(8,128)(2,1)}, bf16[2048,1536]{1,0:T(8,128)(2,1)}, f32[2048,1536]{1,0:T(8,128)}, f32[8,1536]{1,0:T(8,128)}) custom-call(bf16[2048,768]{1,0:T(8,128)(2,1)} %bitcast.45, bf16[2048,768]{1,0:T(8,128)(2,1)} %get-tuple-element.38.normed_ref, f32[2048,1536]{1,0:T(8,128)} %bitcast.51, ...), custom_call_target="tpu_custom_call" | custom-call | tf_op jit(solution)/shard_map/gate/pallas_call | solution.py:368
  123.0 0.0 copy-done.9
  123.0 0.0 copy-start.10
  123.0 0.0 copy-start.11
  123.0 7.4 %convolution_convert_fusion.1 = bf16[1536,768]{1,0:T(8,128)(2,1)S(1)} fusion(bf16[2048,1536]{1,0:T(8,128)(2,1)} %get-tuple-element.47, bf16[2048,768]{1,0:T(8,128)(2,1)S(1)} %bitcast.50), kind=kOutput, calls=%fused_computation.2 | convolution fusion | flops 4833017856 | bytes 11796480 | tf_op jit(solution)/shard_map/dot_general | solution.py:26
  130.4 0.0 copy-done.10
  130.5 5.6 %convolution_convert_fusion.2 = bf16[768,1536]{1,0:T(8,128)(2,1)S(1)} fusion(bf16[2048,768]{1,0:T(8,128)(2,1)S(1)} %copy-done.11, bf16[2048,1536]{1,0:T(8,128)(2,1)S(1)} %copy-done.10), kind=kOutput, calls=%fused_computation.3 | convolution fusion | flops 4833017856 | bytes 11796480 | tf_op jit(solution)/shard_map/dot_general | solution.py:26
  136.1 0.2 fusion
  136.3 2.4 pad_maximum_fusion
  138.7 0.0 reduce-scatter.2.cloned.1.call-update
  138.7 80.9 %state_backward.1 = (bf16[2,1024,1920]{2,1,0:T(8,128)(2,1)}, f32[32,1792]{1,0:T(8,128)}, f32[8,1792]{1,0:T(8,128)}, f32[8,1536]{1,0:T(8,128)}, f32[8,128]{1,0:T(8,128)}, /*index=5*/f32[8,128]{1,0:T(8,128)}) custom-call(f32[16,128]{1,0:T(8,128)} %reshape.91.seg_ref, f32[2,1024,1792]{2,1,0:T(8,128)} %bitcast.43, f32[2,1024,128]{2,1,0:T(8,128)} %bitcast.58, ...), custom_call_target="tpu_custom_call" | custom-call | tf_op jit(solution)/shard_map/state_backward/pallas_call | solution.py:617
  219.6 0.0 reduce-scatter.2.cloned.1.call-done.zo_ref
  219.7 1.3 collective-permute-start
  220.9 10.7 %convolution_convert_fusion = bf16[768,1920]{1,0:T(8,128)(2,1)S(1)} fusion(bf16[2048,768]{1,0:T(8,128)(2,1)} %get-tuple-element.38.normed_ref, bf16[2048,1920]{1,0:T(8,128)(2,1)} %bitcast.53), kind=kOutput, calls=%fused_computation.1 | convolution fusion | flops 6041272320 | bytes 13959168 | tf_op jit(solution)/shard_map/dot_general | solution.py:26
  231.6 0.0 copy-start.2
  231.6 0.0 copy-start.3
  231.6 0.0 copy-start.7
  231.7 20.0 %token_grad.1 = (bf16[2048,768]{1,0:T(8,128)(2,1)}, f32[8,768]{1,0:T(8,128)}) custom-call(bf16[2048,768]{1,0:T(8,128)(2,1)} %bitcast.46, bf16[2048,768]{1,0:T(8,128)(2,1)} %bitcast.49, bf16[2048,1536]{1,0:T(8,128)(2,1)} %get-tuple-element.44.gz_ref, bf16[2048,1920]{1,0:T(8,128)(2,1)} %bitcast.54, bf16[16,192,768]{2,1,0:T(8,128)(2,1)} %bitcast.40, ...), custom_call_target="tpu_custom_call" | custom-call | tf_op jit(solution)/shard_map/token_grad/pallas_call | solution.py:685
  251.7 0.0 collective-permute-done.zo_got_ref
  251.8 0.0 copy-start.6
  251.8 0.7 copy-done.6
  252.5 33.5 %finish.1 = (f32[8,1792]{1,0:T(8,128)S(1)}, f32[48,3352]{1,0:T(8,128)S(1)}, f32[96,768]{1,0:T(8,128)S(1)}) custom-call(f32[32,1792]{1,0:T(8,128)S(1)} %copy-done.2, f32[8,1792]{1,0:T(8,128)S(1)} %copy-done.3, f32[8,1536]{1,0:T(8,128)S(1)} %copy-done.4, f32[8,1536]{1,0:T(8,128)S(1)} %copy-done.5, f32[8,768]{1,0:T(8,128)S(1)} %copy-done.6, ...), custom_call_target="tpu_custom_call" | custom-call | tf_op jit(solution)/shard_map/finish/pallas_call | solution.py:911
  286.1 0.5 slice_bitcast_fusion
  286.6 0.6 slice_reduce_fusion.2
  287.2 0.6 slice_reduce_fusion.1
  287.8 0.6 slice_reduce_fusion
  288.4 0.6 slice.42
  289.0 0.8 copy.25
  289.9 0.7 copy.26
  (28 shorter events, 0.1 us)
Async XLA Ops:
  7.2 32.1 %copy-start.15 = (f32[768]{0:T(1024)S(1)}, f32[768]{0:T(1024)}, u32[]{:S(2)}) copy-start(f32[768]{0:T(1024)} %param.15) | copy-start | bytes 9220
  7.2 32.7 %copy-start.12 = (f32[1536]{0:T(1024)S(1)}, f32[1536]{0:T(1024)}, u32[]{:S(2)}) copy-start(f32[1536]{0:T(1024)} %param.22) | copy-start | bytes 18436
  7.2 33.2 %copy-start.14 = (f32[1792]{0:T(1024)S(1)}, f32[1792]{0:T(1024)}, u32[]{:S(2)}) copy-start(f32[1792]{0:T(1024)} %param.18) | copy-start | bytes 21508
  7.2 33.8 %copy-start.13 = (s32[2,1024]{1,0:T(2,128)S(1)}, s32[2,1024]{1,0:T(2,128)}, u32[]{:S(2)}) copy-start(s32[2,1024]{1,0:T(2,128)} %param.13) | copy-start | bytes 24580
  7.2 87.4 %all-gather.2.cloned.1.call-start = ((), (), s32[]{:S(2)}) async-start(), calls=%async_computation.1 | async-start | bytes 5013504 | tf_op jit(solution)/shard_map/all_gather | solution.py:965
  9.2 45.2 %copy-start.18 = (f32[24]{0:T(128)S(1)}, f32[24]{0:T(128)}, u32[]{:S(2)}) copy-start(f32[24]{0:T(128)} %param.20) | copy-start | bytes 292
  9.2 45.2 %copy-start.16 = (f32[24]{0:T(128)S(1)}, f32[24]{0:T(128)}, u32[]{:S(2)}) copy-start(f32[24]{0:T(128)} %param.21) | copy-start | bytes 292
  9.2 45.2 %copy-start.17 = (f32[24]{0:T(128)S(1)}, f32[24]{0:T(128)}, u32[]{:S(2)}) copy-start(f32[24]{0:T(128)} %param.19) | copy-start | bytes 292
  35.8 1.7 copy-start
  39.2 180.4 %reduce-scatter.2.cloned.1.call-start = ((), (), s32[]{:S(2)}) async-start(), calls=%async_computation.2 | async-start | bytes 5013504 | tf_op jit(solution)/shard_map/reduce_scatter | solution.py:988
  94.6 28.4 %copy-start.9 = (bf16[2,1024,768]{2,1,0:T(8,128)(2,1)S(1)}, bf16[2,1024,768]{2,1,0:T(8,128)(2,1)}, u32[]{:S(2)}) copy-start(bf16[2,1024,768]{2,1,0:T(8,128)(2,1)} %param.14) | copy-start | bytes 9437188
  123.0 7.4 %copy-start.10 = (bf16[2048,1536]{1,0:T(8,128)(2,1)S(1)}, bf16[2048,1536]{1,0:T(8,128)(2,1)}, u32[]{:S(2)}) copy-start(bf16[2048,1536]{1,0:T(8,128)(2,1)} %get-tuple-element.44.gz_ref) | copy-start | bytes 18874372
  123.0 7.4 %copy-start.11 = (bf16[2048,768]{1,0:T(8,128)(2,1)S(1)}, bf16[2048,768]{1,0:T(8,128)(2,1)}, u32[]{:S(2)}) copy-start(bf16[2048,768]{1,0:T(8,128)(2,1)} %get-tuple-element.38.normed_ref) | copy-start | bytes 9437188
  219.7 32.0 %collective-permute-start = (bf16[192,768]{1,0:T(8,128)(2,1)}, bf16[192,768]{1,0:T(8,128)(2,1)S(1)}, u32[]{:S(2)}, u32[]{:S(2)}) collective-permute-start(bf16[192,768]{1,0:T(8,128)(2,1)} %reduce-scatter.2.cloned.1.call-done.zo_ref), channel_id=1, source_target_pairs={{0,1},{1,0},{2,3},{3,2},{4,5},{5,4},{6,7},{7,6},{8,9},{9,8},{10,11... | collective-permute-start | bytes 884744 | tf_op jit(solution)/shard_map/ppermute | solution.py:994
  231.6 20.1 %copy-start.1 = (bf16[192,768]{1,0:T(8,128)(2,1)S(1)}, bf16[192,768]{1,0:T(8,128)(2,1)}, u32[]{:S(2)}) copy-start(bf16[192,768]{1,0:T(8,128)(2,1)} %reduce-scatter.2.cloned.1.call-done.zo_ref) | copy-start | bytes 884740
  231.6 20.1 %copy-start.2 = (f32[32,1792]{1,0:T(8,128)S(1)}, f32[32,1792]{1,0:T(8,128)}, u32[]{:S(2)}) copy-start(f32[32,1792]{1,0:T(8,128)} %get-tuple-element.52.cw_ref) | copy-start | bytes 688132
  231.6 20.1 %copy-start.3 = (f32[8,1792]{1,0:T(8,128)S(1)}, f32[8,1792]{1,0:T(8,128)}, u32[]{:S(2)}) copy-start(f32[8,1792]{1,0:T(8,128)} %get-tuple-element.53.cb_ref) | copy-start | bytes 172036
  231.6 20.1 %copy-start.4 = (f32[8,1536]{1,0:T(8,128)S(1)}, f32[8,1536]{1,0:T(8,128)}, u32[]{:S(2)}) copy-start(f32[8,1536]{1,0:T(8,128)} %get-tuple-element.54.ggain_ref) | copy-start | bytes 147460
  231.6 20.1 %copy-start.5 = (f32[8,1536]{1,0:T(8,128)S(1)}, f32[8,1536]{1,0:T(8,128)}, u32[]{:S(2)}) copy-start(f32[8,1536]{1,0:T(8,128)} %get-tuple-element.55.skip_ref) | copy-start | bytes 147460
  231.6 20.1 %copy-start.7 = (f32[8,128]{1,0:T(8,128)S(1)}, f32[8,128]{1,0:T(8,128)}, u32[]{:S(2)}) copy-start(f32[8,128]{1,0:T(8,128)} %get-tuple-element.57.alog_ref) | copy-start | bytes 12292
  231.6 20.1 %copy-start.8 = (f32[8,128]{1,0:T(8,128)S(1)}, f32[8,128]{1,0:T(8,128)}, u32[]{:S(2)}) copy-start(f32[8,128]{1,0:T(8,128)} %get-tuple-element.58.dtb_ref) | copy-start | bytes 12292
  251.8 0.7 copy-start.6
Sparse Core Ops, SparseCore 0:
  39.3 54.9 all-gather.1
  138.8 77.6 reduce-scatter.1

commit v8 on v7

--- a/solution.py
+++ b/solution.py
@@ -808,10 +808,10 @@
 
 
 def finish_kernel(
-    line, bits, cw_ref, cb_ref, ggain_ref, skip_ref, ngain_ref, alog_ref, dtb_ref, zo_ref, zo_got_ref, d_ref,
+    line, bits, cw_ref, cb_ref, ggain_ref, skip_ref, ngain_ref, alog_ref, dtb_ref, zo_ref, zo_got_ref, d_ref, from_x_ref, from_y_ref,
     small_ref, din_ref, dout_ref,
-    acc, got, core_got, one, two_got, two, three_got, three, line_got, last, last_got,
-    small_send, small_recv, core_send, core_recv, two_send, two_recv, three_send, three_recv,
+    acc, got, one, two_got, two, three_got, three, line_got, last, last_got,
+    small_send, small_recv, two_send, two_recv, three_send, three_recv,
     line_send, line_recv, last_sem,
 ):
     l, x, c, index, y = place(line)
@@ -820,9 +820,6 @@
     others = [{"dp": index((l + k) % line, x, c)} for k in range(1, line)]
     beside, sibling, across = {"dp": index(l, 1 - x, c)}, {"dp": index(l, x, 1 - c)}, {"seq": 1 - y}
     meet(doubling + others + [beside, sibling, across])
-    order = list(range(1, line)) + [0]
-    at = [(l + k) % line for k in order]
-
     def plus(a, b):
         return a.astype(f32) + b.astype(f32)
 
@@ -831,48 +828,44 @@
         copy.start()
         return copy
 
-    first = []
+    second, third = [], []
     for i in range(line):
-        first.append(
-            launch(d_ref.at[at[i], :, 1 - c], core_got.at[i], core_send.at[i], core_recv.at[i], sibling)
-        )
+        for j in range(2):
+            for n in range(2):
+                if i % 2 == 0:
+                    one[i, j, n] = plus(d_ref[i, x, j, n], from_x_ref[i // 2, j, n]).astype(bf16)
+                else:
+                    one[i, n, j] = plus(d_ref[i, j, n, y], from_y_ref[i // 2, j, n]).astype(bf16)
+        second.append(launch(one.at[i, 1 - c], two_got.at[i], two_send.at[i], two_recv.at[i], sibling))
     pack_small(acc.at[0], cw_ref, cb_ref, ggain_ref, skip_ref, ngain_ref, alog_ref, dtb_ref)
     smalls = doubling + [across]
-    second, third, fourth = [], [], []
 
     def small_start(k):
         return launch(acc.at[k], got.at[k], small_send.at[k], small_recv.at[k], smalls[k])
 
-    for t in range(max(line + 2, len(smalls))):
-        small = small_start(t) if t < len(smalls) else None
-        if t < line:
-            i = t
-            first[i].wait()
-            for a in range(2):
-                for h in range(2):
-                    one[i, a, h] = plus(d_ref[at[i], a, c, h], core_got[i, a, h]).astype(bf16)
-            src, device = (one.at[i, 1 - x], beside) if i % 2 == 0 else (one.at[i, :, 1 - y], across)
-            second.append(launch(src, two_got.at[i], two_send.at[i], two_recv.at[i], device))
-        if 1 <= t <= line:
-            i = t - 1
-            second[i].wait()
-            for j in range(2):
-                kept = one[i, x, j] if i % 2 == 0 else one[i, j, y]
-                two[i, j] = plus(kept, two_got[i, j]).astype(bf16)
-            src, device = (two.at[i, 1 - y], across) if i % 2 == 0 else (two.at[i, 1 - x], beside)
-            third.append(launch(src, three_got.at[i], three_send.at[i], three_recv.at[i], device))
-        if 2 <= t <= line + 1:
-            i = t - 2
-            third[i].wait()
-            kept = two[i, y] if i % 2 == 0 else two[i, x]
-            three[i] = plus(kept, three_got[i]).astype(bf16)
-            if order[i] > 0:
-                fourth.append(
-                    launch(three.at[i], line_got.at[l], line_send.at[i], line_recv.at[l], others[order[i] - 1])
-                )
-        if small is not None:
-            small.wait()
-            acc[t + 1] = acc[t] + got[t]
+    small = small_start(0)
+    for i in range(line):
+        second[i].wait()
+        for j in range(2):
+            two[i, j] = plus(one[i, c, j], two_got[i, j]).astype(bf16)
+        src, device = (two.at[i, 1 - y], across) if i % 2 == 0 else (two.at[i, 1 - x], beside)
+        third.append(launch(src, three_got.at[i], three_send.at[i], three_recv.at[i], device))
+    for i in range(line):
+        third[i].wait()
+        kept = two[i, y] if i % 2 == 0 else two[i, x]
+        three[i] = plus(kept, three_got[i]).astype(bf16)
+
+    def to_owner(k):
+        target = (l + k) % line
+        return remote(three.at[target], line_got.at[l], line_send.at[k], line_recv.at[l], others[k - 1])
+
+    for k in range(1, line):
+        to_owner(k).start()
+    for k in range(len(smalls)):
+        small.wait()
+        acc[k + 1] = acc[k] + got[k]
+        if k + 1 < len(smalls):
+            small = small_start(k + 1)
 
     small_ref[...] = acc[len(smalls)]
     own, half = din_ref.shape[0], zo_ref.shape[1]
@@ -881,15 +874,15 @@
     din_ref[:, half : 2 * half] = zo[own : 2 * own]
     dout_ref[...] = zo[2 * own :]
 
-    total = three[line - 1].astype(f32)
+    total = three[l].astype(f32)
     for k in range(1, line):
         at_k = (l + k) % line
         remote(three.at[0], line_got.at[at_k], last_sem.at[2], line_recv.at[at_k], sibling).wait_recv()
         total += line_got[at_k].astype(f32)
     last[...] = total.astype(bf16)
     final = launch(last, last_got, last_sem.at[0], last_sem.at[1], across)
-    for copy in fourth:
-        copy.wait_send()
+    for k in range(1, line):
+        to_owner(k).wait_send()
     final.wait()
     left = din_ref.shape[1] - 2 * half
     kept, came = last[...].astype(f32), last_got[...].astype(f32)
@@ -898,9 +891,9 @@
     din_ref[own // 2 :, 2 * half :] = (came * lower + kept * (1.0 - lower))[:, :left]
 
 
-def finish(smalls, d_zo, zo_got, d_x, own, proj):
-    owners = d_x.shape[0] // own
-    line, columns, half = owners // 4, d_x.shape[1], d_zo.shape[1]
+def finish(smalls, d_zo, zo_got, parts, from_x, from_y, own, proj):
+    line, columns, half = parts.shape[0], parts.shape[-1], d_zo.shape[1]
+    owners = 4 * line
     bits = [1 << i for i in range(owners.bit_length() - 1)]
     channels = smalls[1].shape[1]
     vmem = pl.BlockSpec(memory_space=pltpu.VMEM)
@@ -910,7 +903,7 @@
     low = lambda *dims: pltpu.VMEM(dims + piece, bf16)
     return pl.pallas_call(
         functools.partial(finish_kernel, line, bits),
-        in_specs=[vmem] * 10,
+        in_specs=[vmem] * 12,
         out_specs=[vmem] * 3,
         out_shape=[
             jax.ShapeDtypeStruct((8, channels), f32),
@@ -920,14 +913,14 @@
         scratch_shapes=[
             pltpu.VMEM((steps + 1, 8, channels), f32),
             pltpu.VMEM((steps, 8, channels), f32),
-            low(line, 2, 2), low(line, 2, 2), low(line, 2), low(line, 2), low(line), low(line), low(line), low(), low(),
+            low(line, 2, 2), low(line, 2), low(line, 2), low(line), low(line), low(line), low(), low(),
             dma((steps,)), dma((steps,)),
         ]
-        + [dma((line,))] * 8
+        + [dma((line,))] * 6
         + [dma((3,))],
         compiler_params=params(48 << 20, collective_id=0, has_side_effects=True),
         name="finish",
-    )(*smalls, d_zo, zo_got, d_x.reshape(line, 2, 2, 2, own // 2, columns))
+    )(*smalls, d_zo, zo_got, parts, from_x, from_y)
 
 
 def finish_plain(smalls, d_zo, d_x, own, proj):
@@ -988,11 +981,19 @@
     d_zo = lax.psum_scatter(d_zo, "dp", scatter_dimension=0, tiled=True)
     gx, p_cw, p_cb, p_skip, p_alog, p_dtb = state_backward(seg, xbc, dt, s, sin, gm, conv_weight, head, seqs)
     d_x = dot(normed, gx, TN).astype(bf16)
+    if owned:
+        line = owners // 4
+        parts = d_x.reshape(line, 2, 2, 2, own // 2, d_x.shape[1])
+        beside, across = 1 - (lax.axis_index("dp") // 2) % 2, 1 - lax.axis_index("seq")
+        to_x = lax.dynamic_index_in_dim(parts[0::2], beside, 1, keepdims=False)
+        to_y = lax.dynamic_index_in_dim(parts[1::2], across, 3, keepdims=False)
+        from_x = lax.ppermute(to_x, "dp", [(i, i + 2 - 4 * ((i // 2) % 2)) for i in range(owners)])
+        from_y = lax.ppermute(to_y, "seq", [(0, 1), (1, 0)])
     g_tok, p_ngain = token_grad(tok, cot, gz, gx, weights[:2], wx, ngain)
     smalls = (p_cw, p_cb, p_ggain, p_skip, p_ngain, p_alog, p_dtb)
     if owned:
         zo_got = lax.ppermute(d_zo, "seq", [(0, 1), (1, 0)])
-        small, d_in, d_out = finish(smalls, d_zo, zo_got, d_x, own, weight_in.shape[1])
+        small, d_in, d_out = finish(smalls, d_zo, zo_got, parts, from_x, from_y, own, weight_in.shape[1])
     else:
         small, d_in, d_out = finish_plain(smalls, d_zo, d_x, own, weight_in.shape[1])
     return (

time: 298 us -> 309 us (1.037)
  local copies, waits for them, and re-layouts: 11.5 us -> 15.9 us
    pallas_call x1, Pallas kernels: 33.5 us -> 36.8 us  [finish(): pl.pallas_call(functools.partial(finish_kernel, line, bits), in_specs=[vm...]
    unnamed x40 -> x44, local copies, waits for them, and re-layouts: 4.11 us -> 7.21 us
  transfers between devices with their start and end apart: 3 -> 5, of which waited for: 0 -> 1; matrix products, arithmetic and copies ran while one was open for 5% -> 4% of each run, Pallas kernels for 52% -> 50%
where the time goes in v8:
time: 309 us; the launch traced here: 308 us
  Pallas kernels  245 us (79%)
  matrix products  23.1 us (7%)
  local copies, waits for them, and re-layouts  15.9 us (5%)
  between operations  14.4 us (5%)
  other arithmetic  3.75 us (1%)
    pallas_call x1, Pallas kernels, state_backward(): pl.pallas_call(bwd_kernel, grid=(blocks,), in_specs=[fixed(seg.shape), pl...  80.9 us
    pallas_call x1, Pallas kernels, state_forward(): pl.pallas_call(fwd_kernel, grid=(blocks,), in_specs=[fixed(seg.shape), pl...  39.6 us
    pallas_call x1, Pallas kernels, finish(): pl.pallas_call(functools.partial(finish_kernel, line, bits), in_specs=[vm...  36.8 us
    pallas_call x1, Pallas kernels, gate(): pl.pallas_call(gate_kernel, grid=(rows // tile,), in_specs=[pl.BlockSpec(...  28.4 us
    pallas_call x1, Pallas kernels, gather(): pl.pallas_call(functools.partial(gather_kernel, line), in_specs=[vmem], o...  26.6 us
    dot_general x3, matrix products, dot(): return lax.dot_general(a, b, dims, preferred_element_type=f32)  23.1 us
    pallas_call x1, Pallas kernels, token_grad(): pl.pallas_call(token_kernel, grid=(rows // tile,), in_specs=[pl.BlockSpec...  20.1 us
    pallas_call x1, Pallas kernels, project(): pl.pallas_call(proj_kernel, grid=(rows // tile,), in_specs=[pl.BlockSpec(...  12.7 us
  transfers between devices with their start and end apart: 5, of which 1 were waited for; matrix products, arithmetic and copies ran while one was open for 4% of the time, Pallas kernels for 50%

profile of v8, /device:TPU:0, one launch (start us, length us, event | category | flops | bytes accessed | tf_op | source)
XLA Modules:
  0.0 308.2 jit_solution(10289473909213374396)
XLA Ops:
  7.2 0.0 all-gather.2.cloned.1.call-start
  7.3 1.0 fusion.2
  8.2 0.9 slice.42
  9.2 26.6 %gather.1 = bf16[4,2,2,2,24,1920]{5,4,3,2,1,0:T(8,128)(2,1)S(1)} custom-call(bf16[2,24,1920]{2,1,0:T(8,128)(2,1)S(1)} %bitcast.39), custom_call_target="tpu_custom_call" | custom-call | tf_op jit(solution)/shard_map/gather/pallas_call | solution.py:780
  35.8 1.7 copy-done
  37.5 0.7 pad_maximum_fusion.1
  38.3 0.0 all-gather.2.cloned.1.call-update
  38.3 0.0 copy-start.20
  38.3 0.0 copy-start.17
  38.3 0.0 copy-start.18
  38.3 0.0 reduce-scatter.2.cloned.1.call-start
  38.4 0.6 reshape.88.gain_ref
  39.0 0.6 reshape.91.seg_ref
  39.6 0.6 reshape.94.cb_ref
  40.2 0.6 reshape.98.gain_ref
  40.8 12.7 %project.1 = (bf16[2048,768]{1,0:T(8,128)(2,1)}, f32[2048,1792]{1,0:T(8,128)}, f32[2048,128]{1,0:T(8,128)}) custom-call(bf16[2048,768]{1,0:T(8,128)(2,1)} %bitcast.47, f32[1,768]{1,0:T(1,128)} %reshape.88.gain_ref, bf16[768,1920]{1,0:T(8,128)(2,1)} %bitcast.37), custom_call_target="tpu_custom_call" | custom-call | tf_op jit(solution)/shard_map/project/pallas_call | solution.py:82
  53.6 0.6 select_maximum_fusion.head_ref
  54.2 39.6 %state_forward.1 = (f32[2,1024,1536]{2,1,0:T(8,128)}, f32[2,1024,1792]{2,1,0:T(8,128)}, bf16[2,8,128,1536]{3,2,1,0:T(8,128)(2,1)}) custom-call(f32[16,128]{1,0:T(8,128)} %reshape.91.seg_ref, f32[2,1024,1792]{2,1,0:T(8,128)} %bitcast.45, f32[2,1024,128]{2,1,0:T(8,128)} %bitcast.62, f32[4,1792]{1,0:T(4,128)} %cw_ref.3, f32[1,1792]{1,0:T(1,128)} %reshape.94.cb_ref, ...), custom_call_target="tpu_custom_call" | custom-call | tf_op jit(solution)/shard_map/state_forward/pallas_call | solution.py:283
  93.8 28.4 %gate.1 = (bf16[2048,1536]{1,0:T(8,128)(2,1)}, bf16[2048,768]{1,0:T(8,128)(2,1)}, bf16[2048,1536]{1,0:T(8,128)(2,1)}, f32[2048,1536]{1,0:T(8,128)}, f32[8,1536]{1,0:T(8,128)}) custom-call(bf16[2048,768]{1,0:T(8,128)(2,1)} %bitcast.48, bf16[2048,768]{1,0:T(8,128)(2,1)} %get-tuple-element.38.normed_ref, f32[2048,1536]{1,0:T(8,128)} %bitcast.54, ...), custom_call_target="tpu_custom_call" | custom-call | tf_op jit(solution)/shard_map/gate/pallas_call | solution.py:368
  122.2 8.3 %convolution_convert_fusion.2 = bf16[768,1536]{1,0:T(8,128)(2,1)S(1)} fusion(bf16[2048,768]{1,0:T(8,128)(2,1)S(1)} %copy-done.11, bf16[2048,1536]{1,0:T(8,128)(2,1)} %get-tuple-element.44.gz_ref), kind=kOutput, calls=%fused_computation.3 | convolution fusion | flops 4833017856 | bytes 11796480 | tf_op jit(solution)/shard_map/dot_general | solution.py:26
  130.4 0.0 copy-start.9
  130.4 0.2 fusion.1
  130.6 1.7 copy-done.9
  132.3 5.5 %convolution_convert_fusion.1 = bf16[1536,768]{1,0:T(8,128)(2,1)S(1)} fusion(bf16[2048,1536]{1,0:T(8,128)(2,1)S(1)} %copy-done.19, bf16[2048,768]{1,0:T(8,128)(2,1)S(1)} %bitcast.53), kind=kOutput, calls=%fused_computation.2 | convolution fusion | flops 4833017856 | bytes 11796480 | tf_op jit(solution)/shard_map/dot_general | solution.py:26
  137.8 2.4 pad_maximum_fusion
  140.2 0.0 reduce-scatter.2.cloned.1.call-update
  140.3 80.9 %state_backward.1 = (bf16[2,1024,1920]{2,1,0:T(8,128)(2,1)}, f32[32,1792]{1,0:T(8,128)}, f32[8,1792]{1,0:T(8,128)}, f32[8,1536]{1,0:T(8,128)}, f32[8,128]{1,0:T(8,128)}, /*index=5*/f32[8,128]{1,0:T(8,128)}) custom-call(f32[16,128]{1,0:T(8,128)} %reshape.91.seg_ref, f32[2,1024,1792]{2,1,0:T(8,128)} %bitcast.46, f32[2,1024,128]{2,1,0:T(8,128)} %bitcast.63, ...), custom_call_target="tpu_custom_call" | custom-call | tf_op jit(solution)/shard_map/state_backward/pallas_call | solution.py:617
  221.2 9.4 %convolution_convert_fusion = bf16[768,1920]{1,0:T(8,128)(2,1)S(1)} fusion(bf16[2048,768]{1,0:T(8,128)(2,1)S(1)} %copy-done.11, bf16[2048,1920]{1,0:T(8,128)(2,1)} %bitcast.58), kind=kOutput, calls=%fused_computation.1 | convolution fusion | flops 6041272320 | bytes 13959168 | tf_op jit(solution)/shard_map/dot_general | solution.py:26
  230.6 0.2 fusion
  230.8 0.1 dynamic-slice_bitcast_fusion.1
  230.9 1.4 copy-done.10
  232.3 0.9 collective-permute-start.1
  233.1 1.0 dynamic-slice_bitcast_fusion
  234.1 0.0 copy-start.7
  234.1 1.1 collective-permute-start.2
  235.2 1.0 collective-permute-start
  236.2 20.1 %token_grad.1 = (bf16[2048,768]{1,0:T(8,128)(2,1)}, f32[8,768]{1,0:T(8,128)}) custom-call(bf16[2048,768]{1,0:T(8,128)(2,1)} %bitcast.49, bf16[2048,768]{1,0:T(8,128)(2,1)} %bitcast.52, bf16[2048,1536]{1,0:T(8,128)(2,1)} %get-tuple-element.44.gz_ref, bf16[2048,1920]{1,0:T(8,128)(2,1)} %bitcast.59, bf16[16,192,768]{2,1,0:T(8,128)(2,1)} %bitcast.43, ...), custom_call_target="tpu_custom_call" | custom-call | tf_op jit(solution)/shard_map/token_grad/pallas_call | solution.py:685
  256.3 2.9 collective-permute-done.zo_got_ref
  259.3 0.0 copy-start.6
  259.3 0.7 copy-done.6
  260.0 36.8 %finish.1 = (f32[8,1792]{1,0:T(8,128)S(1)}, f32[48,3352]{1,0:T(8,128)S(1)}, f32[96,768]{1,0:T(8,128)S(1)}) custom-call(f32[32,1792]{1,0:T(8,128)S(1)} %copy-done.2, f32[8,1792]{1,0:T(8,128)S(1)} %copy-done.3, f32[8,1536]{1,0:T(8,128)S(1)} %copy-done.4, f32[8,1536]{1,0:T(8,128)S(1)} %copy-done.5, f32[8,768]{1,0:T(8,128)S(1)} %copy-done.6, ...), custom_call_target="tpu_custom_call" | custom-call | tf_op jit(solution)/shard_map/finish/pallas_call | solution.py:904
  296.8 0.6 slice.50
  297.4 0.6 slice_reduce_fusion
  298.0 0.6 slice_reduce_fusion.1
  298.7 0.6 slice_reduce_fusion.2
  299.3 0.5 slice_bitcast_fusion
  299.8 0.8 copy.25
  300.6 0.7 copy.26
  (39 shorter events, 0.1 us)
Async XLA Ops:
  7.2 30.4 %copy-start.12 = (bf16[96,768]{1,0:T(8,128)(2,1)S(1)}, bf16[96,768]{1,0:T(8,128)(2,1)}, u32[]{:S(2)}) copy-start(bf16[96,768]{1,0:T(8,128)(2,1)} %param.23) | copy-start | bytes 442372
  7.2 31.2 %copy-start.16 = (f32[768]{0:T(1024)S(1)}, f32[768]{0:T(1024)}, u32[]{:S(2)}) copy-start(f32[768]{0:T(1024)} %param.15) | copy-start | bytes 9220
  7.2 31.8 %copy-start.14 = (s32[2,1024]{1,0:T(2,128)S(1)}, s32[2,1024]{1,0:T(2,128)}, u32[]{:S(2)}) copy-start(s32[2,1024]{1,0:T(2,128)} %param.13) | copy-start | bytes 24580
  7.2 32.4 %copy-start.15 = (f32[1792]{0:T(1024)S(1)}, f32[1792]{0:T(1024)}, u32[]{:S(2)}) copy-start(f32[1792]{0:T(1024)} %param.18) | copy-start | bytes 21508
  7.2 33.0 %copy-start.13 = (f32[1536]{0:T(1024)S(1)}, f32[1536]{0:T(1024)}, u32[]{:S(2)}) copy-start(f32[1536]{0:T(1024)} %param.22) | copy-start | bytes 18436
  7.2 86.5 %all-gather.2.cloned.1.call-start = ((), (), s32[]{:S(2)}) async-start(), calls=%async_computation.1 | async-start | bytes 5013504 | tf_op jit(solution)/shard_map/all_gather | solution.py:958
  35.8 1.7 copy-start
  38.3 15.2 %copy-start.20 = (f32[24]{0:T(128)S(1)}, f32[24]{0:T(128)}, u32[]{:S(2)}) copy-start(f32[24]{0:T(128)} %param.20) | copy-start | bytes 292
  38.3 15.2 %copy-start.17 = (f32[24]{0:T(128)S(1)}, f32[24]{0:T(128)}, u32[]{:S(2)}) copy-start(f32[24]{0:T(128)} %param.21) | copy-start | bytes 292
  38.3 15.2 %copy-start.18 = (f32[24]{0:T(128)S(1)}, f32[24]{0:T(128)}, u32[]{:S(2)}) copy-start(f32[24]{0:T(128)} %param.19) | copy-start | bytes 292
  38.3 196.9 %reduce-scatter.2.cloned.1.call-start = ((), (), s32[]{:S(2)}) async-start(), calls=%async_computation.2 | async-start | bytes 5013504 | tf_op jit(solution)/shard_map/reduce_scatter | solution.py:981
  93.8 28.4 %copy-start.11 = (bf16[2048,768]{1,0:T(8,128)(2,1)S(1)}, bf16[2048,768]{1,0:T(8,128)(2,1)}, u32[]{:S(2)}) copy-start(bf16[2048,768]{1,0:T(8,128)(2,1)} %get-tuple-element.38.normed_ref) | copy-start | bytes 9437188
  122.1 8.5 %copy-start.19 = (bf16[2048,1536]{1,0:T(8,128)(2,1)S(1)}, bf16[2048,1536]{1,0:T(8,128)(2,1)}, u32[]{:S(2)}) copy-start(bf16[2048,1536]{1,0:T(8,128)(2,1)} %get-tuple-element.47) | copy-start | bytes 18874372
  130.4 1.9 copy-start.9
  230.6 1.7 copy-start.10
  232.3 24.0 %collective-permute-start.1 = (bf16[2,2,2,24,1920]{4,3,2,1,0:T(8,128)(2,1)S(1)}, bf16[2,2,2,24,1920]{4,3,2,1,0:T(8,128)(2,1)S(1)}, u32[]{:S(2)}, u32[]{:S(2)}) collective-permute-start(bf16[2,2,2,24,1920]{4,3,2,1,0:T(8,128)(2,1)S(1)} %dynamic-slice_bitcast_fusion.1), channel_id=1, source_target_pairs={{0,4},{2,6},{4,0},{6,2},{8,12},{10,14},{12,8},{14,10},{16,20},{18,... | collective-permute-start | bytes 2211848 | tf_op jit(solution)/shard_map/ppermute | solution.py:990
  234.1 25.1 %copy-start.2 = (f32[32,1792]{1,0:T(8,128)S(1)}, f32[32,1792]{1,0:T(8,128)}, u32[]{:S(2)}) copy-start(f32[32,1792]{1,0:T(8,128)} %get-tuple-element.52.cw_ref) | copy-start | bytes 688132
  234.1 25.1 %copy-start.3 = (f32[8,1792]{1,0:T(8,128)S(1)}, f32[8,1792]{1,0:T(8,128)}, u32[]{:S(2)}) copy-start(f32[8,1792]{1,0:T(8,128)} %get-tuple-element.53.cb_ref) | copy-start | bytes 172036
  234.1 25.1 %copy-start.4 = (f32[8,1536]{1,0:T(8,128)S(1)}, f32[8,1536]{1,0:T(8,128)}, u32[]{:S(2)}) copy-start(f32[8,1536]{1,0:T(8,128)} %get-tuple-element.54.ggain_ref) | copy-start | bytes 147460
  234.1 25.1 %copy-start.5 = (f32[8,1536]{1,0:T(8,128)S(1)}, f32[8,1536]{1,0:T(8,128)}, u32[]{:S(2)}) copy-start(f32[8,1536]{1,0:T(8,128)} %get-tuple-element.55.skip_ref) | copy-start | bytes 147460
  234.1 25.1 %copy-start.7 = (f32[8,128]{1,0:T(8,128)S(1)}, f32[8,128]{1,0:T(8,128)}, u32[]{:S(2)}) copy-start(f32[8,128]{1,0:T(8,128)} %get-tuple-element.57.alog_ref) | copy-start | bytes 12292
  234.1 25.1 %copy-start.8 = (f32[8,128]{1,0:T(8,128)S(1)}, f32[8,128]{1,0:T(8,128)}, u32[]{:S(2)}) copy-start(f32[8,128]{1,0:T(8,128)} %get-tuple-element.58.dtb_ref) | copy-start | bytes 12292
  234.1 22.2 %collective-permute-start.2 = (bf16[2,2,2,24,1920]{4,3,2,1,0:T(8,128)(2,1)}, bf16[2,2,2,24,1920]{4,3,2,1,0:T(8,128)(2,1)S(1)}, u32[]{:S(2)}, u32[]{:S(2)}) collective-permute-start(bf16[2,2,2,24,1920]{4,3,2,1,0:T(8,128)(2,1)} %dynamic-slice_bitcast_fusion), channel_id=1, source_target_pairs={{0,1},{1,0},{2,3},{3,2},{4,5},{5,4},{6,7},{7,6},{8,9},{9,8},{10,11... | collective-permute-start | bytes 2211848 | tf_op jit(solution)/shard_map/ppermute | solution.py:991
  235.2 24.0 %copy-start.1 = (bf16[192,768]{1,0:T(8,128)(2,1)S(1)}, bf16[192,768]{1,0:T(8,128)(2,1)}, u32[]{:S(2)}) copy-start(bf16[192,768]{1,0:T(8,128)(2,1)} %reduce-scatter.2.cloned.1.call-done.zo_ref) | copy-start | bytes 884740
  235.2 24.0 %collective-permute-start = (bf16[192,768]{1,0:T(8,128)(2,1)}, bf16[192,768]{1,0:T(8,128)(2,1)S(1)}, u32[]{:S(2)}, u32[]{:S(2)}) collective-permute-start(bf16[192,768]{1,0:T(8,128)(2,1)} %reduce-scatter.2.cloned.1.call-done.zo_ref), channel_id=1, source_target_pairs={{0,1},{1,0},{2,3},{3,2},{4,5},{5,4},{6,7},{7,6},{8,9},{9,8},{10,11... | collective-permute-start | bytes 884744 | tf_op jit(solution)/shard_map/ppermute | solution.py:995
  259.3 0.7 copy-start.6
Sparse Core Ops, SparseCore 0:
  38.4 55.1 all-gather.1
  140.3 77.7 reduce-scatter.1
